TPU v7x, 32 devices: a whole 2x2x4 slice. The times are simulated.
32 devices in a mesh: gx: 2 (over y), gy: 4 (over x, core), gz: 4 (over z).
Axes of the slice: x: 2, y: 2, z: 4, core: 2. Of those that a mesh axis runs over, the one named last changes fastest.
Arguments:
- pressure: float32 [24, 64, 512], P('gx', 'gy', 'gz'), may hold values from -8 to 8
- wind: float32 [3, 24, 64, 512], P(None, 'gx', 'gy', 'gz'), may hold values from -6 to 6
Outputs:
- result: float32 [24, 64, 512], P('gx', 'gy', 'gz')
All inputs are finite; a program needn't handle non-finite values.
Results may differ from a plain program's by a relative error of at most 0.00019.
Values sent between devices are 32-bit elements; how exact they have to be, the bound alone decides.
No kernel may reach another device: no remote copies, remote signals or barrier semaphores. Data moves between devices by JAX's collectives and lax.ppermute only.
A program may use at most 64 MiB of HBM per device.

v0:
```python
import jax
import jax.numpy as jnp
from jax import lax
from jax.sharding import PartitionSpec as P

SWEEPS = 2
COARSE_SWEEPS = 4


OMEGA = 0.8
VISCOSITY = 1.0
REACTION = 1.0


def with_halo(cells, sides, width):
    for axis, dim in sides:
        count = lax.axis_size(axis)
        ends = count - 1
        head = lax.slice_in_dim(cells, 0, width, axis=dim)
        tail = lax.slice_in_dim(cells, cells.shape[dim] - width, cells.shape[dim], axis=dim)
        cells = jnp.concatenate(
            [
                lax.ppermute(tail, axis, [(i, (i + 1) % count) for i in range(ends)]),
                cells,
                lax.ppermute(head, axis, [((i + 1) % count, i) for i in range(ends)]),
            ],
            axis=dim,
        )
    return cells


def six_sum(padded):
    return (
        padded[..., 2:, 1:-1, 1:-1]
        + padded[..., :-2, 1:-1, 1:-1]
        + padded[..., 1:-1, 2:, 1:-1]
        + padded[..., 1:-1, :-2, 1:-1]
        + padded[..., 1:-1, 1:-1, 2:]
        + padded[..., 1:-1, 1:-1, :-2]
    )


def central_parts(padded):
    return (
        (padded[..., 2:, 1:-1, 1:-1] - padded[..., :-2, 1:-1, 1:-1]) * 0.5,
        (padded[..., 1:-1, 2:, 1:-1] - padded[..., 1:-1, :-2, 1:-1]) * 0.5,
        (padded[..., 1:-1, 1:-1, 2:] - padded[..., 1:-1, 1:-1, :-2]) * 0.5,
    )


def crop(values, margin):
    return values[..., margin:-margin, margin:-margin, margin:-margin]


def axis_inside(position, extent, pieces, rim_width):
    places = position * extent + jnp.arange(-rim_width, extent + rim_width, dtype=jnp.int32)
    return ((places >= 0) & (places < extent * pieces)).astype(jnp.float32)


def inside_mask(extents, rim_width):
    along_x = axis_inside(lax.axis_index("gx"), extents[0], lax.axis_size("gx"), rim_width)
    along_y = axis_inside(lax.axis_index("gy"), extents[1], lax.axis_size("gy"), rim_width)
    along_z = axis_inside(lax.axis_index("gz"), extents[2], lax.axis_size("gz"), rim_width)
    return along_x[:, None, None] * along_y[None, :, None] * along_z[None, None, :]


def laplace(values, padded, weight_scale):
    return weight_scale * (6.0 * values - six_sum(padded))


def sweep(source, values, padded, weight_scale):
    return values + OMEGA / (6.0 * weight_scale) * (source - laplace(values, padded, weight_scale))


def start_sweep(source, weight_scale):
    return OMEGA / (6.0 * weight_scale) * source


def smooth_faces(values):
    return with_halo(values, (("gx", 0), ("gy", 1), ("gz", 2)), 1)


def smooth(source, values, weight_scale, sweep_count):
    for sweep_number in range(sweep_count):
        if values is None:
            values = start_sweep(source, weight_scale)
        else:
            values = sweep(source, values, smooth_faces(values), weight_scale)
    return values


def coarse_solve(source, weight_scale):
    reach = COARSE_SWEEPS - 1
    padded_source = with_halo(source, (("gx", 0), ("gy", 1), ("gz", 2)), reach)
    values = start_sweep(padded_source, weight_scale)
    for sweep_number in range(1, COARSE_SWEEPS):
        rim_width = reach - sweep_number
        values = sweep(crop(padded_source, sweep_number), crop(values, 1), values, weight_scale)
        if rim_width > 0:
            values = values * inside_mask(source.shape, rim_width)
    return values


def restrict(values):
    extent_x, extent_y, extent_z = values.shape
    blocks = values.reshape(extent_x // 2, 2, extent_y // 2, 2, extent_z // 2, 2)
    return 0.125 * jnp.sum(blocks, axis=(1, 3, 5))


def prolong(values):
    extent_x, extent_y, extent_z = values.shape
    spread = jnp.broadcast_to(
        values[:, None, :, None, :, None], (extent_x, 2, extent_y, 2, extent_z, 2)
    )
    return spread.reshape(2 * extent_x, 2 * extent_y, 2 * extent_z)


def vcycle(source, values, depth_index):
    weight_scale = 0.25**depth_index
    if depth_index == 2:
        return coarse_solve(source, weight_scale)
    values = smooth(source, values, weight_scale, SWEEPS)
    residual = source - laplace(values, smooth_faces(values), weight_scale)
    correction = vcycle(restrict(residual), None, depth_index + 1)
    values = values + prolong(correction)
    return smooth(source, values, weight_scale, SWEEPS)


def solve(source):
    values = None
    values = vcycle(source, values, 0)
    return values


def momentum(padded_velocity, wind):
    centre = padded_velocity[:, 1:-1, 1:-1, 1:-1]
    diffusion = 6.0 * centre - six_sum(padded_velocity)
    slopes = central_parts(padded_velocity)
    convection = wind[0:1] * slopes[0] + wind[1:2] * slopes[1] + wind[2:3] * slopes[2]
    return REACTION * centre + VISCOSITY * diffusion + convection


def body(pressure, wind):
    first = solve(pressure)
    padded = with_halo(first, (("gx", 0), ("gy", 1), ("gz", 2)), 1)
    velocity = jnp.stack(central_parts(padded))
    padded_velocity = with_halo(velocity, (("gx", 1), ("gy", 2), ("gz", 3)), 1)
    flux = momentum(padded_velocity, wind)
    padded_flux = with_halo(flux, (("gx", 1), ("gy", 2), ("gz", 3)), 1)
    slopes = central_parts(padded_flux)
    product = -(slopes[0][0] + slopes[1][1] + slopes[2][2])
    return solve(product)


def solution(mesh):
    in_specs = (P("gx", "gy", "gz"), P(None, "gx", "gy", "gz"))
    out_specs = P("gx", "gy", "gz")
    return jax.shard_map(body, mesh=mesh, in_specs=in_specs, out_specs=out_specs, check_vma=False)
```

profile of v0, /device:TPU:0, one launch (start us, length us, event | category | flops | bytes accessed | tf_op | source)
XLA Modules:
  0.0 551.5 jit_solution(5317152724919394749)
XLA Ops:
  2.2 4.9 collective-permute-start.1
  15.1 5.2 collective-permute-start.5
  27.2 4.5 collective-permute-start.7
  39.7 5.0 collective-permute-start.11
  49.9 7.7 %reshape.155 = f32[6,2,8,2,64,2]{5,4,3,2,1,0:T(8,128)} reshape(f32[12,16,128]{2,1,0:T(8,128)S(1)} %fusion.97) | data formatting | bytes 196608 | tf_op jit(solution)/shard_map/reshape | solution.py:106
  62.2 4.5 collective-permute-start.13
  74.6 5.0 collective-permute-start.17
  82.9 4.5 collective-permute-start.19
  95.3 5.0 collective-permute-start.23
  103.3 4.2 collective-permute-start.24
  117.8 5.8 %collective-permute-done.27 = f32[9,3,32]{2,1,0:T(4,128)S(1)} collective-permute-done((f32[9,3,32]{2,1,0:T(4,128)S(1)}, f32[9,3,32]{2,1,0:T(4,128)S(1)}, u32[]{:S(2)}, u32[]{:S(2)}) %collective-permute-start.27) | collective-permute-done | bytes 3488 | tf_op jit(solution)/shard_map/ppermute | solution.py:25
  123.7 4.3 collective-permute-start.28
  130.0 4.3 collective-permute-done.29
  136.6 4.5 collective-permute-start.31
  149.1 4.5 collective-permute-start.35
  156.9 4.5 collective-permute-start.37
  169.3 4.9 collective-permute-start.41
  179.8 5.6 %reshape.158 = f32[12,16,128]{2,1,0:T(8,128)S(1)} reshape(f32[6,2,8,2,64,2]{5,4,3,2,1,0:T(8,128)} %broadcast_in_dim.9) | data formatting | bytes 196608 | tf_op jit(solution)/shard_map/reshape | solution.py:115
  186.9 4.5 collective-permute-start.43
  194.1 4.2 collective-permute-start.45
  200.5 4.6 collective-permute-start.47
  209.5 4.5 collective-permute-start.49
  216.8 5.1 collective-permute-start.51
  224.1 4.7 collective-permute-start.53
  233.2 4.5 collective-permute-start.55
  240.4 5.1 collective-permute-start.57
  247.8 4.7 collective-permute-start.59
  256.9 4.5 collective-permute-start.61
  264.3 5.1 collective-permute-start.63
  271.8 4.9 collective-permute-start.65
  276.8 6.5 %collective-permute-done.64 = f32[3,14,18,1]{3,2,1,0:T(8,128)S(1)} collective-permute-done((f32[3,14,18,1]{3,2,1,0:T(8,128)S(1)}, f32[3,14,18,1]{3,2,1,0:T(8,128)S(1)}, u32[]{:S(2)}, u32[]{:S(2)}) %collective-permute-start.64) | collective-permute-done | bytes 3056 | tf_op jit(solution)/shard_map/ppermute | solution.py:25
  286.7 4.5 collective-permute-start.67
  294.1 5.2 collective-permute-start.69
  301.7 4.8 collective-permute-start.71
  306.5 5.5 collective-permute-done.70
  315.2 4.5 collective-permute-start.73
  322.4 6.4 %collective-permute-start.75 = (f32[14,1,128]{2,1,0:T(1,128)S(1)}, f32[14,1,128]{2,1,0:T(1,128)S(1)}, u32[]{:S(2)}, u32[]{:S(2)}) collective-permute-start(f32[14,1,128]{2,1,0:T(1,128)S(1)} %get-tuple-element.50), channel_id=1, source_target_pairs={{0,4},{4,8},{8,12},{1,5},{5,9},{9,13},{2,6},{6,10},{10,14},{3,7},{... | collective-permute-start | bytes 21512 | tf_op jit(solution)/shard_map/ppermute | solution.py:23
  331.1 4.7 collective-permute-start.77
  340.2 4.5 collective-permute-start.79
  347.4 7.4 %collective-permute-start.81 = (f32[14,1,128]{2,1,0:T(1,128)S(1)}, f32[14,1,128]{2,1,0:T(1,128)S(1)}, u32[]{:S(2)}, u32[]{:S(2)}) collective-permute-start(f32[14,1,128]{2,1,0:T(1,128)S(1)} %get-tuple-element.48), channel_id=1, source_target_pairs={{0,4},{4,8},{8,12},{1,5},{5,9},{9,13},{2,6},{6,10},{10,14},{3,7},{... | collective-permute-start | bytes 21512 | tf_op jit(solution)/shard_map/ppermute | solution.py:23
  357.1 4.8 collective-permute-start.83
  365.0 7.7 %reshape.159 = f32[6,2,8,2,64,2]{5,4,3,2,1,0:T(8,128)} reshape(f32[12,16,128]{2,1,0:T(8,128)S(1)} %fusion.49) | data formatting | bytes 196608 | tf_op jit(solution)/shard_map/reshape | solution.py:106
  377.3 4.5 collective-permute-start.85
  384.5 4.9 collective-permute-start.87
  391.7 4.7 collective-permute-start.89
  399.7 4.5 collective-permute-start.91
  406.9 5.0 collective-permute-start.93
  414.1 4.6 collective-permute-start.95
  426.9 4.2 collective-permute-done.97
  431.1 4.4 collective-permute-start.98
  436.9 5.8 %collective-permute-done.99 = f32[9,3,32]{2,1,0:T(4,128)S(1)} collective-permute-done((f32[9,3,32]{2,1,0:T(4,128)S(1)}, f32[9,3,32]{2,1,0:T(4,128)S(1)}, u32[]{:S(2)}, u32[]{:S(2)}) %collective-permute-start.99) | collective-permute-done | bytes 3488 | tf_op jit(solution)/shard_map/ppermute | solution.py:25
  442.8 4.3 collective-permute-start.100
  449.0 4.3 collective-permute-done.101
  455.7 4.5 collective-permute-start.103
  468.1 4.5 collective-permute-start.107
  476.0 4.5 collective-permute-start.109
  488.4 4.9 collective-permute-start.113
  498.9 5.6 %reshape.162 = f32[12,16,128]{2,1,0:T(8,128)S(1)} reshape(f32[6,2,8,2,64,2]{5,4,3,2,1,0:T(8,128)} %broadcast_in_dim.11) | data formatting | bytes 196608 | tf_op jit(solution)/shard_map/reshape | solution.py:115
  505.8 4.5 collective-permute-start.115
  513.0 4.2 collective-permute-start.117
  519.5 4.6 collective-permute-start.119
  528.5 4.5 collective-permute-start.121
  535.7 5.1 collective-permute-start.123
  543.0 4.7 collective-permute-start.125
  (339 shorter events, 234.0 us)
Async XLA Ops:
  0.9 6.2 %collective-permute-start = (f32[1,16,128]{2,1,0:T(8,128)S(1)}, f32[1,16,128]{2,1,0:T(8,128)S(1)}, u32[]{:S(2)}, u32[]{:S(2)}) collective-permute-start(f32[1,16,128]{2,1,0:T(8,128)S(1)} %get-tuple-element.81), channel_id=1, source_target_pairs={{16,0},{17,1},{18,2},{19,3},{20,4},{21,5},{22,6},{23,7},{24,8},{25... | collective-permute-start | bytes 24584 | tf_op jit(solution)/shard_map/ppermute | solution.py:25
  2.2 6.3 %collective-permute-start.1 = (f32[1,16,128]{2,1,0:T(8,128)S(1)}, f32[1,16,128]{2,1,0:T(8,128)S(1)}, u32[]{:S(2)}, u32[]{:S(2)}) collective-permute-start(f32[1,16,128]{2,1,0:T(8,128)S(1)} %get-tuple-element.80), channel_id=1, source_target_pairs={{0,16},{1,17},{2,18},{3,19},{4,20},{5,21},{6,22},{7,23},{8,24},{9,... | collective-permute-start | bytes 24584 | tf_op jit(solution)/shard_map/ppermute | solution.py:23
  13.8 9.3 %collective-permute-start.4 = (f32[14,18,1]{2,1,0:T(8,128)S(1)}, f32[14,18,1]{2,1,0:T(8,128)S(1)}, u32[]{:S(2)}, u32[]{:S(2)}) collective-permute-start(f32[14,18,1]{2,1,0:T(8,128)S(1)} %get-tuple-element.42), channel_id=1, source_target_pairs={{1,0},{2,1},{3,2},{5,4},{6,5},{7,6},{9,8},{10,9},{11,10},{13,12},{... | collective-permute-start | bytes 3032 | tf_op jit(solution)/shard_map/ppermute | solution.py:25
  15.1 9.7 %collective-permute-start.5 = (f32[14,18,1]{2,1,0:T(8,128)S(1)}, f32[14,18,1]{2,1,0:T(8,128)S(1)}, u32[]{:S(2)}, u32[]{:S(2)}) collective-permute-start(f32[14,18,1]{2,1,0:T(8,128)S(1)} %get-tuple-element.43), channel_id=1, source_target_pairs={{0,1},{1,2},{2,3},{4,5},{5,6},{6,7},{8,9},{9,10},{10,11},{12,13},{... | collective-permute-start | bytes 3032 | tf_op jit(solution)/shard_map/ppermute | solution.py:23
  27.2 5.9 %collective-permute-start.7 = (f32[1,16,128]{2,1,0:T(8,128)S(1)}, f32[1,16,128]{2,1,0:T(8,128)S(1)}, u32[]{:S(2)}, u32[]{:S(2)}) collective-permute-start(f32[1,16,128]{2,1,0:T(8,128)S(1)} %get-tuple-element.78), channel_id=1, source_target_pairs={{0,16},{1,17},{2,18},{3,19},{4,20},{5,21},{6,22},{7,23},{8,24},{9,... | collective-permute-start | bytes 24584 | tf_op jit(solution)/shard_map/ppermute | solution.py:23
  38.4 8.6 %collective-permute-start.10 = (f32[14,18,1]{2,1,0:T(8,128)S(1)}, f32[14,18,1]{2,1,0:T(8,128)S(1)}, u32[]{:S(2)}, u32[]{:S(2)}) collective-permute-start(f32[14,18,1]{2,1,0:T(8,128)S(1)} %get-tuple-element.40), channel_id=1, source_target_pairs={{1,0},{2,1},{3,2},{5,4},{6,5},{7,6},{9,8},{10,9},{11,10},{13,12},{... | collective-permute-start | bytes 3032 | tf_op jit(solution)/shard_map/ppermute | solution.py:25
  39.7 9.1 %collective-permute-start.11 = (f32[14,18,1]{2,1,0:T(8,128)S(1)}, f32[14,18,1]{2,1,0:T(8,128)S(1)}, u32[]{:S(2)}, u32[]{:S(2)}) collective-permute-start(f32[14,18,1]{2,1,0:T(8,128)S(1)} %get-tuple-element.41), channel_id=1, source_target_pairs={{0,1},{1,2},{2,3},{4,5},{5,6},{6,7},{8,9},{9,10},{10,11},{12,13},{... | collective-permute-start | bytes 3032 | tf_op jit(solution)/shard_map/ppermute | solution.py:23
  73.3 6.6 %collective-permute-start.16 = (f32[8,10,1]{2,1,0:T(8,128)S(1)}, f32[8,10,1]{2,1,0:T(8,128)S(1)}, u32[]{:S(2)}, u32[]{:S(2)}) collective-permute-start(f32[8,10,1]{2,1,0:T(8,128)S(1)} %get-tuple-element.100), channel_id=1, source_target_pairs={{1,0},{2,1},{3,2},{5,4},{6,5},{7,6},{9,8},{10,9},{11,10},{13,12},{... | collective-permute-start | bytes 968 | tf_op jit(solution)/shard_map/ppermute | solution.py:25
  74.6 6.9 %collective-permute-start.17 = (f32[8,10,1]{2,1,0:T(8,128)S(1)}, f32[8,10,1]{2,1,0:T(8,128)S(1)}, u32[]{:S(2)}, u32[]{:S(2)}) collective-permute-start(f32[8,10,1]{2,1,0:T(8,128)S(1)} %get-tuple-element.101), channel_id=1, source_target_pairs={{0,1},{1,2},{2,3},{4,5},{5,6},{6,7},{8,9},{9,10},{10,11},{12,13},{... | collective-permute-start | bytes 968 | tf_op jit(solution)/shard_map/ppermute | solution.py:23
  81.6 5.9 %collective-permute-start.18 = (f32[1,8,64]{2,1,0:T(8,128)S(1)}, f32[1,8,64]{2,1,0:T(8,128)S(1)}, u32[]{:S(2)}, u32[]{:S(2)}) collective-permute-start(f32[1,8,64]{2,1,0:T(8,128)S(1)} %get-tuple-element.131), channel_id=1, source_target_pairs={{16,0},{17,1},{18,2},{19,3},{20,4},{21,5},{22,6},{23,7},{24,8},{25... | collective-permute-start | bytes 6152 | tf_op jit(solution)/shard_map/ppermute | solution.py:25
  94.0 6.6 %collective-permute-start.22 = (f32[8,10,1]{2,1,0:T(8,128)S(1)}, f32[8,10,1]{2,1,0:T(8,128)S(1)}, u32[]{:S(2)}, u32[]{:S(2)}) collective-permute-start(f32[8,10,1]{2,1,0:T(8,128)S(1)} %get-tuple-element.98), channel_id=1, source_target_pairs={{1,0},{2,1},{3,2},{5,4},{6,5},{7,6},{9,8},{10,9},{11,10},{13,12},{... | collective-permute-start | bytes 968 | tf_op jit(solution)/shard_map/ppermute | solution.py:25
  95.3 6.9 %collective-permute-start.23 = (f32[8,10,1]{2,1,0:T(8,128)S(1)}, f32[8,10,1]{2,1,0:T(8,128)S(1)}, u32[]{:S(2)}, u32[]{:S(2)}) collective-permute-start(f32[8,10,1]{2,1,0:T(8,128)S(1)} %get-tuple-element.99), channel_id=1, source_target_pairs={{0,1},{1,2},{2,3},{4,5},{5,6},{6,7},{8,9},{9,10},{10,11},{12,13},{... | collective-permute-start | bytes 968 | tf_op jit(solution)/shard_map/ppermute | solution.py:23
  116.5 7.1 %collective-permute-start.27 = (f32[9,3,32]{2,1,0:T(4,128)S(1)}, f32[9,3,32]{2,1,0:T(4,128)S(1)}, u32[]{:S(2)}, u32[]{:S(2)}) collective-permute-start(f32[9,3,32]{2,1,0:T(4,128)S(1)} %get-tuple-element.137), channel_id=1, source_target_pairs={{4,0},{8,4},{12,8},{5,1},{9,5},{13,9},{6,2},{10,6},{14,10},{7,3},{... | collective-permute-start | bytes 10376 | tf_op jit(solution)/shard_map/ppermute | solution.py:25
  123.7 6.2 %collective-permute-start.28 = (f32[9,10,3]{2,1,0:T(8,128)S(1)}, f32[9,10,3]{2,1,0:T(8,128)S(1)}, u32[]{:S(2)}, u32[]{:S(2)}) collective-permute-start(f32[9,10,3]{2,1,0:T(8,128)S(1)} %get-tuple-element.84), channel_id=1, source_target_pairs={{0,1},{1,2},{2,3},{4,5},{5,6},{6,7},{8,9},{9,10},{10,11},{12,13},{... | collective-permute-start | bytes 3248 | tf_op jit(solution)/shard_map/ppermute | solution.py:23
  128.0 6.2 %collective-permute-start.29 = (f32[9,10,3]{2,1,0:T(8,128)S(1)}, f32[9,10,3]{2,1,0:T(8,128)S(1)}, u32[]{:S(2)}, u32[]{:S(2)}) collective-permute-start(f32[9,10,3]{2,1,0:T(8,128)S(1)} %get-tuple-element.85), channel_id=1, source_target_pairs={{1,0},{2,1},{3,2},{5,4},{6,5},{7,6},{9,8},{10,9},{11,10},{13,12},{... | collective-permute-start | bytes 3248 | tf_op jit(solution)/shard_map/ppermute | solution.py:25
  147.8 6.2 %collective-permute-start.34 = (f32[8,10,1]{2,1,0:T(8,128)S(1)}, f32[8,10,1]{2,1,0:T(8,128)S(1)}, u32[]{:S(2)}, u32[]{:S(2)}) collective-permute-start(f32[8,10,1]{2,1,0:T(8,128)S(1)} %get-tuple-element.96), channel_id=1, source_target_pairs={{1,0},{2,1},{3,2},{5,4},{6,5},{7,6},{9,8},{10,9},{11,10},{13,12},{... | collective-permute-start | bytes 968 | tf_op jit(solution)/shard_map/ppermute | solution.py:25
  149.1 6.4 %collective-permute-start.35 = (f32[8,10,1]{2,1,0:T(8,128)S(1)}, f32[8,10,1]{2,1,0:T(8,128)S(1)}, u32[]{:S(2)}, u32[]{:S(2)}) collective-permute-start(f32[8,10,1]{2,1,0:T(8,128)S(1)} %get-tuple-element.97), channel_id=1, source_target_pairs={{0,1},{1,2},{2,3},{4,5},{5,6},{6,7},{8,9},{9,10},{10,11},{12,13},{... | collective-permute-start | bytes 968 | tf_op jit(solution)/shard_map/ppermute | solution.py:23
  168.0 6.5 %collective-permute-start.40 = (f32[8,10,1]{2,1,0:T(8,128)S(1)}, f32[8,10,1]{2,1,0:T(8,128)S(1)}, u32[]{:S(2)}, u32[]{:S(2)}) collective-permute-start(f32[8,10,1]{2,1,0:T(8,128)S(1)} %get-tuple-element.94), channel_id=1, source_target_pairs={{1,0},{2,1},{3,2},{5,4},{6,5},{7,6},{9,8},{10,9},{11,10},{13,12},{... | collective-permute-start | bytes 968 | tf_op jit(solution)/shard_map/ppermute | solution.py:25
  169.3 6.8 %collective-permute-start.41 = (f32[8,10,1]{2,1,0:T(8,128)S(1)}, f32[8,10,1]{2,1,0:T(8,128)S(1)}, u32[]{:S(2)}, u32[]{:S(2)}) collective-permute-start(f32[8,10,1]{2,1,0:T(8,128)S(1)} %get-tuple-element.95), channel_id=1, source_target_pairs={{0,1},{1,2},{2,3},{4,5},{5,6},{6,7},{8,9},{9,10},{10,11},{12,13},{... | collective-permute-start | bytes 968 | tf_op jit(solution)/shard_map/ppermute | solution.py:23
  185.4 6.0 %collective-permute-start.42 = (f32[1,16,128]{2,1,0:T(8,128)S(1)}, f32[1,16,128]{2,1,0:T(8,128)S(1)}, u32[]{:S(2)}, u32[]{:S(2)}) collective-permute-start(f32[1,16,128]{2,1,0:T(8,128)S(1)} %get-tuple-element.77), channel_id=1, source_target_pairs={{16,0},{17,1},{18,2},{19,3},{20,4},{21,5},{22,6},{23,7},{24,8},{25... | collective-permute-start | bytes 24584 | tf_op jit(solution)/shard_map/ppermute | solution.py:25
  199.2 7.4 %collective-permute-start.46 = (f32[14,18,1]{2,1,0:T(8,128)S(1)}, f32[14,18,1]{2,1,0:T(8,128)S(1)}, u32[]{:S(2)}, u32[]{:S(2)}) collective-permute-start(f32[14,18,1]{2,1,0:T(8,128)S(1)} %get-tuple-element.38), channel_id=1, source_target_pairs={{1,0},{2,1},{3,2},{5,4},{6,5},{7,6},{9,8},{10,9},{11,10},{13,12},{... | collective-permute-start | bytes 3032 | tf_op jit(solution)/shard_map/ppermute | solution.py:25
  200.5 7.5 %collective-permute-start.47 = (f32[14,18,1]{2,1,0:T(8,128)S(1)}, f32[14,18,1]{2,1,0:T(8,128)S(1)}, u32[]{:S(2)}, u32[]{:S(2)}) collective-permute-start(f32[14,18,1]{2,1,0:T(8,128)S(1)} %get-tuple-element.39), channel_id=1, source_target_pairs={{0,1},{1,2},{2,3},{4,5},{5,6},{6,7},{8,9},{9,10},{10,11},{12,13},{... | collective-permute-start | bytes 3032 | tf_op jit(solution)/shard_map/ppermute | solution.py:23
  215.5 6.4 %collective-permute-start.50 = (f32[14,1,128]{2,1,0:T(1,128)S(1)}, f32[14,1,128]{2,1,0:T(1,128)S(1)}, u32[]{:S(2)}, u32[]{:S(2)}) collective-permute-start(f32[14,1,128]{2,1,0:T(1,128)S(1)} %get-tuple-element.57), channel_id=1, source_target_pairs={{4,0},{8,4},{12,8},{5,1},{9,5},{13,9},{6,2},{10,6},{14,10},{7,3},{... | collective-permute-start | bytes 21512 | tf_op jit(solution)/shard_map/ppermute | solution.py:25
  222.8 7.5 %collective-permute-start.52 = (f32[14,18,1]{2,1,0:T(8,128)S(1)}, f32[14,18,1]{2,1,0:T(8,128)S(1)}, u32[]{:S(2)}, u32[]{:S(2)}) collective-permute-start(f32[14,18,1]{2,1,0:T(8,128)S(1)} %get-tuple-element.36), channel_id=1, source_target_pairs={{1,0},{2,1},{3,2},{5,4},{6,5},{7,6},{9,8},{10,9},{11,10},{13,12},{... | collective-permute-start | bytes 3032 | tf_op jit(solution)/shard_map/ppermute | solution.py:25
  224.1 7.6 %collective-permute-start.53 = (f32[14,18,1]{2,1,0:T(8,128)S(1)}, f32[14,18,1]{2,1,0:T(8,128)S(1)}, u32[]{:S(2)}, u32[]{:S(2)}) collective-permute-start(f32[14,18,1]{2,1,0:T(8,128)S(1)} %get-tuple-element.37), channel_id=1, source_target_pairs={{0,1},{1,2},{2,3},{4,5},{5,6},{6,7},{8,9},{9,10},{10,11},{12,13},{... | collective-permute-start | bytes 3032 | tf_op jit(solution)/shard_map/ppermute | solution.py:23
  239.1 6.4 %collective-permute-start.56 = (f32[14,1,128]{2,1,0:T(1,128)S(1)}, f32[14,1,128]{2,1,0:T(1,128)S(1)}, u32[]{:S(2)}, u32[]{:S(2)}) collective-permute-start(f32[14,1,128]{2,1,0:T(1,128)S(1)} %get-tuple-element.55), channel_id=1, source_target_pairs={{4,0},{8,4},{12,8},{5,1},{9,5},{13,9},{6,2},{10,6},{14,10},{7,3},{... | collective-permute-start | bytes 21512 | tf_op jit(solution)/shard_map/ppermute | solution.py:25
  246.5 7.5 %collective-permute-start.58 = (f32[14,18,1]{2,1,0:T(8,128)S(1)}, f32[14,18,1]{2,1,0:T(8,128)S(1)}, u32[]{:S(2)}, u32[]{:S(2)}) collective-permute-start(f32[14,18,1]{2,1,0:T(8,128)S(1)} %get-tuple-element.34), channel_id=1, source_target_pairs={{1,0},{2,1},{3,2},{5,4},{6,5},{7,6},{9,8},{10,9},{11,10},{13,12},{... | collective-permute-start | bytes 3032 | tf_op jit(solution)/shard_map/ppermute | solution.py:25
  247.8 7.6 %collective-permute-start.59 = (f32[14,18,1]{2,1,0:T(8,128)S(1)}, f32[14,18,1]{2,1,0:T(8,128)S(1)}, u32[]{:S(2)}, u32[]{:S(2)}) collective-permute-start(f32[14,18,1]{2,1,0:T(8,128)S(1)} %get-tuple-element.35), channel_id=1, source_target_pairs={{0,1},{1,2},{2,3},{4,5},{5,6},{6,7},{8,9},{9,10},{10,11},{12,13},{... | collective-permute-start | bytes 3032 | tf_op jit(solution)/shard_map/ppermute | solution.py:23
  256.9 6.1 %collective-permute-start.61 = (f32[3,1,16,128]{3,2,1,0:T(8,128)S(1)}, f32[3,1,16,128]{3,2,1,0:T(8,128)S(1)}, u32[]{:S(2)}, u32[]{:S(2)}) collective-permute-start(f32[3,1,16,128]{3,2,1,0:T(8,128)S(1)} %get-tuple-element.24), channel_id=1, source_target_pairs={{0,16},{1,17},{2,18},{3,19},{4,20},{5,21},{6,22},{7,23},{8,24},{9,... | collective-permute-start | bytes 73736 | tf_op jit(solution)/shard_map/ppermute | solution.py:23
  263.0 6.4 %collective-permute-start.62 = (f32[3,14,1,128]{3,2,1,0:T(1,128)S(1)}, f32[3,14,1,128]{3,2,1,0:T(1,128)S(1)}, u32[]{:S(2)}, u32[]{:S(2)}) collective-permute-start(f32[3,14,1,128]{3,2,1,0:T(1,128)S(1)} %get-tuple-element.18), channel_id=1, source_target_pairs={{4,0},{8,4},{12,8},{5,1},{9,5},{13,9},{6,2},{10,6},{14,10},{7,3},{... | collective-permute-start | bytes 64520 | tf_op jit(solution)/shard_map/ppermute | solution.py:25
  264.3 5.9 %collective-permute-start.63 = (f32[3,14,1,128]{3,2,1,0:T(1,128)S(1)}, f32[3,14,1,128]{3,2,1,0:T(1,128)S(1)}, u32[]{:S(2)}, u32[]{:S(2)}) collective-permute-start(f32[3,14,1,128]{3,2,1,0:T(1,128)S(1)} %get-tuple-element.17), channel_id=1, source_target_pairs={{0,4},{4,8},{8,12},{1,5},{5,9},{9,13},{2,6},{6,10},{10,14},{3,7},{... | collective-permute-start | bytes 64520 | tf_op jit(solution)/shard_map/ppermute | solution.py:23
  270.5 12.7 %collective-permute-start.64 = (f32[3,14,18,1]{3,2,1,0:T(8,128)S(1)}, f32[3,14,18,1]{3,2,1,0:T(8,128)S(1)}, u32[]{:S(2)}, u32[]{:S(2)}) collective-permute-start(f32[3,14,18,1]{3,2,1,0:T(8,128)S(1)} %get-tuple-element.13), channel_id=1, source_target_pairs={{1,0},{2,1},{3,2},{5,4},{6,5},{7,6},{9,8},{10,9},{11,10},{13,12},{... | collective-permute-start | bytes 9080 | tf_op jit(solution)/shard_map/ppermute | solution.py:25
  271.8 13.2 %collective-permute-start.65 = (f32[3,14,18,1]{3,2,1,0:T(8,128)S(1)}, f32[3,14,18,1]{3,2,1,0:T(8,128)S(1)}, u32[]{:S(2)}, u32[]{:S(2)}) collective-permute-start(f32[3,14,18,1]{3,2,1,0:T(8,128)S(1)} %get-tuple-element.14), channel_id=1, source_target_pairs={{0,1},{1,2},{2,3},{4,5},{5,6},{6,7},{8,9},{9,10},{10,11},{12,13},{... | collective-permute-start | bytes 9080 | tf_op jit(solution)/shard_map/ppermute | solution.py:23
  286.7 6.1 %collective-permute-start.67 = (f32[3,1,16,128]{3,2,1,0:T(8,128)S(1)}, f32[3,1,16,128]{3,2,1,0:T(8,128)S(1)}, u32[]{:S(2)}, u32[]{:S(2)}) collective-permute-start(f32[3,1,16,128]{3,2,1,0:T(8,128)S(1)} %get-tuple-element.19), channel_id=1, source_target_pairs={{0,16},{1,17},{2,18},{3,19},{4,20},{5,21},{6,22},{7,23},{8,24},{9,... | collective-permute-start | bytes 73736 | tf_op jit(solution)/shard_map/ppermute | solution.py:23
  292.8 6.5 %collective-permute-start.68 = (f32[3,14,1,128]{3,2,1,0:T(1,128)S(1)}, f32[3,14,1,128]{3,2,1,0:T(1,128)S(1)}, u32[]{:S(2)}, u32[]{:S(2)}) collective-permute-start(f32[3,14,1,128]{3,2,1,0:T(1,128)S(1)} %get-tuple-element.16), channel_id=1, source_target_pairs={{4,0},{8,4},{12,8},{5,1},{9,5},{13,9},{6,2},{10,6},{14,10},{7,3},{... | collective-permute-start | bytes 64520 | tf_op jit(solution)/shard_map/ppermute | solution.py:25
  294.1 6.0 %collective-permute-start.69 = (f32[3,14,1,128]{3,2,1,0:T(1,128)S(1)}, f32[3,14,1,128]{3,2,1,0:T(1,128)S(1)}, u32[]{:S(2)}, u32[]{:S(2)}) collective-permute-start(f32[3,14,1,128]{3,2,1,0:T(1,128)S(1)} %get-tuple-element.15), channel_id=1, source_target_pairs={{0,4},{4,8},{8,12},{1,5},{5,9},{9,13},{2,6},{6,10},{10,14},{3,7},{... | collective-permute-start | bytes 64520 | tf_op jit(solution)/shard_map/ppermute | solution.py:23
  300.4 11.6 %collective-permute-start.70 = (f32[3,14,18,1]{3,2,1,0:T(8,128)S(1)}, f32[3,14,18,1]{3,2,1,0:T(8,128)S(1)}, u32[]{:S(2)}, u32[]{:S(2)}) collective-permute-start(f32[3,14,18,1]{3,2,1,0:T(8,128)S(1)} %get-tuple-element.11), channel_id=1, source_target_pairs={{1,0},{2,1},{3,2},{5,4},{6,5},{7,6},{9,8},{10,9},{11,10},{13,12},{... | collective-permute-start | bytes 9080 | tf_op jit(solution)/shard_map/ppermute | solution.py:25
  301.7 12.0 %collective-permute-start.71 = (f32[3,14,18,1]{3,2,1,0:T(8,128)S(1)}, f32[3,14,18,1]{3,2,1,0:T(8,128)S(1)}, u32[]{:S(2)}, u32[]{:S(2)}) collective-permute-start(f32[3,14,18,1]{3,2,1,0:T(8,128)S(1)} %get-tuple-element.12), channel_id=1, source_target_pairs={{0,1},{1,2},{2,3},{4,5},{5,6},{6,7},{8,9},{9,10},{10,11},{12,13},{... | collective-permute-start | bytes 9080 | tf_op jit(solution)/shard_map/ppermute | solution.py:23
  321.1 7.7 %collective-permute-start.74 = (f32[14,1,128]{2,1,0:T(1,128)S(1)}, f32[14,1,128]{2,1,0:T(1,128)S(1)}, u32[]{:S(2)}, u32[]{:S(2)}) collective-permute-start(f32[14,1,128]{2,1,0:T(1,128)S(1)} %get-tuple-element.51), channel_id=1, source_target_pairs={{4,0},{8,4},{12,8},{5,1},{9,5},{13,9},{6,2},{10,6},{14,10},{7,3},{... | collective-permute-start | bytes 21512 | tf_op jit(solution)/shard_map/ppermute | solution.py:25
  322.4 7.2 %collective-permute-start.75 = (f32[14,1,128]{2,1,0:T(1,128)S(1)}, f32[14,1,128]{2,1,0:T(1,128)S(1)}, u32[]{:S(2)}, u32[]{:S(2)}) collective-permute-start(f32[14,1,128]{2,1,0:T(1,128)S(1)} %get-tuple-element.50), channel_id=1, source_target_pairs={{0,4},{4,8},{8,12},{1,5},{5,9},{9,13},{2,6},{6,10},{10,14},{3,7},{... | collective-permute-start | bytes 21512 | tf_op jit(solution)/shard_map/ppermute | solution.py:23
  329.8 7.5 %collective-permute-start.76 = (f32[14,18,1]{2,1,0:T(8,128)S(1)}, f32[14,18,1]{2,1,0:T(8,128)S(1)}, u32[]{:S(2)}, u32[]{:S(2)}) collective-permute-start(f32[14,18,1]{2,1,0:T(8,128)S(1)} %get-tuple-element.32), channel_id=1, source_target_pairs={{1,0},{2,1},{3,2},{5,4},{6,5},{7,6},{9,8},{10,9},{11,10},{13,12},{... | collective-permute-start | bytes 3032 | tf_op jit(solution)/shard_map/ppermute | solution.py:25
  331.1 7.6 %collective-permute-start.77 = (f32[14,18,1]{2,1,0:T(8,128)S(1)}, f32[14,18,1]{2,1,0:T(8,128)S(1)}, u32[]{:S(2)}, u32[]{:S(2)}) collective-permute-start(f32[14,18,1]{2,1,0:T(8,128)S(1)} %get-tuple-element.33), channel_id=1, source_target_pairs={{0,1},{1,2},{2,3},{4,5},{5,6},{6,7},{8,9},{9,10},{10,11},{12,13},{... | collective-permute-start | bytes 3032 | tf_op jit(solution)/shard_map/ppermute | solution.py:23
  346.1 8.7 %collective-permute-start.80 = (f32[14,1,128]{2,1,0:T(1,128)S(1)}, f32[14,1,128]{2,1,0:T(1,128)S(1)}, u32[]{:S(2)}, u32[]{:S(2)}) collective-permute-start(f32[14,1,128]{2,1,0:T(1,128)S(1)} %get-tuple-element.49), channel_id=1, source_target_pairs={{4,0},{8,4},{12,8},{5,1},{9,5},{13,9},{6,2},{10,6},{14,10},{7,3},{... | collective-permute-start | bytes 21512 | tf_op jit(solution)/shard_map/ppermute | solution.py:25
  347.4 8.3 %collective-permute-start.81 = (f32[14,1,128]{2,1,0:T(1,128)S(1)}, f32[14,1,128]{2,1,0:T(1,128)S(1)}, u32[]{:S(2)}, u32[]{:S(2)}) collective-permute-start(f32[14,1,128]{2,1,0:T(1,128)S(1)} %get-tuple-element.48), channel_id=1, source_target_pairs={{0,4},{4,8},{8,12},{1,5},{5,9},{9,13},{2,6},{6,10},{10,14},{3,7},{... | collective-permute-start | bytes 21512 | tf_op jit(solution)/shard_map/ppermute | solution.py:23
  355.8 7.6 %collective-permute-start.82 = (f32[14,18,1]{2,1,0:T(8,128)S(1)}, f32[14,18,1]{2,1,0:T(8,128)S(1)}, u32[]{:S(2)}, u32[]{:S(2)}) collective-permute-start(f32[14,18,1]{2,1,0:T(8,128)S(1)} %get-tuple-element.30), channel_id=1, source_target_pairs={{1,0},{2,1},{3,2},{5,4},{6,5},{7,6},{9,8},{10,9},{11,10},{13,12},{... | collective-permute-start | bytes 3032 | tf_op jit(solution)/shard_map/ppermute | solution.py:25
  357.1 7.8 %collective-permute-start.83 = (f32[14,18,1]{2,1,0:T(8,128)S(1)}, f32[14,18,1]{2,1,0:T(8,128)S(1)}, u32[]{:S(2)}, u32[]{:S(2)}) collective-permute-start(f32[14,18,1]{2,1,0:T(8,128)S(1)} %get-tuple-element.31), channel_id=1, source_target_pairs={{0,1},{1,2},{2,3},{4,5},{5,6},{6,7},{8,9},{9,10},{10,11},{12,13},{... | collective-permute-start | bytes 3032 | tf_op jit(solution)/shard_map/ppermute | solution.py:23
  383.2 6.3 %collective-permute-start.86 = (f32[8,1,64]{2,1,0:T(1,128)S(1)}, f32[8,1,64]{2,1,0:T(1,128)S(1)}, u32[]{:S(2)}, u32[]{:S(2)}) collective-permute-start(f32[8,1,64]{2,1,0:T(1,128)S(1)} %get-tuple-element.109), channel_id=1, source_target_pairs={{4,0},{8,4},{12,8},{5,1},{9,5},{13,9},{6,2},{10,6},{14,10},{7,3},{... | collective-permute-start | bytes 6152 | tf_op jit(solution)/shard_map/ppermute | solution.py:25
  390.4 6.3 %collective-permute-start.88 = (f32[8,10,1]{2,1,0:T(8,128)S(1)}, f32[8,10,1]{2,1,0:T(8,128)S(1)}, u32[]{:S(2)}, u32[]{:S(2)}) collective-permute-start(f32[8,10,1]{2,1,0:T(8,128)S(1)} %get-tuple-element.92), channel_id=1, source_target_pairs={{1,0},{2,1},{3,2},{5,4},{6,5},{7,6},{9,8},{10,9},{11,10},{13,12},{... | collective-permute-start | bytes 968 | tf_op jit(solution)/shard_map/ppermute | solution.py:25
  391.7 6.6 %collective-permute-start.89 = (f32[8,10,1]{2,1,0:T(8,128)S(1)}, f32[8,10,1]{2,1,0:T(8,128)S(1)}, u32[]{:S(2)}, u32[]{:S(2)}) collective-permute-start(f32[8,10,1]{2,1,0:T(8,128)S(1)} %get-tuple-element.93), channel_id=1, source_target_pairs={{0,1},{1,2},{2,3},{4,5},{5,6},{6,7},{8,9},{9,10},{10,11},{12,13},{... | collective-permute-start | bytes 968 | tf_op jit(solution)/shard_map/ppermute | solution.py:23
  405.6 6.4 %collective-permute-start.92 = (f32[8,1,64]{2,1,0:T(1,128)S(1)}, f32[8,1,64]{2,1,0:T(1,128)S(1)}, u32[]{:S(2)}, u32[]{:S(2)}) collective-permute-start(f32[8,1,64]{2,1,0:T(1,128)S(1)} %get-tuple-element.107), channel_id=1, source_target_pairs={{4,0},{8,4},{12,8},{5,1},{9,5},{13,9},{6,2},{10,6},{14,10},{7,3},{... | collective-permute-start | bytes 6152 | tf_op jit(solution)/shard_map/ppermute | solution.py:25
  412.8 6.2 %collective-permute-start.94 = (f32[8,10,1]{2,1,0:T(8,128)S(1)}, f32[8,10,1]{2,1,0:T(8,128)S(1)}, u32[]{:S(2)}, u32[]{:S(2)}) collective-permute-start(f32[8,10,1]{2,1,0:T(8,128)S(1)} %get-tuple-element.90), channel_id=1, source_target_pairs={{1,0},{2,1},{3,2},{5,4},{6,5},{7,6},{9,8},{10,9},{11,10},{13,12},{... | collective-permute-start | bytes 968 | tf_op jit(solution)/shard_map/ppermute | solution.py:25
  414.1 6.5 %collective-permute-start.95 = (f32[8,10,1]{2,1,0:T(8,128)S(1)}, f32[8,10,1]{2,1,0:T(8,128)S(1)}, u32[]{:S(2)}, u32[]{:S(2)}) collective-permute-start(f32[8,10,1]{2,1,0:T(8,128)S(1)} %get-tuple-element.91), channel_id=1, source_target_pairs={{0,1},{1,2},{2,3},{4,5},{5,6},{6,7},{8,9},{9,10},{10,11},{12,13},{... | collective-permute-start | bytes 968 | tf_op jit(solution)/shard_map/ppermute | solution.py:23
  435.6 7.1 %collective-permute-start.99 = (f32[9,3,32]{2,1,0:T(4,128)S(1)}, f32[9,3,32]{2,1,0:T(4,128)S(1)}, u32[]{:S(2)}, u32[]{:S(2)}) collective-permute-start(f32[9,3,32]{2,1,0:T(4,128)S(1)} %get-tuple-element.135), channel_id=1, source_target_pairs={{4,0},{8,4},{12,8},{5,1},{9,5},{13,9},{6,2},{10,6},{14,10},{7,3},{... | collective-permute-start | bytes 10376 | tf_op jit(solution)/shard_map/ppermute | solution.py:25
  442.8 6.2 %collective-permute-start.100 = (f32[9,10,3]{2,1,0:T(8,128)S(1)}, f32[9,10,3]{2,1,0:T(8,128)S(1)}, u32[]{:S(2)}, u32[]{:S(2)}) collective-permute-start(f32[9,10,3]{2,1,0:T(8,128)S(1)} %get-tuple-element.82), channel_id=1, source_target_pairs={{0,1},{1,2},{2,3},{4,5},{5,6},{6,7},{8,9},{9,10},{10,11},{12,13},{... | collective-permute-start | bytes 3248 | tf_op jit(solution)/shard_map/ppermute | solution.py:23
  447.1 6.2 %collective-permute-start.101 = (f32[9,10,3]{2,1,0:T(8,128)S(1)}, f32[9,10,3]{2,1,0:T(8,128)S(1)}, u32[]{:S(2)}, u32[]{:S(2)}) collective-permute-start(f32[9,10,3]{2,1,0:T(8,128)S(1)} %get-tuple-element.83), channel_id=1, source_target_pairs={{1,0},{2,1},{3,2},{5,4},{6,5},{7,6},{9,8},{10,9},{11,10},{13,12},{... | collective-permute-start | bytes 3248 | tf_op jit(solution)/shard_map/ppermute | solution.py:25
  466.8 6.2 %collective-permute-start.106 = (f32[8,10,1]{2,1,0:T(8,128)S(1)}, f32[8,10,1]{2,1,0:T(8,128)S(1)}, u32[]{:S(2)}, u32[]{:S(2)}) collective-permute-start(f32[8,10,1]{2,1,0:T(8,128)S(1)} %get-tuple-element.88), channel_id=1, source_target_pairs={{1,0},{2,1},{3,2},{5,4},{6,5},{7,6},{9,8},{10,9},{11,10},{13,12},{... | collective-permute-start | bytes 968 | tf_op jit(solution)/shard_map/ppermute | solution.py:25
  468.1 6.4 %collective-permute-start.107 = (f32[8,10,1]{2,1,0:T(8,128)S(1)}, f32[8,10,1]{2,1,0:T(8,128)S(1)}, u32[]{:S(2)}, u32[]{:S(2)}) collective-permute-start(f32[8,10,1]{2,1,0:T(8,128)S(1)} %get-tuple-element.89), channel_id=1, source_target_pairs={{0,1},{1,2},{2,3},{4,5},{5,6},{6,7},{8,9},{9,10},{10,11},{12,13},{... | collective-permute-start | bytes 968 | tf_op jit(solution)/shard_map/ppermute | solution.py:23
  487.1 6.5 %collective-permute-start.112 = (f32[8,10,1]{2,1,0:T(8,128)S(1)}, f32[8,10,1]{2,1,0:T(8,128)S(1)}, u32[]{:S(2)}, u32[]{:S(2)}) collective-permute-start(f32[8,10,1]{2,1,0:T(8,128)S(1)} %get-tuple-element.86), channel_id=1, source_target_pairs={{1,0},{2,1},{3,2},{5,4},{6,5},{7,6},{9,8},{10,9},{11,10},{13,12},{... | collective-permute-start | bytes 968 | tf_op jit(solution)/shard_map/ppermute | solution.py:25
  488.4 6.8 %collective-permute-start.113 = (f32[8,10,1]{2,1,0:T(8,128)S(1)}, f32[8,10,1]{2,1,0:T(8,128)S(1)}, u32[]{:S(2)}, u32[]{:S(2)}) collective-permute-start(f32[8,10,1]{2,1,0:T(8,128)S(1)} %get-tuple-element.87), channel_id=1, source_target_pairs={{0,1},{1,2},{2,3},{4,5},{5,6},{6,7},{8,9},{9,10},{10,11},{12,13},{... | collective-permute-start | bytes 968 | tf_op jit(solution)/shard_map/ppermute | solution.py:23
  518.2 7.4 %collective-permute-start.118 = (f32[14,18,1]{2,1,0:T(8,128)S(1)}, f32[14,18,1]{2,1,0:T(8,128)S(1)}, u32[]{:S(2)}, u32[]{:S(2)}) collective-permute-start(f32[14,18,1]{2,1,0:T(8,128)S(1)} %get-tuple-element.28), channel_id=1, source_target_pairs={{1,0},{2,1},{3,2},{5,4},{6,5},{7,6},{9,8},{10,9},{11,10},{13,12},{... | collective-permute-start | bytes 3032 | tf_op jit(solution)/shard_map/ppermute | solution.py:25
  519.5 7.5 %collective-permute-start.119 = (f32[14,18,1]{2,1,0:T(8,128)S(1)}, f32[14,18,1]{2,1,0:T(8,128)S(1)}, u32[]{:S(2)}, u32[]{:S(2)}) collective-permute-start(f32[14,18,1]{2,1,0:T(8,128)S(1)} %get-tuple-element.29), channel_id=1, source_target_pairs={{0,1},{1,2},{2,3},{4,5},{5,6},{6,7},{8,9},{9,10},{10,11},{12,13},{... | collective-permute-start | bytes 3032 | tf_op jit(solution)/shard_map/ppermute | solution.py:23
  534.4 6.4 %collective-permute-start.122 = (f32[14,1,128]{2,1,0:T(1,128)S(1)}, f32[14,1,128]{2,1,0:T(1,128)S(1)}, u32[]{:S(2)}, u32[]{:S(2)}) collective-permute-start(f32[14,1,128]{2,1,0:T(1,128)S(1)} %get-tuple-element.45), channel_id=1, source_target_pairs={{4,0},{8,4},{12,8},{5,1},{9,5},{13,9},{6,2},{10,6},{14,10},{7,3},{... | collective-permute-start | bytes 21512 | tf_op jit(solution)/shard_map/ppermute | solution.py:25
  541.7 7.5 %collective-permute-start.124 = (f32[14,18,1]{2,1,0:T(8,128)S(1)}, f32[14,18,1]{2,1,0:T(8,128)S(1)}, u32[]{:S(2)}, u32[]{:S(2)}) collective-permute-start(f32[14,18,1]{2,1,0:T(8,128)S(1)} %get-tuple-element.26), channel_id=1, source_target_pairs={{1,0},{2,1},{3,2},{5,4},{6,5},{7,6},{9,8},{10,9},{11,10},{13,12},{... | collective-permute-start | bytes 3032 | tf_op jit(solution)/shard_map/ppermute | solution.py:25
  543.0 7.6 %collective-permute-start.125 = (f32[14,18,1]{2,1,0:T(8,128)S(1)}, f32[14,18,1]{2,1,0:T(8,128)S(1)}, u32[]{:S(2)}, u32[]{:S(2)}) collective-permute-start(f32[14,18,1]{2,1,0:T(8,128)S(1)} %get-tuple-element.27), channel_id=1, source_target_pairs={{0,1},{1,2},{2,3},{4,5},{5,6},{6,7},{8,9},{9,10},{10,11},{12,13},{... | collective-permute-start | bytes 3032 | tf_op jit(solution)/shard_map/ppermute | solution.py:23
  (64 other events, 453.2 us)
where the time goes:
time: 561 us; the launch traced here: 551 us
  starting transfers between devices  366 us (65%)
  waiting for transfers between devices  130 us (23%)
  local copies, waits for them, and re-layouts  38.6 us (7%)
  other arithmetic  15.4 us (3%)
    ppermute x63, starting transfers between devices, with_halo(): lax.ppermute(tail, axis, [(i, (i + 1) % count) for i in range(ends)])  284 us
    ppermute x63, starting transfers between devices, with_halo(): lax.ppermute(head, axis, [((i + 1) % count, i) for i in range(ends)])  81.5 us
    ppermute x63, waiting for transfers between devices, with_halo(): lax.ppermute(tail, axis, [(i, (i + 1) % count) for i in range(ends)])  71.7 us
    ppermute x63, waiting for transfers between devices, with_halo(): lax.ppermute(head, axis, [((i + 1) % count, i) for i in range(ends)])  58.1 us
    reshape x4, local copies, waits for them, and re-layouts, restrict(): values.reshape(extent_x // 2, 2, extent_y // 2, 2, extent_z // 2, 2)  17 us
    reshape x4, local copies, waits for them, and re-layouts, prolong(): return spread.reshape(2 * extent_x, 2 * extent_y, 2 * extent_z)  12 us
  transfers between devices with their start and end apart: 126, of which 84 were waited for; matrix products, arithmetic and copies ran while one was open for 0% of the time, Pallas kernels for 0%

commit v1 on v0

v1 whole, which is shorter than its diff:
```python
import functools

import jax
import jax.numpy as jnp
from jax import lax
from jax.experimental import pallas as pl
from jax.experimental.pallas import tpu as pltpu
from jax.sharding import PartitionSpec as P

OMEGA = 0.8
W = OMEGA / 6.0
C0, C1, C2 = W, 4.0 * W, 16.0 * W
SIDE = 8
PLANE = ("gx", "gy")


def up(v, axis):
    return pltpu.roll(v, v.shape[axis] - 1, axis)


def down(v, axis):
    return pltpu.roll(v, 1, axis)


def mix(s, i):
    c = s[i]
    near = (s[i - 1] + s[i + 1]) + (up(c, 0) + down(c, 0)) + (up(c, 1) + down(c, 1))
    return (1.0 - OMEGA) * c + W * near


def each(n, step):
    lax.fori_loop(0, n, lambda i, _: step(i), None, unroll=2 if n % 2 == 0 else 1)


def iota(shape, axis):
    return lax.broadcasted_iota(jnp.int32, shape, axis)


def pair_matrix(rows, columns, value):
    hit = (iota((rows, columns), 0) >> 1) == iota((rows, columns), 1)
    return jnp.where(hit, value, 0.0).astype(jnp.float32)


def spread_matrix(rows, columns):
    hit = (iota((rows, columns), 1) >> 1) == iota((rows, columns), 0)
    return jnp.where(hit, 1.0, 0.0).astype(jnp.float32)


def dot(a, b):
    return jnp.dot(a, b, precision=lax.Precision.HIGHEST, preferred_element_type=jnp.float32)


def window_mask(shape, y_first, y_count, z_first, z_count):
    y = iota(shape, 0) + y_first
    z = iota(shape, 1) + z_first
    good = (y >= 0) & (y < y_count) & (z >= 0) & (z < z_count)
    return jnp.where(good, 1.0, 0.0).astype(jnp.float32)


class Sizes:
    def __init__(self, gx, gy, gz, bx, by, bz):
        self.gx, self.gy, self.gz = gx, gy, gz
        self.bx, self.by, self.bz = bx, by, bz
        self.rows, self.lanes = by + 2 * SIDE, 2 * bz
        self.one = gx == 2
        self.c1_n = bx // 2 + (1 if self.one else 2)
        self.c2_n = bx // 2 + (2 if self.one else 4)
        self.yf_n = bx + (3 if self.one else 6)
        self.nx1, self.ny1 = gx * bx // 2, gy * by // 2
        self.rows1 = self.ny1 + SIDE
        self.rows1p = -(-self.rows1 // 16) * 16
        self.l1 = bz
        self.c1_rows = by // 2 + 4
        self.c2_rows = by // 2 + 8
        self.edge = 5
        self.edge_sets = 1 if self.one else 2
        self.pack1 = self.c1_n * self.c1_rows + self.edge_sets * self.edge * 2 * by
        self.pack2 = self.c2_n * self.c2_rows + self.yf_n * 8

    def c1_first(self, i):
        return -i if self.one else -1

    def c2_first(self, i):
        return -2 * i if self.one else -2

    def yf_first(self, i):
        return -3 * i if self.one else -3


def slab_kernel(k, p_ref, w_ref, right_ref, left_ref):
    bx, bz = k.bx, k.bz
    half, part = bz // 2, bz // 4
    lane = iota((k.by, bz), 1)
    for x in range(bx):
        p = pltpu.roll(p_ref[x], half, 1)
        a, b = w_ref[0, x], w_ref[1, x]
        right_ref[x] = jnp.where(lane < half, p, jnp.where(lane < half + part, pltpu.roll(a, bz - part, 1), b))
        left_ref[x] = jnp.where(lane >= half, p, jnp.where(lane < part, a, pltpu.roll(b, part, 1)))
    for q in range(-(-bx // 4)):
        r_all, l_all = jnp.zeros((k.by, bz), jnp.float32), jnp.zeros((k.by, bz), jnp.float32)
        for r in range(min(4, bx - 4 * q)):
            c = w_ref[2, 4 * q + r]
            here = (lane >= part * r) & (lane < part * (r + 1))
            r_all = jnp.where(here, pltpu.roll(c, (part * r + part) % bz, 1), r_all)
            l_all = jnp.where(here, pltpu.roll(c, part * r, 1) if r else c, l_all)
        right_ref[bx + q] = r_all
        left_ref[bx + q] = l_all


def lane_roll(v, shift):
    shift = shift % v.shape[1]
    return pltpu.roll(v, shift, 1) if shift else v


def pressure_window(k, p, low, high):
    half = k.bz // 2
    lane = iota(p.shape, 1)
    p = pltpu.roll(p, half, 1)
    return jnp.concatenate([jnp.where(lane < half, low, p), jnp.where(lane < half, p, high)], axis=1)


def wind_window(k, w, low, low_at, high, high_at):
    half, part = k.bz // 2, k.bz // 4
    lane = iota(w.shape, 1)
    w = pltpu.roll(w, half, 1)
    first = jnp.where(lane >= half, w, jnp.where(lane >= part, lane_roll(low, part - low_at), 0.0))
    second = jnp.where(lane < half, w, jnp.where(lane < half + part, lane_roll(high, half - high_at), 0.0))
    return jnp.concatenate([first, second], axis=1)


def place():
    return lax.axis_index("gx"), lax.axis_index("gy"), lax.axis_index("gz")


def fine_mask(k, iy, iz):
    return window_mask((k.rows, k.lanes), iy * k.by - SIDE, k.gy * k.by, iz * k.bz - k.bz // 2, k.gz * k.bz)


def x_inside(k, ix, plane):
    place_x = ix * k.bx + plane
    return jnp.where((place_x >= 0) & (place_x < k.gx * k.bx), 1.0, 0.0).astype(jnp.float32)


def restrict_planes(src, first, n, half_ref, out, value):
    rows, lanes = src.shape[1], src.shape[2]
    a = pair_matrix(lanes, half_ref.shape[2], value)

    def step(j):
        s = src[first + 2 * j] + src[first + 2 * j + 1]
        half_ref[j] = dot(s + up(s, 0), a)

    for j in range(n):
        step(j)
    for j in range(n):
        out[j] = half_ref[j, pl.ds(0, rows // 2, stride=2), :]


def zero(ref):
    ref[...] = jnp.zeros(ref.shape, ref.dtype)


def first_kernel(k, p_ref, low_ref, high_ref, win_ref, send_a, send_b, pack_ref, b, m, half_ref, c1):
    ix, iy, iz = place()
    bx, by = k.bx, k.by
    pad = 3
    zero(b)
    zero(m)
    for x in range(bx):
        w = pressure_window(k, p_ref[x], low_ref[x], high_ref[x])
        win_ref[x] = w
        b[x + pad, SIDE:SIDE + by, :] = w
    tail = lax.rem(iy, 2) == 0
    for x in range(bx):
        head_rows, tail_rows = win_ref[x, :8, :], win_ref[x, by - 8:, :]
        send_a[x] = jnp.where(tail, tail_rows, head_rows)
        send_b[x] = jnp.where(tail, head_rows, tail_rows)
    mask = fine_mask(k, iy, iz)

    def step1(i):
        m[i + pad - 1] = mix(b, i + pad - 1) * (mask * x_inside(k, ix, i - 1))

    each(bx + 2, step1)

    def step2(i):
        b[i + pad - 2] = mix(m, i + pad - 2)

    each(bx + 4, step2)
    restrict_planes(b, pad - 2, bx // 2 + 2, half_ref, c1, 0.125)
    start = (k.c1_first(ix) + 1) if k.one else 0
    for j in range(k.c1_n):
        pack_ref[j * k.c1_rows:(j + 1) * k.c1_rows, :] = c1[start + j, 2:2 + k.c1_rows, :]
    at = k.c1_n * k.c1_rows
    starts = [(1 - ix) * (bx - k.edge)] if k.one else [0, bx - k.edge]
    for first in starts:
        for j in range(k.edge):
            for t in range(2):
                pack_ref[at:at + by, :] = win_ref[first + j, :, t * k.bz:(t + 1) * k.bz]
                at += by


def coarse(k, iz, b1, m1, e1, half_ref, b2, u2, v2):
    n1, n2 = k.nx1, k.nx1 // 2
    rows1, rows2, l1 = k.rows1, k.rows1p // 2, k.l1
    y0 = -(SIDE // 2)
    mask1 = window_mask((rows1, l1), y0, k.ny1, iz * (k.bz // 2) - k.bz // 4, k.gz * (k.bz // 2))
    lane2 = iota((rows2, l1), 1)
    mask2 = window_mask((rows2, l1), y0 // 2, k.ny1 // 2, iz * (k.bz // 4) - k.bz // 8, k.gz * (k.bz // 4))
    mask2 = jnp.where(lane2 < l1 // 2, mask2, 0.0)
    zero(m1)
    zero(e1)
    zero(u2)
    zero(v2)
    for i in range(n1):
        b1[i + 2] = b1[i + 2] * mask1

    def pre(i):
        c = mix(b1, i + 2) * mask1
        m1[i + 2] = c
        e1[i + 2] = C1 * (b1[i + 2] + c)

    each(n1, pre)
    a = pair_matrix(l1, l1, 0.125)
    for j in range(n2):
        s = mix(m1, 2 * j + 2) + mix(m1, 2 * j + 3)
        half_ref[j, :rows1, :] = dot(s + up(s, 0), a)
        if k.rows1p > rows1:
            half_ref[j, rows1:, :] = jnp.zeros((k.rows1p - rows1, l1), jnp.float32)
    for j in range(n2):
        s = half_ref[j, pl.ds(0, rows2, stride=2), :] * (mask2 * C2)
        b2[j] = s
        u2[j + 1] = s
    src, dst = u2, v2
    for _ in range(3):
        for j in range(n2):
            dst[j + 1] = (mix(src, j + 1) + b2[j]) * mask2
        src, dst = dst, src
    spread = spread_matrix(l1, l1)
    for j in range(n2):
        e = dot(src[j + 1], spread)
        half_ref[j, pl.ds(0, rows2, stride=2), :] = e
        half_ref[j, pl.ds(1, rows2, stride=2), :] = e
    for j in range(n2):
        e = half_ref[j, :rows1, :]
        e1[2 * j + 2] += e
        e1[2 * j + 3] += e
    for src, dst in ((e1, m1), (m1, e1)):

        def post(i):
            dst[i + 2] = (mix(src, i + 2) + C1 * b1[i + 2]) * mask1

        each(n1, post)


def prolonged(k, e1, ix, iy, first, n, half_ref, put):
    by = k.by
    for j in range(n):
        e = e1[ix * (k.bx // 2) + (first + j + 2), pl.ds(pl.multiple_of(iy * (by // 2), 8), k.rows // 2), :]
        half_ref[j, pl.ds(0, k.rows // 2, stride=2), :] = e
        half_ref[j, pl.ds(1, k.rows // 2, stride=2), :] = e
    spread = spread_matrix(k.l1, k.lanes)
    for j in range(n):
        put(j, dot(half_ref[j], spread))


def overlap_add(k, g_ref, b1, n, rows, y_skip, first_of):
    zero(b1)
    for i in range(k.gx):
        for j in range(k.gy):
            at_y = j * (k.by // 2) + y_skip
            for q in range(n):
                x = i * (k.bx // 2) + first_of(i) + q
                if 0 <= x < k.nx1:
                    part = g_ref[i * k.gy + j, q * rows:(q + 1) * rows, :]
                    b1[x + 2, at_y:at_y + rows, :] += part


def own_lanes(k, v):
    half = k.bz // 2
    first, second = v[:, :k.bz], v[:, k.bz:]
    lane = iota(first.shape, 1)
    return jnp.where(lane < half, pltpu.roll(first, half, 1), pltpu.roll(second, half, 1))


def middle_kernel(k, g_ref, win_ref, got_a, got_b, w_ref, low_ref, high_ref, pack_ref, xa_ref, xb_ref, own_ref,
                  b1, m1, e1, half1, b2, u2, v2, b, m, v, vel, flux, half_ref, c2):
    ix, iy, iz = place()
    bx, by = k.bx, k.by
    overlap_add(k, g_ref, b1, k.c1_n, k.c1_rows, 2, k.c1_first)
    coarse(k, iz, b1, m1, e1, half1, b2, u2, v2)
    pad = 5
    mask = fine_mask(k, iy, iz)
    even = lax.rem(iy, 2) == 0
    for x in range(bx):
        b[x + pad, :SIDE, :] = jnp.where(even, got_b[x], got_a[x])
        b[x + pad, SIDE:SIDE + by, :] = win_ref[x]
        b[x + pad, SIDE + by:, :] = jnp.where(even, got_a[x], got_b[x])
    base = k.c1_n * k.c1_rows
    span = k.edge * 2 * by
    y_low, y_high = jnp.maximum(iy - 1, 0), jnp.minimum(iy + 1, k.gy - 1)
    for side in range(2):
        if k.one:
            who, shift = 1 - ix, 0
        else:
            who = jnp.maximum(ix - 1, 0) if side == 0 else jnp.minimum(ix + 1, k.gx - 1)
            shift = span if side == 0 else 0
        for j in range(k.edge):
            at = pad - k.edge + j if side == 0 else pad + bx + j
            for t in range(2):
                row = base + shift + (2 * j + t) * by
                lanes = slice(t * k.bz, (t + 1) * k.bz)
                b[at, :SIDE, lanes] = g_ref[who * k.gy + y_low, row + by - 8:row + by, :]
                b[at, SIDE:SIDE + by, lanes] = g_ref[who * k.gy + iy, row:row + by, :]
                b[at, SIDE + by:, lanes] = g_ref[who * k.gy + y_high, row:row + 8, :]

    def clean(i):
        b[i] = b[i] * (mask * x_inside(k, ix, i - pad))

    each(bx + 2 * pad, clean)

    def put(j, e):
        for t in range(2):
            v[pad - 4 + 2 * j + t] = e

    prolonged(k, e1, ix, iy, -2, bx // 2 + 4, half_ref, put)

    def pre(i):
        at = i + pad - 4
        here = mask * x_inside(k, ix, i - 4)
        v[at] = (v[at] + C0 * (b[at] + mix(b, at))) * here

    each(bx + 8, pre)

    def post1(i):
        at = i + pad - 3
        m[at] = (mix(v, at) + C0 * b[at]) * (mask * x_inside(k, ix, i - 3))

    each(bx + 6, post1)

    def post2(i):
        at = i + pad - 2
        v[at] = (mix(m, at) + C0 * b[at]) * (mask * x_inside(k, ix, i - 2))

    each(bx + 4, post2)

    def speed(i):
        at = i + pad - 1
        here = 0.5 * (mask * x_inside(k, ix, i - 1))
        c = v[at]
        vel[0, i] = (v[at + 1] - v[at - 1]) * here
        vel[1, i] = (up(c, 0) - down(c, 0)) * here
        vel[2, i] = (up(c, 1) - down(c, 1)) * here

    each(bx + 2, speed)
    own_mask = mask[SIDE:SIDE + by, :]
    zero(flux)
    half, part = k.bz // 2, k.bz // 4
    for x in range(bx):
        low, high = low_ref[x], high_ref[x]
        w0 = 0.5 * wind_window(k, w_ref[0, x], low, half, high, 0)
        w1 = 0.5 * wind_window(k, w_ref[1, x], low, half + part, high, part)
        q, r = x // 4, x % 4
        w2 = 0.5 * wind_window(k, w_ref[2, x], low_ref[bx + q], part * r, high_ref[bx + q], part * r)
        for d in range(3):
            c = vel[d, x + 1, SIDE:SIDE + by, :]
            xp, xm = vel[d, x + 2, SIDE:SIDE + by, :], vel[d, x, SIDE:SIDE + by, :]
            yp, ym = vel[d, x + 1, SIDE + 1:SIDE + by + 1, :], vel[d, x + 1, SIDE - 1:SIDE + by - 1, :]
            zp, zm = up(c, 1), down(c, 1)
            near = (xp + xm) + (yp + ym) + (zp + zm)
            total = 7.0 * c - near + w0 * (xp - xm) + w1 * (yp - ym) + w2 * (zp - zm)
            flux[d, x + 2, SIDE:SIDE + by, :] = total * own_mask
    zero(b)
    zero(m)

    def spread_flux(i):
        at = i + pad - 1
        f1, f2 = flux[1, i + 1], flux[2, i + 1]
        total = (flux[0, i + 2] - flux[0, i]) + (up(f1, 0) - down(f1, 0)) + (up(f2, 1) - down(f2, 1))
        b[at] = total * (-0.5 * (mask * x_inside(k, ix, i - 1)))

    each(bx + 2, spread_flux)
    zero(v)

    def power1(i):
        at = i + pad - 2
        c = mix(b, at) * (mask * x_inside(k, ix, i - 2))
        m[at] = c
        b[at] = b[at] + c

    def power1_pure(i):
        at = i + pad - 2
        m[at] = mix(b, at) * (mask * x_inside(k, ix, i - 2))

    each(bx + 4, power1_pure)

    def power2(i):
        at = i + pad - 3
        v[at] = mix(m, at) * (mask * x_inside(k, ix, i - 3))

    each(bx + 6, power2)

    def power3(i):
        at = i + pad - 4
        b[at] = C0 * ((b[at] + m[at]) + (v[at] + mix(v, at))) * (mask * x_inside(k, ix, i - 4))

    each(bx + 8, power3)
    restrict_planes(v, pad - 4, bx // 2 + 4, half_ref, c2, 0.125)
    start = (k.c2_first(ix) + 2) if k.one else 0
    for j in range(k.c2_n):
        pack_ref[j * k.c2_rows:(j + 1) * k.c2_rows, :] = c2[start + j]
    row8 = iota((8, k.bz), 0)
    at = k.c2_n * k.c2_rows
    start = (k.yf_first(ix) if k.one else -3) + pad
    for j in range(k.yf_n):
        c = own_lanes(k, jnp.where(iota((8, k.lanes), 0) < 4, b[start + j, SIDE + by:, :], b[start + j, :SIDE, :]))
        pack_ref[at:at + 8, :] = c
        at += 8
    upper = lax.rem(ix, 2) == 0
    first_a = pad + jnp.where(upper, bx, -4)
    first_b = pad + jnp.where(upper, -4, bx)
    for j in range(4):
        xa_ref[j] = own_lanes(k, b[first_a + j, SIDE:SIDE + by, :])
        if xb_ref is not None:
            xb_ref[j] = own_lanes(k, b[first_b + j, SIDE:SIDE + by, :])
    for x in range(bx):
        own_ref[x] = own_lanes(k, b[x + pad, SIDE:SIDE + by, :])


def last_kernel(k, g_ref, own_ref, xa_ref, xb_ref, out_ref, b1, m1, e1, half1, b2, u2, v2, v, m, half_ref):
    ix, iy, iz = place()
    bx, by = k.bx, k.by
    overlap_add(k, g_ref, b1, k.c2_n, k.c2_rows, 0, k.c2_first)
    coarse(k, iz, b1, m1, e1, half1, b2, u2, v2)
    pad = 2
    mask = fine_mask(k, iy, iz)

    def put(j, e):
        for t in range(2):
            plane = -2 + 2 * j + t
            v[pad + plane] = e * (mask * x_inside(k, ix, plane))

    prolonged(k, e1, ix, iy, -1, bx // 2 + 2, half_ref, put)

    def post1(i):
        at = i + pad - 1
        m[at] = mix(v, at) * (mask * x_inside(k, ix, i - 1))

    each(bx + 2, post1)
    base = k.c2_n * k.c2_rows
    low_ok = jnp.where(iy > 0, 1.0, 0.0).astype(jnp.float32)
    high_ok = jnp.where(iy < k.gy - 1, 1.0, 0.0).astype(jnp.float32)
    y_low, y_high = jnp.maximum(iy - 1, 0), jnp.minimum(iy + 1, k.gy - 1)
    row8 = iota((8, k.bz), 0)
    low_keep = jnp.where(row8 < 4, low_ok, 0.0)
    high_keep = jnp.where(row8 >= 4, high_ok, 0.0)
    for x in range(bx):
        out_ref[x] = own_lanes(k, mix(m, x + pad)[SIDE:SIDE + by, :]) + own_ref[x]

    def frame(who, first, x_from, x_to, ok):
        for x in range(x_from, x_to):
            row = base + (x - first) * 8
            if not isinstance(row, int):
                row = pl.multiple_of(row, 8)
            lo = g_ref[who * k.gy + y_low, pl.ds(row, 8), :] * ok
            hi = g_ref[who * k.gy + y_high, pl.ds(row, 8), :] * ok
            out_ref[x, :8, :] += lo * low_keep
            out_ref[x, by - 8:, :] += hi * high_keep

    one = jnp.float32(1.0)
    frame(ix, k.yf_first(ix), 0, bx, one)
    upper = lax.rem(ix, 2) == 0
    if k.one:
        for j in range(3):
            x = jnp.where(ix == 0, bx - 3 + j, j)
            row = pl.multiple_of(base + jnp.where(ix == 0, j, bx + j) * 8, 8)
            lo = g_ref[(1 - ix) * k.gy + y_low, pl.ds(row, 8), :]
            hi = g_ref[(1 - ix) * k.gy + y_high, pl.ds(row, 8), :]
            out_ref[x, :8, :] += lo * low_keep
            out_ref[x, by - 8:, :] += hi * high_keep
    else:
        frame(jnp.maximum(ix - 1, 0), -3 - bx, 0, 3, jnp.where(ix > 0, 1.0, 0.0).astype(jnp.float32))
        frame(jnp.minimum(ix + 1, k.gx - 1), bx - 3, bx - 3, bx, jnp.where(ix < k.gx - 1, 1.0, 0.0).astype(jnp.float32))
    for j in range(4):
        out_ref[jnp.where(upper, bx - 4, 0) + j] += xa_ref[j]
        if xb_ref is not None:
            out_ref[jnp.where(upper, 0, bx - 4) + j] += xb_ref[j]


def call(kernel, outs, scratch, args, flops):
    f32 = lambda s: jax.ShapeDtypeStruct(s, jnp.float32)
    return pl.pallas_call(
        kernel,
        out_shape=[f32(s) for s in outs],
        scratch_shapes=[pltpu.VMEM(s, jnp.float32) for s in scratch],
        compiler_params=pltpu.CompilerParams(vmem_limit_bytes=40 * 1024 * 1024),
        cost_estimate=pl.CostEstimate(flops=flops, bytes_accessed=1 << 20, transcendentals=0),
    )(*args)


def pairs(n):
    first = [(i, i ^ 1) for i in range(n) if (i ^ 1) < n]
    second = [(i + s, i + 1 - s) for i in range(1, n - 1, 2) for s in (0, 1)]
    return first, second


def chain(n, step):
    return [(i, i + step) for i in range(n) if 0 <= i + step < n]


def coarse_scratch(k):
    n1, n2, rows2 = k.nx1, k.nx1 // 2, k.rows1p // 2
    big = (n1 + 4, k.rows1, k.l1)
    return [big, big, big, (n2, k.rows1p, k.l1), (n2, rows2, k.l1), (n2 + 2, rows2, k.l1), (n2 + 2, rows2, k.l1)]


def body(k, pressure, wind):
    bx, by, bz = k.bx, k.by, k.bz
    slab = (bx + -(-bx // 4), by, bz)
    right, left = call(functools.partial(slab_kernel, k), [slab, slab], [], (pressure, wind), 1 << 20)
    low = lax.ppermute(right, "gz", chain(k.gz, 1))
    high = lax.ppermute(left, "gz", chain(k.gz, -1))
    fine = lambda n: (n, k.rows, k.lanes)
    window, send_a, send_b, pack = call(
        functools.partial(first_kernel, k),
        [(bx, by, k.lanes), (bx, 8, k.lanes), (bx, 8, k.lanes), (k.pack1, bz)],
        [fine(bx + 6), fine(bx + 6), (bx // 2 + 2, k.rows, k.l1), (bx // 2 + 2, k.rows // 2, k.l1)],
        (pressure, low, high), 1 << 22)
    ya, yb = pairs(k.gy)
    got_a = lax.ppermute(send_a, "gy", ya)
    got_b = lax.ppermute(send_b, "gy", yb)
    gathered = lax.all_gather(pack, PLANE)
    xa, xb = pairs(k.gx)
    x_outs = [(4, by, bz)] * (2 if xb else 1)
    n_in = 7

    def middle(*refs):
        ins, rest = refs[:n_in], refs[n_in:]
        pack_ref, rest = rest[0], rest[1:]
        xa_ref, rest = rest[0], rest[1:]
        xb_ref = None
        if xb:
            xb_ref, rest = rest[0], rest[1:]
        middle_kernel(k, *ins, pack_ref, xa_ref, xb_ref, *rest)

    big = fine(bx + 10)
    outs = call(
        middle, [(k.pack2, bz)] + x_outs + [(bx, by, bz)],
        coarse_scratch(k) + [big, big, big, (3,) + fine(bx + 2), (3,) + fine(bx + 4),
                             (bx // 2 + 4, k.rows, k.l1), (bx // 2 + 4, k.rows // 2, k.l1)],
        (gathered, window, got_a, got_b, wind, low, high), 1 << 24)
    pack, frames, own = outs[0], outs[1:-1], outs[-1]
    got = [lax.ppermute(f, "gx", perm) for f, perm in zip(frames, (xa, xb))]
    gathered = lax.all_gather(pack, PLANE)

    def last(*refs):
        g_ref, own_ref, xa_ref, rest = refs[0], refs[1], refs[2], refs[3:]
        xb_ref = None
        if xb:
            xb_ref, rest = rest[0], rest[1:]
        last_kernel(k, g_ref, own_ref, xa_ref, xb_ref, *rest)

    (result,) = call(
        last, [(bx, by, bz)],
        coarse_scratch(k) + [fine(bx + 4), fine(bx + 4), (bx // 2 + 2, k.rows, k.l1)],
        (gathered, own, *got), 1 << 23)
    return result


def solution(mesh):
    gx, gy, gz = (mesh.shape[a] for a in ("gx", "gy", "gz"))

    def run(pressure, wind):
        return body(Sizes(gx, gy, gz, *pressure.shape), pressure, wind)

    in_specs = (P("gx", "gy", "gz"), P(None, "gx", "gy", "gz"))
    return jax.shard_map(run, mesh=mesh, in_specs=in_specs, out_specs=P("gx", "gy", "gz"), check_vma=False)
```

time: 561 us -> 60.9 us (0.11); the launches traced: 551 us -> 60.6 us
  starting transfers between devices: 366 us -> 7.09 us
  waiting for transfers between devices: 130 us -> 5.48 us
  local copies, waits for them, and re-layouts: 38.6 us -> 1.86 us
  blocking collectives: 0 us -> 25.8 us
  Pallas kernels: 0 us -> 20.3 us
  other arithmetic: 15.4 us -> 0 us
    ppermute x126 -> x5, starting transfers between devices: 366 us -> 7.09 us  [the longest x1 4.96 us: body(): low = lax.ppermute(right, 'gz', chain(k.gz, 1))]
    ppermute x126 -> x5, waiting for transfers between devices: 130 us -> 5.48 us  [the longest x1 4.22 us: body(): high = lax.ppermute(left, 'gz', chain(k.gz, -1))]
    reshape x8 -> x0, local copies, waits for them, and re-layouts: 29 us -> none  [the longest x4 17 us: restrict(): values.reshape(extent_x // 2, 2, extent_y // 2, 2, extent_z // 2, 2)]
    all_gather x0 -> x2, blocking collectives: none -> 25.8 us  [body(): gathered = lax.all_gather(pack, PLANE)]
    pallas_call x0 -> x4, Pallas kernels: none -> 20.3 us  [call(): pl.pallas_call(kernel, out_shape=[f32(s) for s in outs], scratch_shapes=[...]
    broadcast_in_dim x4 -> x0, local copies, waits for them, and re-layouts: 7.38 us -> none  [prolong(): jnp.broadcast_to(values[:, None, :, None, :, None], (extent_x, 2, extent_...]
    reduce_sum x4 -> x0, other arithmetic: 6.84 us -> none  [restrict(): return 0.125 * jnp.sum(blocks, axis=(1, 3, 5))]
  transfers between devices with their start and end apart: 126 -> 5, of which waited for: 84 -> 2; matrix products, arithmetic and copies ran while one was open for 0% -> 0% of each run, Pallas kernels for 0% -> 0%
where the time goes in v1:
time: 60.9 us; the launch traced here: 60.6 us
  blocking collectives  25.8 us (42%)
  Pallas kernels  20.3 us (33%)
  starting transfers between devices  7.09 us (12%)
  waiting for transfers between devices  5.48 us (9%)
  local copies, waits for them, and re-layouts  1.86 us (3%)
    all_gather x2, blocking collectives, body(): gathered = lax.all_gather(pack, PLANE)  25.8 us
    pallas_call x4, Pallas kernels, call(): pl.pallas_call(kernel, out_shape=[f32(s) for s in outs], scratch_shapes=[...  20.3 us
    ppermute x1, starting transfers between devices, body(): low = lax.ppermute(right, 'gz', chain(k.gz, 1))  4.96 us
    ppermute x1, waiting for transfers between devices, body(): high = lax.ppermute(left, 'gz', chain(k.gz, -1))  4.22 us
    unnamed x6, local copies, waits for them, and re-layouts  1.86 us
    ppermute x1, starting transfers between devices, body(): high = lax.ppermute(left, 'gz', chain(k.gz, -1))  1.29 us
    ppermute x1, waiting for transfers between devices, body(): low = lax.ppermute(right, 'gz', chain(k.gz, 1))  1.26 us
  transfers between devices with their start and end apart: 5, of which 2 were waited for; matrix products, arithmetic and copies ran while one was open for 0% of the time, Pallas kernels for 0%

profile of v1, /device:TPU:0, one launch (start us, length us, event | category | flops | bytes accessed | tf_op | source)
XLA Modules:
  0.0 60.6 jit_solution(14326149969310840125)
XLA Ops:
  0.0 0.0 copy-start
  0.0 1.0 %copy-done = f32[3,12,16,128]{3,2,1,0:T(8,128)S(1)} copy-done((f32[3,12,16,128]{3,2,1,0:T(8,128)S(1)}, f32[3,12,16,128]{3,2,1,0:T(8,128)}, u32[]{:S(2)}) %copy-start) | copy-done | bytes 294936
  1.0 0.0 copy-start.2
  1.0 0.9 %copy-done.2 = f32[12,16,128]{2,1,0:T(8,128)S(1)} copy-done((f32[12,16,128]{2,1,0:T(8,128)S(1)}, f32[12,16,128]{2,1,0:T(8,128)}, u32[]{:S(2)}) %copy-start.2) | copy-done | bytes 98328
  1.9 0.2 shard_map.28
  2.0 5.0 %collective-permute-start = (f32[15,16,128]{2,1,0:T(8,128)S(1)}, f32[15,16,128]{2,1,0:T(8,128)S(1)}, u32[]{:S(2)}, u32[]{:S(2)}) collective-permute-start(f32[15,16,128]{2,1,0:T(8,128)S(1)} %get-tuple-element.14), channel_id=1, source_target_pairs={{0,1},{1,2},{2,3},{4,5},{5,6},{6,7},{8,9},{9,10},{10,11},{12,13},{... | collective-permute-start | bytes 368648 | tf_op jit(solution)/shard_map/ppermute | solution.py:519
  7.0 1.3 %collective-permute-start.1 = (f32[15,16,128]{2,1,0:T(8,128)S(1)}, f32[15,16,128]{2,1,0:T(8,128)S(1)}, u32[]{:S(2)}, u32[]{:S(2)}) collective-permute-start(f32[15,16,128]{2,1,0:T(8,128)S(1)} %get-tuple-element.15), channel_id=1, source_target_pairs={{1,0},{2,1},{3,2},{5,4},{6,5},{7,6},{9,8},{10,9},{11,10},{13,12},{... | collective-permute-start | bytes 368648 | tf_op jit(solution)/shard_map/ppermute | solution.py:520
  8.3 1.3 %collective-permute-done.low_ref.refs_5_ = f32[15,16,128]{2,1,0:T(8,128)S(1)} collective-permute-done((f32[15,16,128]{2,1,0:T(8,128)S(1)}, f32[15,16,128]{2,1,0:T(8,128)S(1)}, u32[]{:S(2)}, u32[]{:S(2)}) %collective-permute-start) | collective-permute-done | bytes 122912 | tf_op jit(solution)/shard_map/ppermute | solution.py:519
  9.6 4.2 %collective-permute-done.1.high_ref.refs_6_ = f32[15,16,128]{2,1,0:T(8,128)S(1)} collective-permute-done((f32[15,16,128]{2,1,0:T(8,128)S(1)}, f32[15,16,128]{2,1,0:T(8,128)S(1)}, u32[]{:S(2)}, u32[]{:S(2)}) %collective-permute-start.1) | collective-permute-done | bytes 122912 | tf_op jit(solution)/shard_map/ppermute | solution.py:520
  13.8 2.3 %shard_map.29 = (f32[12,16,256]{2,1,0:T(8,128)S(1)}, f32[12,8,256]{2,1,0:T(8,128)S(1)}, f32[12,8,256]{2,1,0:T(8,128)S(1)}, f32[244,128]{1,0:T(8,128)S(1)}) custom-call(f32[12,16,128]{2,1,0:T(8,128)S(1)} %copy-done.2, f32[15,16,128]{2,1,0:T(8,128)S(1)} %collective-permute-done.low_ref.refs_5_, f32[15,16,128]{2,1,0:T(8,128)S(1)} %collective-permute-done.1.high_ref.refs_6_), custom_call_target="tpu_custom_call" | custom-call | flops 4194304 | bytes 1048576 | tf_op jit(solution)/shard_map/pallas_call | solution.py:490
  16.1 0.1 collective-permute-start.2
  16.2 0.7 %collective-permute-start.3 = (f32[12,8,256]{2,1,0:T(8,128)S(1)}, f32[12,8,256]{2,1,0:T(8,128)S(1)}, u32[]{:S(2)}, u32[]{:S(2)}) collective-permute-start(f32[12,8,256]{2,1,0:T(8,128)S(1)} %get-tuple-element.19), channel_id=1, source_target_pairs={{4,8},{8,4},{5,9},{9,5},{6,10},{10,6},{7,11},{11,7},{20,24},{24,20... | collective-permute-start | bytes 294920 | tf_op jit(solution)/shard_map/ppermute | solution.py:529
  16.8 0.0 copy-start.1
  16.8 14.4 %all-gather.2.refs_0_ = f32[8,244,128]{2,1,0:T(8,128)S(1)} all-gather(f32[1,244,128]{2,1,0:T(8,128)S(1)} %bitcast.3), channel_id=2, replica_groups=mesh['gx'=2,'gy'=4,'gz'=4] {'gx','gy'}, dimensions={0}, use_global_device_ids=true | all-gather | bytes 1124352 | tf_op jit(solution)/shard_map/all_gather | solution.py:530
  31.2 0.0 collective-permute-done.2.refs_2_
  31.3 0.0 collective-permute-done.3.refs_3_
  31.3 0.0 copy-done.1
  31.3 12.7 %shard_map.30 = (f32[248,128]{1,0:T(8,128)S(1)}, f32[4,16,128]{2,1,0:T(8,128)S(1)}, f32[12,16,128]{2,1,0:T(8,128)S(1)}) custom-call(f32[8,244,128]{2,1,0:T(8,128)S(1)} %all-gather.2.refs_0_, f32[12,16,256]{2,1,0:T(8,128)S(1)} %get-tuple-element.17.refs_1_, f32[12,8,256]{2,1,0:T(8,128)S(1)} %collective-permute-done.2.refs_2_, ...), custom_call_target="tpu_custom_call" | custom-call | flops 16777216 | bytes 1048576 | tf_op jit(solution)/shard_map/pallas_call | solution.py:490
  44.0 0.1 collective-permute-start.4
  44.1 11.4 %all-gather.1 = f32[1984,128]{1,0:T(8,128)S(1)} all-gather(f32[248,128]{1,0:T(8,128)S(1)} %get-tuple-element.20), channel_id=3, replica_groups=mesh['gx'=2,'gy'=4,'gz'=4] {'gx','gy'}, dimensions={0}, use_global_device_ids=true | all-gather | bytes 1142784 | tf_op jit(solution)/shard_map/all_gather | solution.py:552
  55.5 0.0 collective-permute-done.4.refs_2_
  55.5 5.1 %shard_map.31 = f32[12,16,128]{2,1,0:T(8,128)} custom-call(f32[8,248,128]{2,1,0:T(8,128)S(1)} %bitcast.2, f32[12,16,128]{2,1,0:T(8,128)S(1)} %get-tuple-element.21.refs_1_, f32[4,16,128]{2,1,0:T(8,128)S(1)} %collective-permute-done.4.refs_2_), custom_call_target="tpu_custom_call" | custom-call | flops 8388608 | bytes 1048576 | tf_op jit(solution)/shard_map/pallas_call | solution.py:490
Async XLA Ops:
  0.0 1.0 %copy-start = (f32[3,12,16,128]{3,2,1,0:T(8,128)S(1)}, f32[3,12,16,128]{3,2,1,0:T(8,128)}, u32[]{:S(2)}) copy-start(f32[3,12,16,128]{3,2,1,0:T(8,128)} %refs_4_.1) | copy-start | bytes 884740
  1.0 0.9 %copy-start.2 = (f32[12,16,128]{2,1,0:T(8,128)S(1)}, f32[12,16,128]{2,1,0:T(8,128)}, u32[]{:S(2)}) copy-start(f32[12,16,128]{2,1,0:T(8,128)} %p_ref.3) | copy-start | bytes 294916
  2.0 7.5 %collective-permute-start = (f32[15,16,128]{2,1,0:T(8,128)S(1)}, f32[15,16,128]{2,1,0:T(8,128)S(1)}, u32[]{:S(2)}, u32[]{:S(2)}) collective-permute-start(f32[15,16,128]{2,1,0:T(8,128)S(1)} %get-tuple-element.14), channel_id=1, source_target_pairs={{0,1},{1,2},{2,3},{4,5},{5,6},{6,7},{8,9},{9,10},{10,11},{12,13},{... | collective-permute-start | bytes 368648 | tf_op jit(solution)/shard_map/ppermute | solution.py:519
  7.0 6.8 %collective-permute-start.1 = (f32[15,16,128]{2,1,0:T(8,128)S(1)}, f32[15,16,128]{2,1,0:T(8,128)S(1)}, u32[]{:S(2)}, u32[]{:S(2)}) collective-permute-start(f32[15,16,128]{2,1,0:T(8,128)S(1)} %get-tuple-element.15), channel_id=1, source_target_pairs={{1,0},{2,1},{3,2},{5,4},{6,5},{7,6},{9,8},{10,9},{11,10},{13,12},{... | collective-permute-start | bytes 368648 | tf_op jit(solution)/shard_map/ppermute | solution.py:520
  16.1 15.2 %collective-permute-start.2 = (f32[12,8,256]{2,1,0:T(8,128)S(1)}, f32[12,8,256]{2,1,0:T(8,128)S(1)}, u32[]{:S(2)}, u32[]{:S(2)}) collective-permute-start(f32[12,8,256]{2,1,0:T(8,128)S(1)} %get-tuple-element.18), channel_id=1, source_target_pairs={{0,4},{4,0},{8,12},{12,8},{1,5},{5,1},{9,13},{13,9},{2,6},{6,2},{1... | collective-permute-start | bytes 294920 | tf_op jit(solution)/shard_map/ppermute | solution.py:528
  16.2 15.1 %collective-permute-start.3 = (f32[12,8,256]{2,1,0:T(8,128)S(1)}, f32[12,8,256]{2,1,0:T(8,128)S(1)}, u32[]{:S(2)}, u32[]{:S(2)}) collective-permute-start(f32[12,8,256]{2,1,0:T(8,128)S(1)} %get-tuple-element.19), channel_id=1, source_target_pairs={{4,8},{8,4},{5,9},{9,5},{6,10},{10,6},{7,11},{11,7},{20,24},{24,20... | collective-permute-start | bytes 294920 | tf_op jit(solution)/shard_map/ppermute | solution.py:529
  16.8 14.4 %copy-start.1 = (f32[3,12,16,128]{3,2,1,0:T(8,128)S(1)}, f32[3,12,16,128]{3,2,1,0:T(8,128)}, u32[]{:S(2)}) copy-start(f32[3,12,16,128]{3,2,1,0:T(8,128)} %refs_4_.1) | copy-start | bytes 884740
  44.0 11.5 %collective-permute-start.4 = (f32[4,16,128]{2,1,0:T(8,128)S(1)}, f32[4,16,128]{2,1,0:T(8,128)S(1)}, u32[]{:S(2)}, u32[]{:S(2)}) collective-permute-start(f32[4,16,128]{2,1,0:T(8,128)S(1)} %get-tuple-element.22), channel_id=1, source_target_pairs={{0,16},{16,0},{1,17},{17,1},{2,18},{18,2},{3,19},{19,3},{4,20},{20... | collective-permute-start | bytes 98312 | tf_op jit(solution)/shard_map/ppermute | solution.py:551

commit v2 on v1

--- a/solution.py
+++ b/solution.py
@@ -29,7 +29,7 @@
 
 
 def each(n, step):
-    lax.fori_loop(0, n, lambda i, _: step(i), None, unroll=2 if n % 2 == 0 else 1)
+    lax.fori_loop(0, n, lambda i, _: step(i), None, unroll=True)
 
 
 def iota(shape, axis):

time: 60.9 us -> 50.2 us (0.82)
  Pallas kernels: 20.3 us -> 9.6 us
    pallas_call x4, Pallas kernels: 20.3 us -> 9.6 us  [call(): pl.pallas_call(kernel, out_shape=[f32(s) for s in outs], scratch_shapes=[...]
where the time goes in v2:
time: 50.2 us; the launch traced here: 49.9 us
  blocking collectives  25.9 us (52%)
  Pallas kernels  9.6 us (19%)
  starting transfers between devices  7.07 us (14%)
  waiting for transfers between devices  5.48 us (11%)
  local copies, waits for them, and re-layouts  1.86 us (4%)
    all_gather x2, blocking collectives, body(): gathered = lax.all_gather(pack, PLANE)  25.9 us
    pallas_call x4, Pallas kernels, call(): pl.pallas_call(kernel, out_shape=[f32(s) for s in outs], scratch_shapes=[...  9.6 us
    ppermute x1, starting transfers between devices, body(): low = lax.ppermute(right, 'gz', chain(k.gz, 1))  4.96 us
    ppermute x1, waiting for transfers between devices, body(): high = lax.ppermute(left, 'gz', chain(k.gz, -1))  4.22 us
    unnamed x6, local copies, waits for them, and re-layouts  1.86 us
    ppermute x1, starting transfers between devices, body(): high = lax.ppermute(left, 'gz', chain(k.gz, -1))  1.29 us
    ppermute x1, waiting for transfers between devices, body(): low = lax.ppermute(right, 'gz', chain(k.gz, 1))  1.26 us
  transfers between devices with their start and end apart: 5, of which 2 were waited for; matrix products, arithmetic and copies ran while one was open for 0% of the time, Pallas kernels for 0%

profile of v2, /device:TPU:0, one launch (start us, length us, event | category | flops | bytes accessed | tf_op | source)
XLA Modules:
  0.0 49.9 jit_solution(11534771770800539761)
XLA Ops:
  0.0 0.0 copy-start
  0.0 1.0 %copy-done = f32[3,12,16,128]{3,2,1,0:T(8,128)S(1)} copy-done((f32[3,12,16,128]{3,2,1,0:T(8,128)S(1)}, f32[3,12,16,128]{3,2,1,0:T(8,128)}, u32[]{:S(2)}) %copy-start) | copy-done | bytes 294936
  1.0 0.0 copy-start.2
  1.0 0.9 %copy-done.2 = f32[12,16,128]{2,1,0:T(8,128)S(1)} copy-done((f32[12,16,128]{2,1,0:T(8,128)S(1)}, f32[12,16,128]{2,1,0:T(8,128)}, u32[]{:S(2)}) %copy-start.2) | copy-done | bytes 98328
  1.9 0.2 shard_map.28
  2.0 5.0 %collective-permute-start = (f32[15,16,128]{2,1,0:T(8,128)S(1)}, f32[15,16,128]{2,1,0:T(8,128)S(1)}, u32[]{:S(2)}, u32[]{:S(2)}) collective-permute-start(f32[15,16,128]{2,1,0:T(8,128)S(1)} %get-tuple-element.14), channel_id=1, source_target_pairs={{0,1},{1,2},{2,3},{4,5},{5,6},{6,7},{8,9},{9,10},{10,11},{12,13},{... | collective-permute-start | bytes 368648 | tf_op jit(solution)/shard_map/ppermute | solution.py:519
  7.0 1.3 %collective-permute-start.1 = (f32[15,16,128]{2,1,0:T(8,128)S(1)}, f32[15,16,128]{2,1,0:T(8,128)S(1)}, u32[]{:S(2)}, u32[]{:S(2)}) collective-permute-start(f32[15,16,128]{2,1,0:T(8,128)S(1)} %get-tuple-element.15), channel_id=1, source_target_pairs={{1,0},{2,1},{3,2},{5,4},{6,5},{7,6},{9,8},{10,9},{11,10},{13,12},{... | collective-permute-start | bytes 368648 | tf_op jit(solution)/shard_map/ppermute | solution.py:520
  8.3 1.3 %collective-permute-done.low_ref.refs_5_ = f32[15,16,128]{2,1,0:T(8,128)S(1)} collective-permute-done((f32[15,16,128]{2,1,0:T(8,128)S(1)}, f32[15,16,128]{2,1,0:T(8,128)S(1)}, u32[]{:S(2)}, u32[]{:S(2)}) %collective-permute-start) | collective-permute-done | bytes 122912 | tf_op jit(solution)/shard_map/ppermute | solution.py:519
  9.6 4.2 %collective-permute-done.1.high_ref.refs_6_ = f32[15,16,128]{2,1,0:T(8,128)S(1)} collective-permute-done((f32[15,16,128]{2,1,0:T(8,128)S(1)}, f32[15,16,128]{2,1,0:T(8,128)S(1)}, u32[]{:S(2)}, u32[]{:S(2)}) %collective-permute-start.1) | collective-permute-done | bytes 122912 | tf_op jit(solution)/shard_map/ppermute | solution.py:520
  13.8 1.1 %shard_map.29 = (f32[12,16,256]{2,1,0:T(8,128)S(1)}, f32[12,8,256]{2,1,0:T(8,128)S(1)}, f32[12,8,256]{2,1,0:T(8,128)S(1)}, f32[244,128]{1,0:T(8,128)S(1)}) custom-call(f32[12,16,128]{2,1,0:T(8,128)S(1)} %copy-done.2, f32[15,16,128]{2,1,0:T(8,128)S(1)} %collective-permute-done.low_ref.refs_5_, f32[15,16,128]{2,1,0:T(8,128)S(1)} %collective-permute-done.1.high_ref.refs_6_), custom_call_target="tpu_custom_call" | custom-call | flops 4194304 | bytes 1048576 | tf_op jit(solution)/shard_map/pallas_call | solution.py:490
  14.9 0.1 collective-permute-start.2
  15.0 0.7 %collective-permute-start.3 = (f32[12,8,256]{2,1,0:T(8,128)S(1)}, f32[12,8,256]{2,1,0:T(8,128)S(1)}, u32[]{:S(2)}, u32[]{:S(2)}) collective-permute-start(f32[12,8,256]{2,1,0:T(8,128)S(1)} %get-tuple-element.19), channel_id=1, source_target_pairs={{4,8},{8,4},{5,9},{9,5},{6,10},{10,6},{7,11},{11,7},{20,24},{24,20... | collective-permute-start | bytes 294920 | tf_op jit(solution)/shard_map/ppermute | solution.py:529
  15.7 0.0 copy-start.1
  15.7 14.4 %all-gather.2.refs_0_ = f32[8,244,128]{2,1,0:T(8,128)S(1)} all-gather(f32[1,244,128]{2,1,0:T(8,128)S(1)} %bitcast.3), channel_id=2, replica_groups=mesh['gx'=2,'gy'=4,'gz'=4] {'gx','gy'}, dimensions={0}, use_global_device_ids=true | all-gather | bytes 1124352 | tf_op jit(solution)/shard_map/all_gather | solution.py:530
  30.1 0.0 collective-permute-done.2.refs_2_
  30.1 0.0 collective-permute-done.3.refs_3_
  30.1 0.0 copy-done.1
  30.1 5.2 %shard_map.30 = (f32[248,128]{1,0:T(8,128)S(1)}, f32[4,16,128]{2,1,0:T(8,128)S(1)}, f32[12,16,128]{2,1,0:T(8,128)S(1)}) custom-call(f32[8,244,128]{2,1,0:T(8,128)S(1)} %all-gather.2.refs_0_, f32[12,16,256]{2,1,0:T(8,128)S(1)} %get-tuple-element.17.refs_1_, f32[12,8,256]{2,1,0:T(8,128)S(1)} %collective-permute-done.2.refs_2_, ...), custom_call_target="tpu_custom_call" | custom-call | flops 16777216 | bytes 1048576 | tf_op jit(solution)/shard_map/pallas_call | solution.py:490
  35.3 0.1 collective-permute-start.4
  35.4 11.4 %all-gather.1 = f32[1984,128]{1,0:T(8,128)S(1)} all-gather(f32[248,128]{1,0:T(8,128)S(1)} %get-tuple-element.20), channel_id=3, replica_groups=mesh['gx'=2,'gy'=4,'gz'=4] {'gx','gy'}, dimensions={0}, use_global_device_ids=true | all-gather | bytes 1142784 | tf_op jit(solution)/shard_map/all_gather | solution.py:552
  46.9 0.0 collective-permute-done.4.refs_2_
  46.9 3.1 %shard_map.31 = f32[12,16,128]{2,1,0:T(8,128)} custom-call(f32[8,248,128]{2,1,0:T(8,128)S(1)} %bitcast.2, f32[12,16,128]{2,1,0:T(8,128)S(1)} %get-tuple-element.21.refs_1_, f32[4,16,128]{2,1,0:T(8,128)S(1)} %collective-permute-done.4.refs_2_), custom_call_target="tpu_custom_call" | custom-call | flops 8388608 | bytes 1048576 | tf_op jit(solution)/shard_map/pallas_call | solution.py:490
Async XLA Ops:
  0.0 1.0 %copy-start = (f32[3,12,16,128]{3,2,1,0:T(8,128)S(1)}, f32[3,12,16,128]{3,2,1,0:T(8,128)}, u32[]{:S(2)}) copy-start(f32[3,12,16,128]{3,2,1,0:T(8,128)} %refs_4_.1) | copy-start | bytes 884740
  1.0 0.9 %copy-start.2 = (f32[12,16,128]{2,1,0:T(8,128)S(1)}, f32[12,16,128]{2,1,0:T(8,128)}, u32[]{:S(2)}) copy-start(f32[12,16,128]{2,1,0:T(8,128)} %p_ref.3) | copy-start | bytes 294916
  2.0 7.5 %collective-permute-start = (f32[15,16,128]{2,1,0:T(8,128)S(1)}, f32[15,16,128]{2,1,0:T(8,128)S(1)}, u32[]{:S(2)}, u32[]{:S(2)}) collective-permute-start(f32[15,16,128]{2,1,0:T(8,128)S(1)} %get-tuple-element.14), channel_id=1, source_target_pairs={{0,1},{1,2},{2,3},{4,5},{5,6},{6,7},{8,9},{9,10},{10,11},{12,13},{... | collective-permute-start | bytes 368648 | tf_op jit(solution)/shard_map/ppermute | solution.py:519
  7.0 6.8 %collective-permute-start.1 = (f32[15,16,128]{2,1,0:T(8,128)S(1)}, f32[15,16,128]{2,1,0:T(8,128)S(1)}, u32[]{:S(2)}, u32[]{:S(2)}) collective-permute-start(f32[15,16,128]{2,1,0:T(8,128)S(1)} %get-tuple-element.15), channel_id=1, source_target_pairs={{1,0},{2,1},{3,2},{5,4},{6,5},{7,6},{9,8},{10,9},{11,10},{13,12},{... | collective-permute-start | bytes 368648 | tf_op jit(solution)/shard_map/ppermute | solution.py:520
  14.9 15.2 %collective-permute-start.2 = (f32[12,8,256]{2,1,0:T(8,128)S(1)}, f32[12,8,256]{2,1,0:T(8,128)S(1)}, u32[]{:S(2)}, u32[]{:S(2)}) collective-permute-start(f32[12,8,256]{2,1,0:T(8,128)S(1)} %get-tuple-element.18), channel_id=1, source_target_pairs={{0,4},{4,0},{8,12},{12,8},{1,5},{5,1},{9,13},{13,9},{2,6},{6,2},{1... | collective-permute-start | bytes 294920 | tf_op jit(solution)/shard_map/ppermute | solution.py:528
  15.0 15.1 %collective-permute-start.3 = (f32[12,8,256]{2,1,0:T(8,128)S(1)}, f32[12,8,256]{2,1,0:T(8,128)S(1)}, u32[]{:S(2)}, u32[]{:S(2)}) collective-permute-start(f32[12,8,256]{2,1,0:T(8,128)S(1)} %get-tuple-element.19), channel_id=1, source_target_pairs={{4,8},{8,4},{5,9},{9,5},{6,10},{10,6},{7,11},{11,7},{20,24},{24,20... | collective-permute-start | bytes 294920 | tf_op jit(solution)/shard_map/ppermute | solution.py:529
  15.7 14.4 %copy-start.1 = (f32[3,12,16,128]{3,2,1,0:T(8,128)S(1)}, f32[3,12,16,128]{3,2,1,0:T(8,128)}, u32[]{:S(2)}) copy-start(f32[3,12,16,128]{3,2,1,0:T(8,128)} %refs_4_.1) | copy-start | bytes 884740
  35.3 11.5 %collective-permute-start.4 = (f32[4,16,128]{2,1,0:T(8,128)S(1)}, f32[4,16,128]{2,1,0:T(8,128)S(1)}, u32[]{:S(2)}, u32[]{:S(2)}) collective-permute-start(f32[4,16,128]{2,1,0:T(8,128)S(1)} %get-tuple-element.22), channel_id=1, source_target_pairs={{0,16},{16,0},{1,17},{17,1},{2,18},{18,2},{3,19},{19,3},{4,20},{20... | collective-permute-start | bytes 98312 | tf_op jit(solution)/shard_map/ppermute | solution.py:551

commit v3 on v2

--- a/solution.py
+++ b/solution.py
@@ -281,14 +281,11 @@
     return jnp.where(lane < half, pltpu.roll(first, half, 1), pltpu.roll(second, half, 1))
 
 
-def middle_kernel(k, g_ref, win_ref, got_a, got_b, w_ref, low_ref, high_ref, pack_ref, xa_ref, xb_ref, own_ref,
-                  b1, m1, e1, half1, b2, u2, v2, b, m, v, vel, flux, half_ref, c2):
+def assemble_edges(k, refs, b1, b, pad):
+    g_ref, win_ref, got_a, got_b, w_ref, low_ref, high_ref = refs
     ix, iy, iz = place()
     bx, by = k.bx, k.by
     overlap_add(k, g_ref, b1, k.c1_n, k.c1_rows, 2, k.c1_first)
-    coarse(k, iz, b1, m1, e1, half1, b2, u2, v2)
-    pad = 5
-    mask = fine_mask(k, iy, iz)
     even = lax.rem(iy, 2) == 0
     for x in range(bx):
         b[x + pad, :SIDE, :] = jnp.where(even, got_b[x], got_a[x])
@@ -311,6 +308,147 @@
                 b[at, :SIDE, lanes] = g_ref[who * k.gy + y_low, row + by - 8:row + by, :]
                 b[at, SIDE:SIDE + by, lanes] = g_ref[who * k.gy + iy, row:row + by, :]
                 b[at, SIDE + by:, lanes] = g_ref[who * k.gy + y_high, row:row + 8, :]
+    half, part = k.bz // 2, k.bz // 4
+
+    def winds(x):
+        low, high = low_ref[x], high_ref[x]
+        q, r = x // 4, x % 4
+        return (wind_window(k, w_ref[0, x], low, half, high, 0),
+                wind_window(k, w_ref[1, x], low, half + part, high, part),
+                wind_window(k, w_ref[2, x], low_ref[bx + q], part * r, high_ref[bx + q], part * r))
+
+    return winds
+
+
+def slab_places(k):
+    groups = lambda n: -(-n // 4)
+    rows1 = k.ny1
+    fine_n = k.bx + k.edge if k.one else k.bx + 2 * k.edge
+    at_fine = groups(k.nx1) * rows1
+    at_wind = at_fine + groups(fine_n) * k.rows
+    return fine_n, at_fine, at_wind, at_wind + groups(3 * k.bx) * k.by
+
+
+def take_slab(k, ref, base, rows, i, to):
+    part = k.bz // 4
+    at = base + (i // 4) * rows
+    return lane_roll(ref[at:at + rows, :], to - part * (i % 4))
+
+
+def assemble_plane(k, refs, b1, b, pad):
+    c1_ref, win_ref, w_ref, low_ref, high_ref = refs
+    ix, iy, iz = place()
+    bx, by = k.bx, k.by
+    half, part = k.bz // 2, k.bz // 4
+    fine_n, at_fine, at_wind, _ = slab_places(k)
+    zero(b1)
+    top = SIDE // 2
+    lane = iota((k.ny1, k.l1), 1)
+    for x in range(k.nx1):
+        low = take_slab(k, low_ref, 0, k.ny1, x, 1)
+        high = take_slab(k, high_ref, 0, k.ny1, x, 3 * part - 1)
+        low = jnp.where((lane >= 1) & (lane <= part), low, 0.0)
+        high = jnp.where((lane >= 3 * part - 1) & (lane < 4 * part - 1), high, 0.0)
+        b1[x + 2, top:top + k.ny1, :] = c1_ref[x] + (low + high)
+    lane = iota((k.rows, k.bz), 1)
+    zero(b)
+    first = -k.edge * ix if k.one else -k.edge
+    for j in range(fine_n):
+        p = pltpu.roll(win_ref[j], half, 1)
+        low = take_slab(k, low_ref, at_fine, k.rows, j, part)
+        high = take_slab(k, high_ref, at_fine, k.rows, j, half)
+        at = first + j + pad
+        b[at, :, :k.bz] = jnp.where(lane >= half, p, jnp.where(lane >= part, low, 0.0))
+        b[at, :, k.bz:] = jnp.where(lane < half, p, jnp.where(lane < half + part, high, 0.0))
+    lane_w = iota((by, k.bz), 1)
+
+    def winds(x):
+        found = []
+        for d in range(3):
+            w = pltpu.roll(w_ref[d, x], half, 1)
+            low = take_slab(k, low_ref, at_wind, by, d * bx + x, part)
+            high = take_slab(k, high_ref, at_wind, by, d * bx + x, half)
+            found.append(jnp.concatenate(
+                [jnp.where(lane_w >= half, w, jnp.where(lane_w >= part, low, 0.0)),
+                 jnp.where(lane_w < half, w, jnp.where(lane_w < half + part, high, 0.0))], axis=1))
+        return found
+
+    return winds
+
+
+def plane_kernel(k, g_ref, w_ref, c1_ref, win_ref, right_ref, left_ref, p, m, q, half_ref):
+    ix, iy, iz = place()
+    bx, by, bz = k.bx, k.by, k.bz
+    nx, ny = k.gx * bx, k.gy * by
+    half, part = bz // 2, bz // 4
+    pad_x = k.edge
+    fine_n, at_fine, at_wind, _ = slab_places(k)
+    for i in range(pad_x):
+        p[i] = jnp.zeros(p.shape[1:], jnp.float32)
+        p[pad_x + nx + i] = jnp.zeros(p.shape[1:], jnp.float32)
+    for x in range(nx):
+        p[pad_x + x, :SIDE, :] = jnp.zeros((SIDE, bz), jnp.float32)
+        p[pad_x + x, SIDE + ny:, :] = jnp.zeros((SIDE, bz), jnp.float32)
+        for j in range(k.gy):
+            p[pad_x + x, SIDE + j * by:SIDE + (j + 1) * by, :] = g_ref[(x // bx) * k.gy + j, x % bx]
+    zero(m)
+    lane = iota((ny + SIDE, bz), 1)
+    not_last = jnp.where(lane < bz - 1, 1.0, 0.0).astype(jnp.float32)
+    not_first = jnp.where(lane > 0, 1.0, 0.0).astype(jnp.float32)
+    last_ok = jnp.where(iz < k.gz - 1, W * W, 0.0).astype(jnp.float32)
+    first_ok = jnp.where(iz > 0, W * W, 0.0).astype(jnp.float32)
+    ends = (1.0 - not_last) * last_ok + (1.0 - not_first) * first_ok
+    for x in range(nx):
+        c = p[pad_x + x, SIDE:, :]
+        four = (p[pad_x + x - 1, SIDE:, :] + p[pad_x + x + 1, SIDE:, :]) + (up(c, 0) + down(c, 0))
+        along = up(c, 1) * not_last + down(c, 1) * not_first
+        mixed = (1.0 - OMEGA) * c + W * (four + along)
+        m[x + 1, :ny, :] = mixed[:ny]
+        q[x] = ((1.0 - OMEGA + W) * W * c + W * mixed + (W * W) * four)[:ny]
+
+    def twice(x):
+        c = m[x + 1]
+        four = (m[x] + m[x + 2]) + (up(c, 0) + down(c, 0))
+        along = up(c, 1) * not_last + down(c, 1) * not_first
+        return ((1.0 - OMEGA) * c + W * (four + along) + ends * p[pad_x + x, SIDE:, :])[:ny]
+
+    row, column = iota((bz, k.l1), 0), iota((bz, k.l1), 1)
+    own = jnp.where((row >> 1) + part == column, 0.125, 0.0).astype(jnp.float32)
+    rim = ((row == 0) & (column == part - 1)) | ((row == bz - 1) & (column == 3 * part))
+    rim = jnp.where(rim, 0.125, 0.0).astype(jnp.float32)
+    for j in range(k.nx1):
+        s = twice(2 * j) + twice(2 * j + 1)
+        t = q[2 * j] + q[2 * j + 1]
+        half_ref[j] = dot(s + up(s, 0), own) + dot(t + up(t, 0), rim)
+    for j in range(k.nx1):
+        c1_ref[j] = half_ref[j, pl.ds(0, k.ny1, stride=2), :]
+
+    def pack(ref, base, rows, n, load, from_lane):
+        lane = iota((rows, bz), 1)
+        for group in range(-(-n // 4)):
+            total = jnp.zeros((rows, bz), jnp.float32)
+            for r in range(min(4, n - 4 * group)):
+                moved = lane_roll(load(4 * group + r), part * r - from_lane)
+                total = jnp.where((lane >= part * r) & (lane < part * (r + 1)), moved, total)
+            ref[base + group * rows:base + (group + 1) * rows, :] = total
+
+    first = ix * (bx - k.edge) + pad_x if k.one else ix * bx + pad_x - k.edge
+    for j in range(fine_n):
+        win_ref[j] = p[first + j, pl.ds(pl.multiple_of(iy * by, 8), k.rows), :]
+    for ref, lane1, lane0 in ((right_ref, 2 * part + 1, 3 * part), (left_ref, part - 1, 0)):
+        pack(ref, 0, k.ny1, k.nx1, lambda i: c1_ref[i], lane1)
+        pack(ref, at_fine, k.rows, fine_n, lambda i: win_ref[i], lane0)
+        pack(ref, at_wind, by, 3 * bx, lambda i: w_ref[i // bx, i % bx], lane0)
+
+
+def middle_kernel(k, assemble, ins, pack_ref, xa_ref, xb_ref, own_ref,
+                  b1, m1, e1, half1, b2, u2, v2, b, m, v, vel, flux, half_ref, c2):
+    ix, iy, iz = place()
+    bx, by = k.bx, k.by
+    pad = 5
+    winds = assemble(k, ins, b1, b, pad)
+    coarse(k, iz, b1, m1, e1, half1, b2, u2, v2)
+    mask = fine_mask(k, iy, iz)
 
     def clean(i):
         b[i] = b[i] * (mask * x_inside(k, ix, i - pad))
@@ -353,13 +491,8 @@
     each(bx + 2, speed)
     own_mask = mask[SIDE:SIDE + by, :]
     zero(flux)
-    half, part = k.bz // 2, k.bz // 4
     for x in range(bx):
-        low, high = low_ref[x], high_ref[x]
-        w0 = 0.5 * wind_window(k, w_ref[0, x], low, half, high, 0)
-        w1 = 0.5 * wind_window(k, w_ref[1, x], low, half + part, high, part)
-        q, r = x // 4, x % 4
-        w2 = 0.5 * wind_window(k, w_ref[2, x], low_ref[bx + q], part * r, high_ref[bx + q], part * r)
+        w0, w1, w2 = (0.5 * w for w in winds(x))
         for d in range(3):
             c = vel[d, x + 1, SIDE:SIDE + by, :]
             xp, xm = vel[d, x + 2, SIDE:SIDE + by, :], vel[d, x, SIDE:SIDE + by, :]
@@ -379,12 +512,6 @@
 
     each(bx + 2, spread_flux)
     zero(v)
-
-    def power1(i):
-        at = i + pad - 2
-        c = mix(b, at) * (mask * x_inside(k, ix, i - 2))
-        m[at] = c
-        b[at] = b[at] + c
 
     def power1_pure(i):
         at = i + pad - 2
@@ -512,7 +639,7 @@
     return [big, big, big, (n2, k.rows1p, k.l1), (n2, rows2, k.l1), (n2 + 2, rows2, k.l1), (n2 + 2, rows2, k.l1)]
 
 
-def body(k, pressure, wind):
+def edge_form(k, pressure, wind):
     bx, by, bz = k.bx, k.by, k.bz
     slab = (bx + -(-bx // 4), by, bz)
     right, left = call(functools.partial(slab_kernel, k), [slab, slab], [], (pressure, wind), 1 << 20)
@@ -528,25 +655,47 @@
     got_a = lax.ppermute(send_a, "gy", ya)
     got_b = lax.ppermute(send_b, "gy", yb)
     gathered = lax.all_gather(pack, PLANE)
+    return assemble_edges, (gathered, window, got_a, got_b, wind, low, high)
+
+
+def plane_form(k, pressure, wind):
+    bx, by, bz = k.bx, k.by, k.bz
+    nx, ny = k.gx * bx, k.gy * by
+    gathered = lax.all_gather(pressure, PLANE)
+    fine_n, _, _, slab_rows = slab_places(k)
+    c1, window, right, left = call(
+        functools.partial(plane_kernel, k),
+        [(k.nx1, k.ny1, k.l1), (fine_n, k.rows, bz), (slab_rows, bz), (slab_rows, bz)],
+        [(nx + 2 * k.edge, ny + 2 * SIDE, bz), (nx + 2, ny + SIDE, bz), (nx, ny, bz), (k.nx1, ny, k.l1)],
+        (gathered, wind), 1 << 22)
+    low = lax.ppermute(right, "gz", chain(k.gz, 1))
+    high = lax.ppermute(left, "gz", chain(k.gz, -1))
+    return assemble_plane, (c1, window, wind, low, high)
+
+
+def body(k, pressure, wind):
+    bx, by, bz = k.bx, k.by, k.bz
+    fine = lambda n: (n, k.rows, k.lanes)
+    small_plane = k.gx * k.gy * bx * by * bz * 4 <= 1 << 20
+    assemble, args = (plane_form if small_plane else edge_form)(k, pressure, wind)
     xa, xb = pairs(k.gx)
     x_outs = [(4, by, bz)] * (2 if xb else 1)
-    n_in = 7
 
     def middle(*refs):
-        ins, rest = refs[:n_in], refs[n_in:]
+        ins, rest = refs[:len(args)], refs[len(args):]
         pack_ref, rest = rest[0], rest[1:]
         xa_ref, rest = rest[0], rest[1:]
         xb_ref = None
         if xb:
             xb_ref, rest = rest[0], rest[1:]
-        middle_kernel(k, *ins, pack_ref, xa_ref, xb_ref, *rest)
+        middle_kernel(k, assemble, ins, pack_ref, xa_ref, xb_ref, *rest)
 
     big = fine(bx + 10)
     outs = call(
         middle, [(k.pack2, bz)] + x_outs + [(bx, by, bz)],
         coarse_scratch(k) + [big, big, big, (3,) + fine(bx + 2), (3,) + fine(bx + 4),
                              (bx // 2 + 4, k.rows, k.l1), (bx // 2 + 4, k.rows // 2, k.l1)],
-        (gathered, window, got_a, got_b, wind, low, high), 1 << 24)
+        args, 1 << 24)
     pack, frames, own = outs[0], outs[1:-1], outs[-1]
     got = [lax.ppermute(f, "gx", perm) for f, perm in zip(frames, (xa, xb))]
     gathered = lax.all_gather(pack, PLANE)

time: 50.2 us -> 47.2 us (0.940)
  blocking collectives: 25.9 us -> 22.6 us
  waiting for transfers between devices: 5.48 us -> 7.66 us
  local copies, waits for them, and re-layouts: 1.86 us -> 0.01 us
  Pallas kernels: 9.6 us -> 10.7 us
  starting transfers between devices: 7.07 us -> 5.99 us
    all_gather x2 -> x1, blocking collectives: 25.9 us -> 10.3 us  [body(): gathered = lax.all_gather(pack, PLANE)]
    all_gather x0 -> x1, blocking collectives: none -> 12.3 us  [plane_form(): gathered = lax.all_gather(pressure, PLANE)]
    ppermute x4 -> x2, starting transfers between devices: 6.99 us -> 4.78 us  [the longest x1 3.49 us: plane_form(): low = lax.ppermute(right, 'gz', chain(k.gz, 1))]
    ppermute x4 -> x2, waiting for transfers between devices: 5.48 us -> 7.66 us  [the longest x1 4.12 us: plane_form(): high = lax.ppermute(left, 'gz', chain(k.gz, -1))]
    unnamed x6 -> x2, local copies, waits for them, and re-layouts: 1.86 us -> 0.01 us
    ppermute x1, starting transfers between devices: 0.08 us -> 1.21 us  [body(): got = [lax.ppermute(f, 'gx', perm) for f, perm in zip(frames, (xa, xb))]]
    pallas_call x4 -> x3, Pallas kernels: 9.6 us -> 10.7 us  [call(): pl.pallas_call(kernel, out_shape=[f32(s) for s in outs], scratch_shapes=[...]
  transfers between devices with their start and end apart: 5 -> 3, of which waited for: 2 -> 2; matrix products, arithmetic and copies ran while one was open for 0% -> 0% of each run, Pallas kernels for 0% -> 0%
where the time goes in v3:
time: 47.2 us; the launch traced here: 47 us
  blocking collectives  22.6 us (48%)
  Pallas kernels  10.7 us (23%)
  waiting for transfers between devices  7.66 us (16%)
  starting transfers between devices  5.99 us (13%)
    all_gather x1, blocking collectives, plane_form(): gathered = lax.all_gather(pressure, PLANE)  12.3 us
    pallas_call x3, Pallas kernels, call(): pl.pallas_call(kernel, out_shape=[f32(s) for s in outs], scratch_shapes=[...  10.7 us
    all_gather x1, blocking collectives, body(): gathered = lax.all_gather(pack, PLANE)  10.3 us
    ppermute x1, waiting for transfers between devices, plane_form(): high = lax.ppermute(left, 'gz', chain(k.gz, -1))  4.12 us
    ppermute x1, waiting for transfers between devices, plane_form(): low = lax.ppermute(right, 'gz', chain(k.gz, 1))  3.53 us
    ppermute x1, starting transfers between devices, plane_form(): low = lax.ppermute(right, 'gz', chain(k.gz, 1))  3.49 us
    ppermute x1, starting transfers between devices, plane_form(): high = lax.ppermute(left, 'gz', chain(k.gz, -1))  1.29 us
    ppermute x1, starting transfers between devices, body(): got = [lax.ppermute(f, 'gx', perm) for f, perm in zip(frames, (xa, xb))]  1.21 us
  transfers between devices with their start and end apart: 3, of which 2 were waited for; matrix products, arithmetic and copies ran while one was open for 0% of the time, Pallas kernels for 0%

profile of v3, /device:TPU:0, one launch (start us, length us, event | category | flops | bytes accessed | tf_op | source)
XLA Modules:
  0.0 47.0 jit_solution(8259949984076688317)
XLA Ops:
  0.0 0.0 copy-start
  0.0 12.3 %all-gather = f32[96,16,128]{2,1,0:T(8,128)S(1)} all-gather(f32[12,16,128]{2,1,0:T(8,128)} %param.2), channel_id=2, replica_groups=mesh['gx'=2,'gy'=4,'gz'=4] {'gx','gy'}, dimensions={0}, use_global_device_ids=true | all-gather | bytes 884736 | tf_op jit(solution)/shard_map/all_gather | solution.py:664
  12.4 0.0 copy-done
  12.4 1.9 %shard_map.28 = (f32[12,32,128]{2,1,0:T(8,128)S(1)}, f32[17,32,128]{2,1,0:T(8,128)S(1)}, f32[400,128]{1,0:T(8,128)S(1)}, f32[400,128]{1,0:T(8,128)S(1)}) custom-call(f32[8,12,16,128]{3,2,1,0:T(8,128)S(1)} %bitcast.3, f32[3,12,16,128]{3,2,1,0:T(8,128)S(1)} %copy-done), custom_call_target="tpu_custom_call" | custom-call | flops 4194304 | bytes 1048576 | tf_op jit(solution)/shard_map/pallas_call | solution.py:617
  14.3 3.5 %collective-permute-start = (f32[400,128]{1,0:T(8,128)S(1)}, f32[400,128]{1,0:T(8,128)S(1)}, u32[]{:S(2)}, u32[]{:S(2)}) collective-permute-start(f32[400,128]{1,0:T(8,128)S(1)} %get-tuple-element.14), channel_id=1, source_target_pairs={{0,1},{1,2},{2,3},{4,5},{5,6},{6,7},{8,9},{9,10},{10,11},{12,13},{... | collective-permute-start | bytes 614408 | tf_op jit(solution)/shard_map/ppermute | solution.py:671
  17.8 1.3 %collective-permute-start.1 = (f32[400,128]{1,0:T(8,128)S(1)}, f32[400,128]{1,0:T(8,128)S(1)}, u32[]{:S(2)}, u32[]{:S(2)}) collective-permute-start(f32[400,128]{1,0:T(8,128)S(1)} %get-tuple-element.15), channel_id=1, source_target_pairs={{1,0},{2,1},{3,2},{5,4},{6,5},{7,6},{9,8},{10,9},{11,10},{13,12},{... | collective-permute-start | bytes 614408 | tf_op jit(solution)/shard_map/ppermute | solution.py:672
  19.1 3.5 %collective-permute-done.refs_3_ = f32[400,128]{1,0:T(8,128)S(1)} collective-permute-done((f32[400,128]{1,0:T(8,128)S(1)}, f32[400,128]{1,0:T(8,128)S(1)}, u32[]{:S(2)}, u32[]{:S(2)}) %collective-permute-start) | collective-permute-done | bytes 204832 | tf_op jit(solution)/shard_map/ppermute | solution.py:671
  22.6 4.1 %collective-permute-done.1.refs_4_ = f32[400,128]{1,0:T(8,128)S(1)} collective-permute-done((f32[400,128]{1,0:T(8,128)S(1)}, f32[400,128]{1,0:T(8,128)S(1)}, u32[]{:S(2)}, u32[]{:S(2)}) %collective-permute-start.1) | collective-permute-done | bytes 204832 | tf_op jit(solution)/shard_map/ppermute | solution.py:672
  26.7 5.7 %shard_map.29 = (f32[248,128]{1,0:T(8,128)S(1)}, f32[4,16,128]{2,1,0:T(8,128)S(1)}, f32[12,16,128]{2,1,0:T(8,128)S(1)}) custom-call(f32[12,32,128]{2,1,0:T(8,128)S(1)} %get-tuple-element.12.refs_0_, f32[17,32,128]{2,1,0:T(8,128)S(1)} %get-tuple-element.13.refs_1_, f32[3,12,16,128]{3,2,1,0:T(8,128)S(1)} %copy-done, ...), custom_call_target="tpu_custom_call" | custom-call | flops 16777216 | bytes 1048576 | tf_op jit(solution)/shard_map/pallas_call | solution.py:617
  32.4 1.2 %collective-permute-start.2 = (f32[4,16,128]{2,1,0:T(8,128)S(1)}, f32[4,16,128]{2,1,0:T(8,128)S(1)}, u32[]{:S(2)}, u32[]{:S(2)}) collective-permute-start(f32[4,16,128]{2,1,0:T(8,128)S(1)} %get-tuple-element.18), channel_id=1, source_target_pairs={{0,16},{16,0},{1,17},{17,1},{2,18},{18,2},{3,19},{19,3},{4,20},{20... | collective-permute-start | bytes 98312 | tf_op jit(solution)/shard_map/ppermute | solution.py:700
  33.6 10.3 %all-gather.1 = f32[1984,128]{1,0:T(8,128)S(1)} all-gather(f32[248,128]{1,0:T(8,128)S(1)} %get-tuple-element.16), channel_id=3, replica_groups=mesh['gx'=2,'gy'=4,'gz'=4] {'gx','gy'}, dimensions={0}, use_global_device_ids=true | all-gather | bytes 1142784 | tf_op jit(solution)/shard_map/all_gather | solution.py:701
  43.9 0.0 collective-permute-done.2.refs_2_
  43.9 3.1 %shard_map.30 = f32[12,16,128]{2,1,0:T(8,128)} custom-call(f32[8,248,128]{2,1,0:T(8,128)S(1)} %bitcast.2, f32[12,16,128]{2,1,0:T(8,128)S(1)} %get-tuple-element.17.refs_1_, f32[4,16,128]{2,1,0:T(8,128)S(1)} %collective-permute-done.2.refs_2_), custom_call_target="tpu_custom_call" | custom-call | flops 8388608 | bytes 1048576 | tf_op jit(solution)/shard_map/pallas_call | solution.py:617
Async XLA Ops:
  0.0 12.4 %copy-start = (f32[3,12,16,128]{3,2,1,0:T(8,128)S(1)}, f32[3,12,16,128]{3,2,1,0:T(8,128)}, u32[]{:S(2)}) copy-start(f32[3,12,16,128]{3,2,1,0:T(8,128)} %refs_2_.1) | copy-start | bytes 884740
  14.3 8.3 %collective-permute-start = (f32[400,128]{1,0:T(8,128)S(1)}, f32[400,128]{1,0:T(8,128)S(1)}, u32[]{:S(2)}, u32[]{:S(2)}) collective-permute-start(f32[400,128]{1,0:T(8,128)S(1)} %get-tuple-element.14), channel_id=1, source_target_pairs={{0,1},{1,2},{2,3},{4,5},{5,6},{6,7},{8,9},{9,10},{10,11},{12,13},{... | collective-permute-start | bytes 614408 | tf_op jit(solution)/shard_map/ppermute | solution.py:671
  17.8 9.0 %collective-permute-start.1 = (f32[400,128]{1,0:T(8,128)S(1)}, f32[400,128]{1,0:T(8,128)S(1)}, u32[]{:S(2)}, u32[]{:S(2)}) collective-permute-start(f32[400,128]{1,0:T(8,128)S(1)} %get-tuple-element.15), channel_id=1, source_target_pairs={{1,0},{2,1},{3,2},{5,4},{6,5},{7,6},{9,8},{10,9},{11,10},{13,12},{... | collective-permute-start | bytes 614408 | tf_op jit(solution)/shard_map/ppermute | solution.py:672
  32.4 11.5 %collective-permute-start.2 = (f32[4,16,128]{2,1,0:T(8,128)S(1)}, f32[4,16,128]{2,1,0:T(8,128)S(1)}, u32[]{:S(2)}, u32[]{:S(2)}) collective-permute-start(f32[4,16,128]{2,1,0:T(8,128)S(1)} %get-tuple-element.18), channel_id=1, source_target_pairs={{0,16},{16,0},{1,17},{17,1},{2,18},{18,2},{3,19},{19,3},{4,20},{20... | collective-permute-start | bytes 98312 | tf_op jit(solution)/shard_map/ppermute | solution.py:700

commit v4 on v2

--- a/solution.py
+++ b/solution.py
@@ -281,14 +281,11 @@
     return jnp.where(lane < half, pltpu.roll(first, half, 1), pltpu.roll(second, half, 1))
 
 
-def middle_kernel(k, g_ref, win_ref, got_a, got_b, w_ref, low_ref, high_ref, pack_ref, xa_ref, xb_ref, own_ref,
-                  b1, m1, e1, half1, b2, u2, v2, b, m, v, vel, flux, half_ref, c2):
+def assemble_edges(k, refs, b1, b, pad):
+    g_ref, win_ref, got_a, got_b, w_ref, low_ref, high_ref = refs
     ix, iy, iz = place()
     bx, by = k.bx, k.by
     overlap_add(k, g_ref, b1, k.c1_n, k.c1_rows, 2, k.c1_first)
-    coarse(k, iz, b1, m1, e1, half1, b2, u2, v2)
-    pad = 5
-    mask = fine_mask(k, iy, iz)
     even = lax.rem(iy, 2) == 0
     for x in range(bx):
         b[x + pad, :SIDE, :] = jnp.where(even, got_b[x], got_a[x])
@@ -311,6 +308,26 @@
                 b[at, :SIDE, lanes] = g_ref[who * k.gy + y_low, row + by - 8:row + by, :]
                 b[at, SIDE:SIDE + by, lanes] = g_ref[who * k.gy + iy, row:row + by, :]
                 b[at, SIDE + by:, lanes] = g_ref[who * k.gy + y_high, row:row + 8, :]
+    half, part = k.bz // 2, k.bz // 4
+
+    def winds(x):
+        low, high = low_ref[x], high_ref[x]
+        q, r = x // 4, x % 4
+        return (wind_window(k, w_ref[0, x], low, half, high, 0),
+                wind_window(k, w_ref[1, x], low, half + part, high, part),
+                wind_window(k, w_ref[2, x], low_ref[bx + q], part * r, high_ref[bx + q], part * r))
+
+    return winds
+
+
+def middle_kernel(k, assemble, ins, pack_ref, xa_ref, xb_ref, own_ref,
+                  b1, m1, e1, half1, b2, u2, v2, b, m, v, vel, flux, half_ref, c2):
+    ix, iy, iz = place()
+    bx, by = k.bx, k.by
+    pad = 5
+    winds = assemble(k, ins, b1, b, pad)
+    coarse(k, iz, b1, m1, e1, half1, b2, u2, v2)
+    mask = fine_mask(k, iy, iz)
 
     def clean(i):
         b[i] = b[i] * (mask * x_inside(k, ix, i - pad))
@@ -353,13 +370,8 @@
     each(bx + 2, speed)
     own_mask = mask[SIDE:SIDE + by, :]
     zero(flux)
-    half, part = k.bz // 2, k.bz // 4
     for x in range(bx):
-        low, high = low_ref[x], high_ref[x]
-        w0 = 0.5 * wind_window(k, w_ref[0, x], low, half, high, 0)
-        w1 = 0.5 * wind_window(k, w_ref[1, x], low, half + part, high, part)
-        q, r = x // 4, x % 4
-        w2 = 0.5 * wind_window(k, w_ref[2, x], low_ref[bx + q], part * r, high_ref[bx + q], part * r)
+        w0, w1, w2 = (0.5 * w for w in winds(x))
         for d in range(3):
             c = vel[d, x + 1, SIDE:SIDE + by, :]
             xp, xm = vel[d, x + 2, SIDE:SIDE + by, :], vel[d, x, SIDE:SIDE + by, :]
@@ -379,12 +391,6 @@
 
     each(bx + 2, spread_flux)
     zero(v)
-
-    def power1(i):
-        at = i + pad - 2
-        c = mix(b, at) * (mask * x_inside(k, ix, i - 2))
-        m[at] = c
-        b[at] = b[at] + c
 
     def power1_pure(i):
         at = i + pad - 2
@@ -512,7 +518,7 @@
     return [big, big, big, (n2, k.rows1p, k.l1), (n2, rows2, k.l1), (n2 + 2, rows2, k.l1), (n2 + 2, rows2, k.l1)]
 
 
-def body(k, pressure, wind):
+def edge_form(k, pressure, wind):
     bx, by, bz = k.bx, k.by, k.bz
     slab = (bx + -(-bx // 4), by, bz)
     right, left = call(functools.partial(slab_kernel, k), [slab, slab], [], (pressure, wind), 1 << 20)
@@ -528,25 +534,31 @@
     got_a = lax.ppermute(send_a, "gy", ya)
     got_b = lax.ppermute(send_b, "gy", yb)
     gathered = lax.all_gather(pack, PLANE)
+    return assemble_edges, (gathered, window, got_a, got_b, wind, low, high)
+
+
+def general(k, pressure, wind):
+    bx, by, bz = k.bx, k.by, k.bz
+    fine = lambda n: (n, k.rows, k.lanes)
+    assemble, args = edge_form(k, pressure, wind)
     xa, xb = pairs(k.gx)
     x_outs = [(4, by, bz)] * (2 if xb else 1)
-    n_in = 7
 
     def middle(*refs):
-        ins, rest = refs[:n_in], refs[n_in:]
+        ins, rest = refs[:len(args)], refs[len(args):]
         pack_ref, rest = rest[0], rest[1:]
         xa_ref, rest = rest[0], rest[1:]
         xb_ref = None
         if xb:
             xb_ref, rest = rest[0], rest[1:]
-        middle_kernel(k, *ins, pack_ref, xa_ref, xb_ref, *rest)
+        middle_kernel(k, assemble, ins, pack_ref, xa_ref, xb_ref, *rest)
 
     big = fine(bx + 10)
     outs = call(
         middle, [(k.pack2, bz)] + x_outs + [(bx, by, bz)],
         coarse_scratch(k) + [big, big, big, (3,) + fine(bx + 2), (3,) + fine(bx + 4),
                              (bx // 2 + 4, k.rows, k.l1), (bx // 2 + 4, k.rows // 2, k.l1)],
-        (gathered, window, got_a, got_b, wind, low, high), 1 << 24)
+        args, 1 << 24)
     pack, frames, own = outs[0], outs[1:-1], outs[-1]
     got = [lax.ppermute(f, "gx", perm) for f, perm in zip(frames, (xa, xb))]
     gathered = lax.all_gather(pack, PLANE)
@@ -564,12 +576,414 @@
         (gathered, own, *got), 1 << 23)
     return result
 
+FR = 5
+CR = 2
+
+
+class Mirror:
+    def __init__(self, gx, gy, gz, bx, by, bz):
+        self.gx, self.gy, self.gz, self.bx, self.by, self.bz = gx, gy, gz, bx, by, bz
+        self.rows = by + 2 * FR
+        self.core = by + 8
+        self.nx, self.ny = gx * bx, gy * by
+        self.nx1, self.ny1 = self.nx // 2, self.ny // 2
+        self.rows1 = self.ny1 + 8
+        self.part = bz // 4
+        groups = lambda n: -(-n // 4)
+        self.fine_n = bx + 5
+        self.at_fine = groups(self.nx1) * self.ny1
+        self.at_wind = self.at_fine + groups(self.fine_n) * self.rows
+        self.slab_rows = self.at_wind + groups(3 * bx) * by
+        self.c2_n, self.c2_rows = bx // 2 + 2, by // 2 + 4
+        self.yf_n, self.yf_at = bx + 3, (bx // 2 + 2) * (by // 2 + 4)
+        self.pack = self.yf_at + 8 * self.yf_n
+
+
+def exact_dot(x, a):
+    high = x.astype(jnp.bfloat16)
+    low = (x - high.astype(jnp.float32)).astype(jnp.bfloat16)
+    return (jnp.dot(high, a, preferred_element_type=jnp.float32)
+            + jnp.dot(low, a, preferred_element_type=jnp.float32))
+
+
+def matrix(hit, value):
+    return jnp.where(hit, value, 0.0).astype(jnp.float32).astype(jnp.bfloat16)
+
+
+def flag(good):
+    return jnp.where(good, 1.0, 0.0).astype(jnp.float32)
+
+
+def beside(c0, c1):
+    n = c0.shape[1]
+    lane = iota(c0.shape, 1)
+    last, first = lane == n - 1, lane == 0
+    u0, u1, d0, d1 = up(c0, 1), up(c1, 1), down(c0, 1), down(c1, 1)
+    return ((jnp.where(last, u1, u0), jnp.where(last, u0, u1)),
+            (jnp.where(first, d1, d0), jnp.where(first, d0, d1)))
+
+
+def mix_halves(s, i, halves=2):
+    n = s.shape[2] - 2
+    c = [s[i + 1, h, 1:1 + n, :] for h in range(2)]
+    plus, minus = beside(*c)
+    out = []
+    for h in range(halves):
+        near = (s[i, h, 1:1 + n, :] + s[i + 2, h, 1:1 + n, :]) + (s[i + 1, h, 2:2 + n, :] + s[i + 1, h, :n, :])
+        out.append((1.0 - OMEGA) * c[h] + W * (near + (plus[h] + minus[h])))
+    return out
+
+
+def halves_mask(k, iy, iz):
+    y = iota((k.core, k.bz), 0) + (iy * k.by - 4)
+    lane = iota((k.core, k.bz), 1)
+    y_good = (y >= 0) & (y < k.ny)
+    edge = flag(y_good)
+    side = jnp.where(lane < k.bz // 2, jnp.where(iz < k.gz - 1, 1.0, 0.0), jnp.where(iz > 0, 1.0, 0.0))
+    return edge, edge * side.astype(jnp.float32)
+
+
+def zero_rim(s):
+    s[0] = jnp.zeros(s.shape[1:], jnp.float32)
+    n = s.shape[2]
+    for i in range(1, s.shape[0]):
+        for h in range(2):
+            s[i, h, 0:1, :] = jnp.zeros((1, s.shape[3]), jnp.float32)
+            s[i, h, n - 1:n, :] = jnp.zeros((1, s.shape[3]), jnp.float32)
+
+
+def mix1(k, s, i, n, at):
+    c = s[i + 1, at:at + n, :]
+    near = (s[i, at:at + n, :] + s[i + 2, at:at + n, :]) + (s[i + 1, at + 1:at + n + 1, :] + s[i + 1, at - 1:at + n - 1, :])
+    return (1.0 - OMEGA) * c + W * (near + (up(c, 1) + down(c, 1)))
+
+
+def coarse_plane(k, iz, b1, m1, e1, half_ref, b2, u2, v2):
+    n1, n2, ny, l1 = k.nx1, k.nx1 // 2, k.ny1, k.bz
+    ny2 = ny // 2
+    lane = iota((ny, l1), 1)
+    low_ok, high_ok = flag(iz > 0), flag(iz < k.gz - 1)
+    mask1 = jnp.where(lane < l1 // 2, 1.0, jnp.where(lane < 3 * l1 // 4, high_ok, low_ok))
+    lane2 = iota((ny2, l1), 1)
+    own2 = l1 // 8
+    mask2 = jnp.where(lane2 < own2, low_ok, jnp.where(lane2 < 3 * own2, 1.0, jnp.where(lane2 < 4 * own2, high_ok, 0.0)))
+    for s in (m1, e1):
+        for i in (0, n1 + 1):
+            s[i] = jnp.zeros(s.shape[1:], jnp.float32)
+    for s in (b1, m1, e1):
+        for i in range(n1):
+            s[i + 1, :CR, :] = jnp.zeros((CR, l1), jnp.float32)
+            s[i + 1, CR + ny:, :] = jnp.zeros((k.rows1 - CR - ny, l1), jnp.float32)
+    zero(u2)
+    zero(v2)
+    for i in range(n1):
+        b1[i + 1, CR:CR + ny, :] = b1[i + 1, CR:CR + ny, :] * mask1
+    for i in range(n1):
+        c = mix1(k, b1, i, ny, CR) * mask1
+        m1[i + 1, CR:CR + ny, :] = c
+        e1[i + 1, CR:CR + ny, :] = C1 * (b1[i + 1, CR:CR + ny, :] + c)
+    row, column = iota((l1, l1), 0), iota((l1, l1), 1)
+    linear = lambda x: (jnp.where(x < 3 * l1 // 4, x, x - l1) >> 1) + own2
+    for j in range(n2):
+        half_ref[j] = mix1(k, m1, 2 * j, ny, CR) + mix1(k, m1, 2 * j + 1, ny, CR)
+    pairs_sum = [half_ref[j, pl.ds(0, ny2, stride=2), :] + half_ref[j, pl.ds(1, ny2, stride=2), :] for j in range(n2)]
+    r2 = exact_dot(jnp.concatenate(pairs_sum, axis=0), matrix(linear(row) == column, 0.125))
+    for j in range(n2):
+        c = r2[j * ny2:(j + 1) * ny2] * (mask2 * C2)
+        b2[j] = c
+        u2[j + 1, 1:1 + ny2, :] = c
+    src, dst = u2, v2
+    for _ in range(3):
+        for j in range(n2):
+            dst[j + 1, 1:1 + ny2, :] = (mix1(k, src, j, ny2, 1) + b2[j]) * mask2
+        src, dst = dst, src
+    stack = jnp.concatenate([src[j + 1, 1:1 + ny2, :] for j in range(n2)], axis=0)
+    spread = exact_dot(stack, matrix(row == linear(column), 1.0))
+    for j in range(n2):
+        e = spread[j * ny2:(j + 1) * ny2]
+        half_ref[j, pl.ds(0, ny2, stride=2), :] = e
+        half_ref[j, pl.ds(1, ny2, stride=2), :] = e
+    for j in range(n2):
+        e = half_ref[j]
+        for t in range(2):
+            e1[2 * j + t + 1, CR:CR + ny, :] = e1[2 * j + t + 1, CR:CR + ny, :] + e
+    for src, dst in ((e1, m1), (m1, e1)):
+        for i in range(n1):
+            dst[i + 1, CR:CR + ny, :] = (mix1(k, src, i, ny, CR) + C1 * b1[i + 1, CR:CR + ny, :]) * mask1
+
+
+def from_end(ix, i, count):
+    return jnp.where(ix == 0, i, count - 1 - i)
+
+
+def prolong_halves(k, ix, iy, e1, n, v):
+    half, rows = k.bz // 2, k.core // 2
+    first = pl.multiple_of(iy * (k.by // 2), 8)
+    stack = jnp.concatenate([e1[from_end(ix, j, k.nx1) + 1, pl.ds(first, 16), :] for j in range(n)], axis=0)
+    row, column = iota((k.bz, 2 * k.bz), 0), iota((k.bz, 2 * k.bz), 1)
+    spread = exact_dot(stack, matrix(row == (column >> 1), 1.0))
+    for j in range(n):
+        for h in range(2):
+            e = spread[16 * j:16 * j + rows, h * k.bz:(h + 1) * k.bz]
+            for t in range(2):
+                v[2 * j + t + 1, h, pl.ds(1, rows, stride=2), :] = e
+                v[2 * j + t + 1, h, pl.ds(2, rows, stride=2), :] = e
+
+
+def take_slab(k, ref, base, rows, i, to):
+    at = base + (i // 4) * rows
+    return lane_roll(ref[at:at + rows, :], to - k.part * (i % 4))
+
+
+def plane_kernel(k, g_ref, w_ref, c1_ref, win_ref, right_ref, left_ref, p, m, q, half_ref):
+    ix, iy, iz = place()
+    bx, by, bz, nx, ny, part = k.bx, k.by, k.bz, k.nx, k.ny, k.part
+    p[0] = jnp.zeros(p.shape[1:], jnp.float32)
+    p[nx + 1] = jnp.zeros(p.shape[1:], jnp.float32)
+    m[0] = jnp.zeros(m.shape[1:], jnp.float32)
+    m[nx + 1] = jnp.zeros(m.shape[1:], jnp.float32)
+    for x in range(nx):
+        p[x + 1, :FR, :] = jnp.zeros((FR, bz), jnp.float32)
+        p[x + 1, FR + ny:, :] = jnp.zeros((p.shape[1] - FR - ny, bz), jnp.float32)
+        m[x + 1, 0:1, :] = jnp.zeros((1, bz), jnp.float32)
+        m[x + 1, ny + 1:, :] = jnp.zeros((m.shape[1] - ny - 1, bz), jnp.float32)
+        for j in range(k.gy):
+            p[x + 1, FR + j * by:FR + (j + 1) * by, :] = g_ref[(x // bx) * k.gy + j, x % bx]
+    lane = iota((ny, bz), 1)
+    first, last = lane == 0, lane == bz - 1
+    ends = jnp.where(first, flag(iz > 0), jnp.where(last, flag(iz < k.gz - 1), 0.0)) * (W * W)
+
+    def parts(s, x, at):
+        c = s[x + 1, at:at + ny, :]
+        four = (s[x, at:at + ny, :] + s[x + 2, at:at + ny, :]) + (s[x + 1, at + 1:at + ny + 1, :] + s[x + 1, at - 1:at + ny - 1, :])
+        along = jnp.where(last, 0.0, up(c, 1)) + jnp.where(first, 0.0, down(c, 1))
+        return c, four, (1.0 - OMEGA) * c + W * (four + along)
+
+    for x in range(nx):
+        c, four, mixed = parts(p, x, FR)
+        m[x + 1, 1:1 + ny, :] = mixed
+        q[x] = (1.0 - OMEGA + W) * c + (mixed + W * four)
+    row, column = iota((bz, bz), 0), iota((bz, bz), 1)
+    own = matrix((row >> 1) == column, 0.125)
+    rim = ((row == 0) & (column == bz - 1)) | ((row == bz - 1) & (column == bz // 2))
+    rim = matrix(rim, 0.125)
+    half_rows = ny // 2
+    for j in range(k.nx1):
+        s = None
+        for x in (2 * j, 2 * j + 1):
+            r = parts(m, x, 1)[2] + ends * p[x + 1, FR:FR + ny, :]
+            s = r if s is None else s + r
+        half_ref[j] = s
+        t = (q[2 * j, pl.ds(0, half_rows, stride=2), :] + q[2 * j, pl.ds(1, half_rows, stride=2), :]
+             + q[2 * j + 1, pl.ds(0, half_rows, stride=2), :] + q[2 * j + 1, pl.ds(1, half_rows, stride=2), :])
+        s = half_ref[j, pl.ds(0, half_rows, stride=2), :] + half_ref[j, pl.ds(1, half_rows, stride=2), :]
+        c1_ref[j] = exact_dot(s, own) + exact_dot(W * t, rim)
+
+    def pack(ref, base, rows, n, load, from_lane):
+        lane = iota((rows, bz), 1)
+        for group in range(-(-n // 4)):
+            total = jnp.zeros((rows, bz), jnp.float32)
+            for r in range(min(4, n - 4 * group)):
+                moved = lane_roll(load(4 * group + r), part * r - from_lane)
+                total = jnp.where((lane >= part * r) & (lane < part * (r + 1)), moved, total)
+            ref[base + group * rows:base + (group + 1) * rows, :] = total
+
+    for i in range(k.fine_n):
+        win_ref[i] = p[from_end(ix, i, nx) + 1, pl.ds(pl.multiple_of(iy * by, 8), k.rows), :]
+    for ref, lane1, lane0 in ((right_ref, part + 1, 3 * part), (left_ref, bz - 1, 0)):
+        pack(ref, 0, k.ny1, k.nx1, lambda i: c1_ref[i], lane1)
+        pack(ref, k.at_fine, k.rows, k.fine_n, lambda i: win_ref[i], lane0)
+        pack(ref, k.at_wind, by, 3 * bx, lambda i: w_ref[i // bx, from_end(ix, i % bx, bx)], lane0)
+
+
+def solve_kernel(k, c1_ref, win_ref, w_ref, low_ref, high_ref, pack_ref, x_ref, own_ref,
+                 b1, m1, e1, half1, b2, u2, v2, b, m, v, vel, flux, half_ref):
+    ix, iy, iz = place()
+    bx, by, bz, part, n = k.bx, k.by, k.bz, k.part, k.core
+    lane = iota((k.ny1, bz), 1)
+    for s in (b1,):
+        for i in (0, k.nx1 + 1):
+            s[i] = jnp.zeros(s.shape[1:], jnp.float32)
+    for x in range(k.nx1):
+        low = take_slab(k, low_ref, 0, k.ny1, x, 3 * part + 1)
+        high = take_slab(k, high_ref, 0, k.ny1, x, 2 * part - 1)
+        low = jnp.where((lane >= 3 * part + 1) | (lane == 0), low, 0.0)
+        high = jnp.where((lane >= 2 * part - 1) & (lane < 3 * part - 1), high, 0.0)
+        b1[x + 1, CR:CR + k.ny1, :] = c1_ref[x] + (low + high)
+    coarse_plane(k, iz, b1, m1, e1, half1, b2, u2, v2)
+    mask = halves_mask(k, iy, iz)
+    for s in (b, m, v):
+        zero_rim(s)
+
+    def outer(low, high, lane):
+        return jnp.where(lane >= 3 * part, low, jnp.where(lane < part, high, 0.0))
+
+    lane = iota((k.rows, bz), 1)
+    for i in range(k.fine_n):
+        b[i + 1, 0] = win_ref[i]
+        b[i + 1, 1] = outer(take_slab(k, low_ref, k.at_fine, k.rows, i, 3 * part),
+                            take_slab(k, high_ref, k.at_fine, k.rows, i, 0), lane)
+    prolong_halves(k, ix, iy, e1, bx // 2 + 2, v)
+    for i in range(bx + 4):
+        mb = mix_halves(b, i)
+        for h in range(2):
+            v[i + 1, h, 1:1 + n, :] = (v[i + 1, h, 1:1 + n, :] + C0 * (b[i + 1, h, 1:1 + n, :] + mb[h])) * mask[h]
+    for src, dst, count in ((v, m, bx + 3), (m, v, bx + 2)):
+        for i in range(count):
+            c = mix_halves(src, i)
+            for h in range(2):
+                dst[i + 1, h, 1:1 + n, :] = (c[h] + C0 * b[i + 1, h, 1:1 + n, :]) * mask[h]
+    half_mask = [0.5 * c for c in mask]
+    for d in range(3):
+        vel[d, 0] = jnp.zeros(vel.shape[2:], jnp.float32)
+    for i in range(bx + 1):
+        plus, minus = beside(v[i + 1, 0, 1:1 + n, :], v[i + 1, 1, 1:1 + n, :])
+        for h in range(2):
+            vel[0, i + 1, h] = (v[i + 2, h, 1:1 + n, :] - v[i, h, 1:1 + n, :]) * half_mask[h]
+            vel[1, i + 1, h] = (v[i + 1, h, 2:2 + n, :] - v[i + 1, h, :n, :]) * half_mask[h]
+            vel[2, i + 1, h] = (plus[h] - minus[h]) * half_mask[h]
+    own_at = 4
+    zero(flux)
+    sign = jnp.where(ix == 0, 0.5, -0.5).astype(jnp.float32)
+    lane = iota((by, bz), 1)
+    for x in range(bx):
+        winds = []
+        for d in range(3):
+            low = take_slab(k, low_ref, k.at_wind, by, d * bx + x, 3 * part)
+            high = take_slab(k, high_ref, k.at_wind, by, d * bx + x, 0)
+            scale = sign if d == 0 else 0.5
+            winds.append((scale * w_ref[d, from_end(ix, x, bx)], scale * outer(low, high, lane)))
+        for d in range(3):
+            at = lambda i, h, r: vel[d, i + 1, h, own_at + r:own_at + r + by, :]
+            c = [at(x, h, 0) for h in range(2)]
+            plus, minus = beside(*c)
+            for h in range(2):
+                xp, xm, yp, ym, zp, zm = at(x + 1, h, 0), at(x - 1, h, 0), at(x, h, 1), at(x, h, -1), plus[h], minus[h]
+                near = (xp + xm) + (yp + ym) + (zp + zm)
+                total = 7.0 * c[h] - near + winds[0][h] * (xp - xm) + winds[1][h] * (yp - ym) + winds[2][h] * (zp - zm)
+                if h == 1:
+                    total = total * mask[1][own_at:own_at + by]
+                flux[d, x + 1, h, own_at + 1:own_at + 1 + by, :] = total
+    minus_mask = [-0.5 * c for c in mask]
+    for s, first in ((b, bx + 2), (m, bx + 3), (v, bx + 4)):
+        for i in range(first, bx + 6):
+            s[i] = jnp.zeros(s.shape[1:], jnp.float32)
+    for i in range(bx + 1):
+        plus, minus = beside(flux[2, i + 1, 0, 1:1 + n, :], flux[2, i + 1, 1, 1:1 + n, :])
+        for h in range(2):
+            total = (flux[0, i + 2, h, 1:1 + n, :] - flux[0, i, h, 1:1 + n, :]
+                     + (flux[1, i + 1, h, 2:2 + n, :] - flux[1, i + 1, h, :n, :]) + (plus[h] - minus[h]))
+            b[i + 1, h, 1:1 + n, :] = total * minus_mask[h]
+    zero_rows = jnp.zeros((1, bz), jnp.float32)
+    for i in range(bx + 1):
+        for h in range(2):
+            b[i + 1, h, 0:1, :] = zero_rows
+            b[i + 1, h, n + 1:n + 2, :] = zero_rows
+    for src, dst, count in ((b, m, bx + 2), (m, v, bx + 3)):
+        for i in range(count):
+            c = mix_halves(src, i)
+            for h in range(2):
+                dst[i + 1, h, 1:1 + n, :] = c[h] * mask[h]
+    half_rows = n // 2
+    for j in range(k.c2_n):
+        for h in range(2):
+            take = lambda i, r: v[i + 1, h, pl.ds(r, half_rows, stride=2), :]
+            half_ref[h, j, :half_rows, :] = (take(2 * j, 1) + take(2 * j, 2)) + (take(2 * j + 1, 1) + take(2 * j + 1, 2))
+            half_ref[h, j, half_rows:, :] = jnp.zeros((16 - half_rows, bz), jnp.float32)
+    row, column = iota((bz, bz), 0), iota((bz, bz), 1)
+    c2 = (exact_dot(half_ref[0].reshape(k.c2_n * 16, bz), matrix((row >> 1) == column, 0.125))
+          + exact_dot(half_ref[1].reshape(k.c2_n * 16, bz), matrix((row >> 1) + bz // 2 == column, 0.125)))
+    for j in range(k.c2_n):
+        pack_ref[j * k.c2_rows:(j + 1) * k.c2_rows, :] = c2[16 * j:16 * j + k.c2_rows]
+    for i in range(bx + 4):
+        c = mix_halves(v, i, 1)[0]
+        at = lambda s: s[i + 1, 0, 1:1 + n, :]
+        c = C0 * ((at(b) + at(m)) + (at(v) + c)) * mask[0]
+        if i < bx:
+            own_ref[i] = c[4:4 + by]
+        else:
+            x_ref[i - bx] = c[4:4 + by]
+        if i < k.yf_n:
+            row = k.yf_at + 8 * i
+            pack_ref[row:row + 4, :] = c[4 + by:8 + by]
+            pack_ref[row + 4:row + 8, :] = c[:4]
+
+
+def close_kernel(k, g_ref, own_ref, x_ref, out_ref, b1, m1, e1, half1, b2, u2, v2, v, m):
+    ix, iy, iz = place()
+    bx, by, bz, n = k.bx, k.by, k.bz, k.core
+    zero(b1)
+    for i in range(2):
+        for j in range(k.gy):
+            at = j * (by // 2)
+            for q in range(k.c2_n):
+                x = q if i == 0 else k.nx1 - 1 - q
+                part = g_ref[i * k.gy + j, q * k.c2_rows:(q + 1) * k.c2_rows, :]
+                b1[x + 1, at:at + k.c2_rows, :] += part
+    coarse_plane(k, iz, b1, m1, e1, half1, b2, u2, v2)
+    mask = halves_mask(k, iy, iz)
+    for s in (v, m):
+        zero_rim(s)
+    prolong_halves(k, ix, iy, e1, bx // 2 + 1, v)
+    for i in range(bx + 2):
+        for h in range(2):
+            v[i + 1, h, 1:1 + n, :] = v[i + 1, h, 1:1 + n, :] * mask[h]
+    for i in range(bx + 1):
+        c = mix_halves(v, i)
+        for h in range(2):
+            m[i + 1, h, 1:1 + n, :] = c[h] * mask[h]
+    low_ok, high_ok = flag(iy > 0), flag(iy < k.gy - 1)
+    y_low, y_high = jnp.maximum(iy - 1, 0), jnp.minimum(iy + 1, k.gy - 1)
+    for i in range(bx):
+        c = mix_halves(m, i, 1)[0][4:4 + by] + own_ref[i]
+        if i >= bx - 4:
+            c = c + x_ref[bx - 1 - i]
+        at = from_end(ix, i, bx)
+        out_ref[at] = c
+        low, high = 0.0, 0.0
+        for who, plane in ((ix, i), (1 - ix, 2 * bx - 1 - i)):
+            if plane < k.yf_n:
+                row = k.yf_at + 8 * plane
+                low = low + g_ref[who * k.gy + y_low, row:row + 4, :]
+                high = high + g_ref[who * k.gy + y_high, row + 4:row + 8, :]
+        out_ref[at, :4, :] += low * low_ok
+        out_ref[at, by - 4:, :] += high * high_ok
+
+
+def mirrored(k, pressure, wind):
+    bx, by, bz = k.bx, k.by, k.bz
+    n1, n2 = k.nx1, k.nx1 // 2
+    fine = lambda n: (n + 2, 2, k.rows, bz)
+    level1 = [(n1 + 2, k.rows1, bz)] * 3
+    level2 = [(n2, k.ny1, bz), (n2, k.ny1 // 2, bz)] + [(n2 + 2, k.ny1 // 2 + 2, bz)] * 2
+    gathered = lax.all_gather(pressure, PLANE)
+    c1, window, right, left = call(
+        functools.partial(plane_kernel, k),
+        [(n1, k.ny1, bz), (k.fine_n, k.rows, bz), (k.slab_rows, bz), (k.slab_rows, bz)],
+        [(k.nx + 2, -(-(k.ny + 2 * FR) // 8) * 8, bz), (k.nx + 2, k.ny + 2, bz), (k.nx, k.ny, bz), (n1, k.ny, bz)],
+        (gathered, wind), 1 << 22)
+    low = lax.ppermute(right, "gz", chain(k.gz, 1))
+    high = lax.ppermute(left, "gz", chain(k.gz, -1))
+    pack, frame, own = call(
+        functools.partial(solve_kernel, k),
+        [(k.pack, bz), (4, by, bz), (bx, by, bz)],
+        level1 + level2 + [fine(bx + 5)] * 3 + [(3, bx + 3, 2, k.core, bz), (3,) + fine(bx + 1), (2, k.c2_n, 16, bz)],
+        (c1, window, wind, low, high), 1 << 24)
+    frame = lax.ppermute(frame, "gx", pairs(k.gx)[0])
+    gathered = lax.all_gather(pack, PLANE)
+    (result,) = call(
+        functools.partial(close_kernel, k), [(bx, by, bz)],
+        level1 + level2 + [fine(bx + 2)] * 2,
+        (gathered, own, frame), 1 << 23)
+    return result
+
 
 def solution(mesh):
     gx, gy, gz = (mesh.shape[a] for a in ("gx", "gy", "gz"))
 
     def run(pressure, wind):
-        return body(Sizes(gx, gy, gz, *pressure.shape), pressure, wind)
+        form, sizes = (mirrored, Mirror) if gx == 2 else (general, Sizes)
+        return form(sizes(gx, gy, gz, *pressure.shape), pressure, wind)
 
     in_specs = (P("gx", "gy", "gz"), P(None, "gx", "gy", "gz"))
     return jax.shard_map(run, mesh=mesh, in_specs=in_specs, out_specs=P("gx", "gy", "gz"), check_vma=False)

time: 50.2 us -> 43.4 us (0.86)
  blocking collectives: 25.9 us -> 22.4 us
  Pallas kernels: 9.6 us -> 7.39 us
  waiting for transfers between devices: 5.48 us -> 7.39 us
  local copies, waits for them, and re-layouts: 1.86 us -> 0.01 us
  starting transfers between devices: 7.07 us -> 5.99 us
    all_gather x2, blocking collectives: 25.9 us -> 22.4 us  [the longest x1 12.3 us: mirrored(): gathered = lax.all_gather(pressure, PLANE)]
    pallas_call x4 -> x3, Pallas kernels: 9.6 us -> 7.39 us  [call(): pl.pallas_call(kernel, out_shape=[f32(s) for s in outs], scratch_shapes=[...]
    ppermute x5 -> x3, waiting for transfers between devices: 5.48 us -> 7.39 us  [the longest x1 4.12 us: mirrored(): high = lax.ppermute(left, 'gz', chain(k.gz, -1))]
    unnamed x6 -> x2, local copies, waits for them, and re-layouts: 1.86 us -> 0.01 us
    ppermute x5 -> x3, starting transfers between devices: 7.07 us -> 5.99 us  [the longest x1 3.49 us: mirrored(): low = lax.ppermute(right, 'gz', chain(k.gz, 1))]
  transfers between devices with their start and end apart: 5 -> 3, of which waited for: 2 -> 2; matrix products, arithmetic and copies ran while one was open for 0% -> 0% of each run, Pallas kernels for 0% -> 0%
where the time goes in v4:
time: 43.4 us; the launch traced here: 43.2 us
  blocking collectives  22.4 us (52%)
  Pallas kernels  7.39 us (17%)
  waiting for transfers between devices  7.39 us (17%)
  starting transfers between devices  5.99 us (14%)
    all_gather x1, blocking collectives, mirrored(): gathered = lax.all_gather(pressure, PLANE)  12.3 us
    all_gather x1, blocking collectives, mirrored(): gathered = lax.all_gather(pack, PLANE)  10 us
    pallas_call x3, Pallas kernels, call(): pl.pallas_call(kernel, out_shape=[f32(s) for s in outs], scratch_shapes=[...  7.39 us
    ppermute x1, waiting for transfers between devices, mirrored(): high = lax.ppermute(left, 'gz', chain(k.gz, -1))  4.12 us
    ppermute x1, starting transfers between devices, mirrored(): low = lax.ppermute(right, 'gz', chain(k.gz, 1))  3.49 us
    ppermute x1, waiting for transfers between devices, mirrored(): low = lax.ppermute(right, 'gz', chain(k.gz, 1))  3.26 us
    ppermute x1, starting transfers between devices, mirrored(): high = lax.ppermute(left, 'gz', chain(k.gz, -1))  1.29 us
    ppermute x1, starting transfers between devices, mirrored(): frame = lax.ppermute(frame, 'gx', pairs(k.gx)[0])  1.21 us
  transfers between devices with their start and end apart: 3, of which 2 were waited for; matrix products, arithmetic and copies ran while one was open for 0% of the time, Pallas kernels for 0%

profile of v4, /device:TPU:0, one launch (start us, length us, event | category | flops | bytes accessed | tf_op | source)
XLA Modules:
  0.0 43.2 jit_solution(12559238492468822770)
XLA Ops:
  0.0 0.0 copy-start
  0.0 12.3 %all-gather = f32[96,16,128]{2,1,0:T(8,128)S(1)} all-gather(f32[12,16,128]{2,1,0:T(8,128)} %param.2), channel_id=2, replica_groups=mesh['gx'=2,'gy'=4,'gz'=4] {'gx','gy'}, dimensions={0}, use_global_device_ids=true | all-gather | bytes 884736 | tf_op jit(solution)/shard_map/all_gather | solution.py:959
  12.4 0.0 copy-done
  12.4 1.6 %shard_map.28 = (f32[12,32,128]{2,1,0:T(8,128)S(1)}, f32[17,26,128]{2,1,0:T(8,128)S(1)}, f32[370,128]{1,0:T(8,128)S(1)}, f32[370,128]{1,0:T(8,128)S(1)}) custom-call(f32[8,12,16,128]{3,2,1,0:T(8,128)S(1)} %bitcast.3, f32[3,12,16,128]{3,2,1,0:T(8,128)S(1)} %copy-done), custom_call_target="tpu_custom_call" | custom-call | flops 4194304 | bytes 1048576 | tf_op jit(solution)/shard_map/pallas_call | solution.py:496
  13.9 3.5 %collective-permute-start = (f32[370,128]{1,0:T(8,128)S(1)}, f32[370,128]{1,0:T(8,128)S(1)}, u32[]{:S(2)}, u32[]{:S(2)}) collective-permute-start(f32[370,128]{1,0:T(8,128)S(1)} %get-tuple-element.14), channel_id=1, source_target_pairs={{0,1},{1,2},{2,3},{4,5},{5,6},{6,7},{8,9},{9,10},{10,11},{12,13},{... | collective-permute-start | bytes 568328 | tf_op jit(solution)/shard_map/ppermute | solution.py:965
  17.4 1.3 %collective-permute-start.1 = (f32[370,128]{1,0:T(8,128)S(1)}, f32[370,128]{1,0:T(8,128)S(1)}, u32[]{:S(2)}, u32[]{:S(2)}) collective-permute-start(f32[370,128]{1,0:T(8,128)S(1)} %get-tuple-element.15), channel_id=1, source_target_pairs={{1,0},{2,1},{3,2},{5,4},{6,5},{7,6},{9,8},{10,9},{11,10},{13,12},{... | collective-permute-start | bytes 568328 | tf_op jit(solution)/shard_map/ppermute | solution.py:966
  18.7 3.3 %collective-permute-done.low_ref = f32[370,128]{1,0:T(8,128)S(1)} collective-permute-done((f32[370,128]{1,0:T(8,128)S(1)}, f32[370,128]{1,0:T(8,128)S(1)}, u32[]{:S(2)}, u32[]{:S(2)}) %collective-permute-start) | collective-permute-done | bytes 189472 | tf_op jit(solution)/shard_map/ppermute | solution.py:965
  22.0 4.1 %collective-permute-done.1.high_ref = f32[370,128]{1,0:T(8,128)S(1)} collective-permute-done((f32[370,128]{1,0:T(8,128)S(1)}, f32[370,128]{1,0:T(8,128)S(1)}, u32[]{:S(2)}, u32[]{:S(2)}) %collective-permute-start.1) | collective-permute-done | bytes 189472 | tf_op jit(solution)/shard_map/ppermute | solution.py:966
  26.1 3.4 %shard_map.29 = (f32[216,128]{1,0:T(8,128)S(1)}, f32[4,16,128]{2,1,0:T(8,128)S(1)}, f32[12,16,128]{2,1,0:T(8,128)S(1)}) custom-call(f32[12,32,128]{2,1,0:T(8,128)S(1)} %get-tuple-element.12.c1_ref, f32[17,26,128]{2,1,0:T(8,128)S(1)} %get-tuple-element.13.win_ref, f32[3,12,16,128]{3,2,1,0:T(8,128)S(1)} %copy-done, ...), custom_call_target="tpu_custom_call" | custom-call | flops 16777216 | bytes 1048576 | tf_op jit(solution)/shard_map/pallas_call | solution.py:496
  29.6 1.2 %collective-permute-start.2 = (f32[4,16,128]{2,1,0:T(8,128)S(1)}, f32[4,16,128]{2,1,0:T(8,128)S(1)}, u32[]{:S(2)}, u32[]{:S(2)}) collective-permute-start(f32[4,16,128]{2,1,0:T(8,128)S(1)} %get-tuple-element.18), channel_id=1, source_target_pairs={{0,16},{16,0},{1,17},{17,1},{2,18},{18,2},{3,19},{19,3},{4,20},{20... | collective-permute-start | bytes 98312 | tf_op jit(solution)/shard_map/ppermute | solution.py:972
  30.8 10.0 %all-gather.1 = f32[1728,128]{1,0:T(8,128)S(1)} all-gather(f32[216,128]{1,0:T(8,128)S(1)} %get-tuple-element.16), channel_id=3, replica_groups=mesh['gx'=2,'gy'=4,'gz'=4] {'gx','gy'}, dimensions={0}, use_global_device_ids=true | all-gather | bytes 995328 | tf_op jit(solution)/shard_map/all_gather | solution.py:973
  40.8 0.0 collective-permute-done.2.x_ref
  40.8 2.4 %shard_map.30 = f32[12,16,128]{2,1,0:T(8,128)} custom-call(f32[8,216,128]{2,1,0:T(8,128)S(1)} %bitcast.2, f32[12,16,128]{2,1,0:T(8,128)S(1)} %get-tuple-element.17.own_ref, f32[4,16,128]{2,1,0:T(8,128)S(1)} %collective-permute-done.2.x_ref), custom_call_target="tpu_custom_call" | custom-call | flops 8388608 | bytes 1048576 | tf_op jit(solution)/shard_map/pallas_call | solution.py:496
Async XLA Ops:
  0.0 12.4 %copy-start = (f32[3,12,16,128]{3,2,1,0:T(8,128)S(1)}, f32[3,12,16,128]{3,2,1,0:T(8,128)}, u32[]{:S(2)}) copy-start(f32[3,12,16,128]{3,2,1,0:T(8,128)} %w_ref.3) | copy-start | bytes 884740
  13.9 8.1 %collective-permute-start = (f32[370,128]{1,0:T(8,128)S(1)}, f32[370,128]{1,0:T(8,128)S(1)}, u32[]{:S(2)}, u32[]{:S(2)}) collective-permute-start(f32[370,128]{1,0:T(8,128)S(1)} %get-tuple-element.14), channel_id=1, source_target_pairs={{0,1},{1,2},{2,3},{4,5},{5,6},{6,7},{8,9},{9,10},{10,11},{12,13},{... | collective-permute-start | bytes 568328 | tf_op jit(solution)/shard_map/ppermute | solution.py:965
  17.4 8.7 %collective-permute-start.1 = (f32[370,128]{1,0:T(8,128)S(1)}, f32[370,128]{1,0:T(8,128)S(1)}, u32[]{:S(2)}, u32[]{:S(2)}) collective-permute-start(f32[370,128]{1,0:T(8,128)S(1)} %get-tuple-element.15), channel_id=1, source_target_pairs={{1,0},{2,1},{3,2},{5,4},{6,5},{7,6},{9,8},{10,9},{11,10},{13,12},{... | collective-permute-start | bytes 568328 | tf_op jit(solution)/shard_map/ppermute | solution.py:966
  29.6 11.2 %collective-permute-start.2 = (f32[4,16,128]{2,1,0:T(8,128)S(1)}, f32[4,16,128]{2,1,0:T(8,128)S(1)}, u32[]{:S(2)}, u32[]{:S(2)}) collective-permute-start(f32[4,16,128]{2,1,0:T(8,128)S(1)} %get-tuple-element.18), channel_id=1, source_target_pairs={{0,16},{16,0},{1,17},{17,1},{2,18},{18,2},{3,19},{19,3},{4,20},{20... | collective-permute-start | bytes 98312 | tf_op jit(solution)/shard_map/ppermute | solution.py:972

commit v5 on v4

--- a/solution.py
+++ b/solution.py
@@ -595,8 +595,12 @@
         self.at_wind = self.at_fine + groups(self.fine_n) * self.rows
         self.slab_rows = self.at_wind + groups(3 * bx) * by
         self.c2_n, self.c2_rows = bx // 2 + 2, by // 2 + 4
-        self.yf_n, self.yf_at = bx + 3, (bx // 2 + 2) * (by // 2 + 4)
-        self.pack = self.yf_at + 8 * self.yf_n
+        self.c2 = self.c2_n * self.c2_rows
+        self.yf_n = bx + 3
+        self.to3 = self.c2 + 8 * self.yf_n
+        self.to4 = self.c2 + 8 * 3 + 4 * by
+        self.to7 = self.c2 + 8 * 3
+        self.to1 = 4 * self.c2 + 8 * self.yf_n + 8 * 3
 
 
 def exact_dot(x, a):
@@ -716,10 +720,10 @@
     return jnp.where(ix == 0, i, count - 1 - i)
 
 
-def prolong_halves(k, ix, iy, e1, n, v):
+def prolong_halves(k, iy, e1, n, v):
     half, rows = k.bz // 2, k.core // 2
     first = pl.multiple_of(iy * (k.by // 2), 8)
-    stack = jnp.concatenate([e1[from_end(ix, j, k.nx1) + 1, pl.ds(first, 16), :] for j in range(n)], axis=0)
+    stack = jnp.concatenate([e1[j + 1, pl.ds(first, 16), :] for j in range(n)], axis=0)
     row, column = iota((k.bz, 2 * k.bz), 0), iota((k.bz, 2 * k.bz), 1)
     spread = exact_dot(stack, matrix(row == (column >> 1), 1.0))
     for j in range(n):
@@ -747,8 +751,9 @@
         p[x + 1, FR + ny:, :] = jnp.zeros((p.shape[1] - FR - ny, bz), jnp.float32)
         m[x + 1, 0:1, :] = jnp.zeros((1, bz), jnp.float32)
         m[x + 1, ny + 1:, :] = jnp.zeros((m.shape[1] - ny - 1, bz), jnp.float32)
+        who = ix if x < bx else 1 - ix
         for j in range(k.gy):
-            p[x + 1, FR + j * by:FR + (j + 1) * by, :] = g_ref[(x // bx) * k.gy + j, x % bx]
+            p[x + 1, FR + j * by:FR + (j + 1) * by, :] = g_ref[who * k.gy + j, from_end(ix, x % bx, bx)]
     lane = iota((ny, bz), 1)
     first, last = lane == 0, lane == bz - 1
     ends = jnp.where(first, flag(iz > 0), jnp.where(last, flag(iz < k.gz - 1), 0.0)) * (W * W)
@@ -789,14 +794,14 @@
             ref[base + group * rows:base + (group + 1) * rows, :] = total
 
     for i in range(k.fine_n):
-        win_ref[i] = p[from_end(ix, i, nx) + 1, pl.ds(pl.multiple_of(iy * by, 8), k.rows), :]
+        win_ref[i] = p[i + 1, pl.ds(pl.multiple_of(iy * by, 8), k.rows), :]
     for ref, lane1, lane0 in ((right_ref, part + 1, 3 * part), (left_ref, bz - 1, 0)):
         pack(ref, 0, k.ny1, k.nx1, lambda i: c1_ref[i], lane1)
         pack(ref, k.at_fine, k.rows, k.fine_n, lambda i: win_ref[i], lane0)
         pack(ref, k.at_wind, by, 3 * bx, lambda i: w_ref[i // bx, from_end(ix, i % bx, bx)], lane0)
 
 
-def solve_kernel(k, c1_ref, win_ref, w_ref, low_ref, high_ref, pack_ref, x_ref, own_ref,
+def solve_kernel(k, c1_ref, win_ref, w_ref, low_ref, high_ref, to3_ref, to4_ref, to7_ref, own_ref,
                  b1, m1, e1, half1, b2, u2, v2, b, m, v, vel, flux, half_ref):
     ix, iy, iz = place()
     bx, by, bz, part, n = k.bx, k.by, k.bz, k.part, k.core
@@ -823,7 +828,7 @@
         b[i + 1, 0] = win_ref[i]
         b[i + 1, 1] = outer(take_slab(k, low_ref, k.at_fine, k.rows, i, 3 * part),
                             take_slab(k, high_ref, k.at_fine, k.rows, i, 0), lane)
-    prolong_halves(k, ix, iy, e1, bx // 2 + 2, v)
+    prolong_halves(k, iy, e1, bx // 2 + 2, v)
     for i in range(bx + 4):
         mb = mix_halves(b, i)
         for h in range(2):
@@ -894,7 +899,8 @@
     c2 = (exact_dot(half_ref[0].reshape(k.c2_n * 16, bz), matrix((row >> 1) == column, 0.125))
           + exact_dot(half_ref[1].reshape(k.c2_n * 16, bz), matrix((row >> 1) + bz // 2 == column, 0.125)))
     for j in range(k.c2_n):
-        pack_ref[j * k.c2_rows:(j + 1) * k.c2_rows, :] = c2[16 * j:16 * j + k.c2_rows]
+        for ref in (to3_ref, to4_ref, to7_ref):
+            ref[j * k.c2_rows:(j + 1) * k.c2_rows, :] = c2[16 * j:16 * j + k.c2_rows]
     for i in range(bx + 4):
         c = mix_halves(v, i, 1)[0]
         at = lambda s: s[i + 1, 0, 1:1 + n, :]
@@ -902,29 +908,44 @@
         if i < bx:
             own_ref[i] = c[4:4 + by]
         else:
-            x_ref[i - bx] = c[4:4 + by]
-        if i < k.yf_n:
-            row = k.yf_at + 8 * i
-            pack_ref[row:row + 4, :] = c[4 + by:8 + by]
-            pack_ref[row + 4:row + 8, :] = c[:4]
-
-
-def close_kernel(k, g_ref, own_ref, x_ref, out_ref, b1, m1, e1, half1, b2, u2, v2, v, m):
+            row = k.to7 + by * (i - bx)
+            to4_ref[row:row + by, :] = c[4:4 + by]
+        places = [(to3_ref, k.c2 + 8 * i)] if i < k.yf_n else []
+        if bx <= i < k.yf_n:
+            places += [(ref, k.c2 + 8 * (i - bx)) for ref in (to4_ref, to7_ref)]
+        for ref, row in places:
+            ref[row:row + 4, :] = c[4 + by:8 + by]
+            ref[row + 4:row + 8, :] = c[:4]
+
+
+def share_kernel(k, own_ref, got3_ref, got4_ref, got7_ref, out_ref):
+    c2 = k.c2
+    for n, ref in enumerate((own_ref, got3_ref, got4_ref, got7_ref)):
+        out_ref[n * c2:(n + 1) * c2, :] = ref[:c2, :]
+    out_ref[4 * c2:4 * c2 + 8 * k.yf_n, :] = own_ref[c2:, :]
+    out_ref[4 * c2 + 8 * k.yf_n:, :] = got4_ref[c2:c2 + 24, :]
+
+
+def close_kernel(k, mine_ref, got_ref, got3_ref, got4_ref, got7_ref, own_ref, out_ref,
+                 parts, b1, m1, e1, half1, b2, u2, v2, v, m):
     ix, iy, iz = place()
-    bx, by, bz, n = k.bx, k.by, k.bz, k.core
+    bx, by, bz, n, c2 = k.bx, k.by, k.bz, k.core, k.c2
+    for slot, near, far in ((0, mine_ref, 0), (3, mine_ref, 1), (1, got_ref, 0), (2, got_ref, 1)):
+        parts[slot] = near[far * c2:(far + 1) * c2, :]
+        parts[4 + slot] = near[(2 + far) * c2:(3 + far) * c2, :]
     zero(b1)
-    for i in range(2):
+    for side in range(2):
         for j in range(k.gy):
             at = j * (by // 2)
+            slot = 4 * side + (iy ^ j)
             for q in range(k.c2_n):
-                x = q if i == 0 else k.nx1 - 1 - q
-                part = g_ref[i * k.gy + j, q * k.c2_rows:(q + 1) * k.c2_rows, :]
-                b1[x + 1, at:at + k.c2_rows, :] += part
+                x = q if side == 0 else k.nx1 - 1 - q
+                b1[x + 1, at:at + k.c2_rows, :] += parts[slot, q * k.c2_rows:(q + 1) * k.c2_rows, :]
     coarse_plane(k, iz, b1, m1, e1, half1, b2, u2, v2)
     mask = halves_mask(k, iy, iz)
     for s in (v, m):
         zero_rim(s)
-    prolong_halves(k, ix, iy, e1, bx // 2 + 1, v)
+    prolong_halves(k, iy, e1, bx // 2 + 1, v)
     for i in range(bx + 2):
         for h in range(2):
             v[i + 1, h, 1:1 + n, :] = v[i + 1, h, 1:1 + n, :] * mask[h]
@@ -932,22 +953,29 @@
         c = mix_halves(v, i)
         for h in range(2):
             m[i + 1, h, 1:1 + n, :] = c[h] * mask[h]
-    low_ok, high_ok = flag(iy > 0), flag(iy < k.gy - 1)
-    y_low, y_high = jnp.maximum(iy - 1, 0), jnp.minimum(iy + 1, k.gy - 1)
+    odd = lax.rem(iy, 2) == 1
+    chip_ok = flag((iy > 0) & (iy < k.gy - 1))
+
+    def frames(core, core_at, chip, chip_at):
+        row = lambda ref, at, r: ref[at + r:at + r + 4, :]
+        low = jnp.where(odd, row(core, core_at, 0), row(chip, chip_at, 0) * chip_ok)
+        high = jnp.where(odd, row(chip, chip_at, 4) * chip_ok, row(core, core_at, 4))
+        return low, high
+
     for i in range(bx):
         c = mix_halves(m, i, 1)[0][4:4 + by] + own_ref[i]
         if i >= bx - 4:
-            c = c + x_ref[bx - 1 - i]
+            row = k.to7 + by * (bx - 1 - i)
+            c = c + got4_ref[row:row + by, :]
         at = from_end(ix, i, bx)
         out_ref[at] = c
-        low, high = 0.0, 0.0
-        for who, plane in ((ix, i), (1 - ix, 2 * bx - 1 - i)):
-            if plane < k.yf_n:
-                row = k.yf_at + 8 * plane
-                low = low + g_ref[who * k.gy + y_low, row:row + 4, :]
-                high = high + g_ref[who * k.gy + y_high, row + 4:row + 8, :]
-        out_ref[at, :4, :] += low * low_ok
-        out_ref[at, by - 4:, :] += high * high_ok
+        low, high = frames(got_ref, 4 * c2 + 8 * i, got3_ref, c2 + 8 * i)
+        if i >= bx - 3:
+            row = 8 * (bx - 1 - i)
+            low2, high2 = frames(got_ref, 4 * c2 + 8 * k.yf_n + row, got7_ref, c2 + row)
+            low, high = low + low2, high + high2
+        out_ref[at, :4, :] += low
+        out_ref[at, by - 4:, :] += high
 
 
 def mirrored(k, pressure, wind):
@@ -964,17 +992,18 @@
         (gathered, wind), 1 << 22)
     low = lax.ppermute(right, "gz", chain(k.gz, 1))
     high = lax.ppermute(left, "gz", chain(k.gz, -1))
-    pack, frame, own = call(
+    to3, to4, to7, own = call(
         functools.partial(solve_kernel, k),
-        [(k.pack, bz), (4, by, bz), (bx, by, bz)],
+        [(k.to3, bz), (k.to4, bz), (k.to7, bz), (bx, by, bz)],
         level1 + level2 + [fine(bx + 5)] * 3 + [(3, bx + 3, 2, k.core, bz), (3,) + fine(bx + 1), (2, k.c2_n, 16, bz)],
         (c1, window, wind, low, high), 1 << 24)
-    frame = lax.ppermute(frame, "gx", pairs(k.gx)[0])
-    gathered = lax.all_gather(pack, PLANE)
+    crossed = lambda v, d: lax.ppermute(v, PLANE, [(i, i ^ d) for i in range(k.gx * k.gy)])
+    got3, got4, got7 = crossed(to3, 3), crossed(to4, 4), crossed(to7, 7)
+    (mine,) = call(functools.partial(share_kernel, k), [(k.to1, bz)], [], (to3, got3, got4, got7), 1 << 12)
     (result,) = call(
         functools.partial(close_kernel, k), [(bx, by, bz)],
-        level1 + level2 + [fine(bx + 2)] * 2,
-        (gathered, own, frame), 1 << 23)
+        [(8, k.c2, bz)] + level1 + level2 + [fine(bx + 2)] * 2,
+        (mine, crossed(mine, 1), got3, got4, got7, own), 1 << 23)
     return result
 
 
@@ -982,7 +1011,7 @@
     gx, gy, gz = (mesh.shape[a] for a in ("gx", "gy", "gz"))
 
     def run(pressure, wind):
-        form, sizes = (mirrored, Mirror) if gx == 2 else (general, Sizes)
+        form, sizes = (mirrored, Mirror) if (gx, gy) == (2, 4) else (general, Sizes)
         return form(sizes(gx, gy, gz, *pressure.shape), pressure, wind)
 
     in_specs = (P("gx", "gy", "gz"), P(None, "gx", "gy", "gz"))

time: 43.4 us -> 40.3 us (0.929)
  blocking collectives: 22.4 us -> 12.3 us
  waiting for transfers between devices: 7.39 us -> 11.9 us
  starting transfers between devices: 5.99 us -> 8.39 us
    all_gather x1 -> x0, blocking collectives: 10 us -> none  [mirrored(): gathered = lax.all_gather(pack, PLANE)]
    ppermute x1 -> x4, waiting for transfers between devices: 0.01 us -> 4.49 us  [mirrored(): lax.ppermute(v, PLANE, [(i, i ^ d) for i in range(k.gx * k.gy)])]
    ppermute x1 -> x4, starting transfers between devices: 1.21 us -> 3.6 us  [mirrored(): lax.ppermute(v, PLANE, [(i, i ^ d) for i in range(k.gx * k.gy)])]
    pallas_call x3 -> x4, Pallas kernels: 7.39 us -> 7.39 us  [call(): pl.pallas_call(kernel, out_shape=[f32(s) for s in outs], scratch_shapes=[...]
  transfers between devices with their start and end apart: 3 -> 6, of which waited for: 2 -> 4; matrix products, arithmetic and copies ran while one was open for 0% -> 0% of each run, Pallas kernels for 0% -> 0%
where the time goes in v5:
time: 40.3 us; the launch traced here: 40.1 us
  blocking collectives  12.3 us (31%)
  waiting for transfers between devices  11.9 us (30%)
  starting transfers between devices  8.39 us (21%)
  Pallas kernels  7.39 us (18%)
    all_gather x1, blocking collectives, mirrored(): gathered = lax.all_gather(pressure, PLANE)  12.3 us
    pallas_call x4, Pallas kernels, call(): pl.pallas_call(kernel, out_shape=[f32(s) for s in outs], scratch_shapes=[...  7.39 us
    ppermute x4, waiting for transfers between devices, mirrored(): lax.ppermute(v, PLANE, [(i, i ^ d) for i in range(k.gx * k.gy)])  4.49 us
    ppermute x1, waiting for transfers between devices, mirrored(): high = lax.ppermute(left, 'gz', chain(k.gz, -1))  4.12 us
    ppermute x4, starting transfers between devices, mirrored(): lax.ppermute(v, PLANE, [(i, i ^ d) for i in range(k.gx * k.gy)])  3.6 us
    ppermute x1, starting transfers between devices, mirrored(): low = lax.ppermute(right, 'gz', chain(k.gz, 1))  3.49 us
    ppermute x1, waiting for transfers between devices, mirrored(): low = lax.ppermute(right, 'gz', chain(k.gz, 1))  3.26 us
    ppermute x1, starting transfers between devices, mirrored(): high = lax.ppermute(left, 'gz', chain(k.gz, -1))  1.29 us
  transfers between devices with their start and end apart: 6, of which 4 were waited for; matrix products, arithmetic and copies ran while one was open for 0% of the time, Pallas kernels for 0%

profile of v5, /device:TPU:0, one launch (start us, length us, event | category | flops | bytes accessed | tf_op | source)
XLA Modules:
  0.0 40.1 jit_solution(4652551672183151050)
XLA Ops:
  0.0 0.0 copy-start
  0.0 12.3 %all-gather = f32[96,16,128]{2,1,0:T(8,128)S(1)} all-gather(f32[12,16,128]{2,1,0:T(8,128)} %param.2), channel_id=2, replica_groups=mesh['gx'=2,'gy'=4,'gz'=4] {'gx','gy'}, dimensions={0}, use_global_device_ids=true | all-gather | bytes 884736 | tf_op jit(solution)/shard_map/all_gather | solution.py:987
  12.4 0.0 copy-done
  12.4 1.6 %shard_map.28 = (f32[12,32,128]{2,1,0:T(8,128)S(1)}, f32[17,26,128]{2,1,0:T(8,128)S(1)}, f32[370,128]{1,0:T(8,128)S(1)}, f32[370,128]{1,0:T(8,128)S(1)}) custom-call(f32[8,12,16,128]{3,2,1,0:T(8,128)S(1)} %bitcast.1, f32[3,12,16,128]{3,2,1,0:T(8,128)S(1)} %copy-done), custom_call_target="tpu_custom_call" | custom-call | flops 4194304 | bytes 1048576 | tf_op jit(solution)/shard_map/pallas_call | solution.py:496
  14.0 3.5 %collective-permute-start = (f32[370,128]{1,0:T(8,128)S(1)}, f32[370,128]{1,0:T(8,128)S(1)}, u32[]{:S(2)}, u32[]{:S(2)}) collective-permute-start(f32[370,128]{1,0:T(8,128)S(1)} %get-tuple-element.15), channel_id=1, source_target_pairs={{0,1},{1,2},{2,3},{4,5},{5,6},{6,7},{8,9},{9,10},{10,11},{12,13},{... | collective-permute-start | bytes 568328 | tf_op jit(solution)/shard_map/ppermute | solution.py:993
  17.5 1.3 %collective-permute-start.1 = (f32[370,128]{1,0:T(8,128)S(1)}, f32[370,128]{1,0:T(8,128)S(1)}, u32[]{:S(2)}, u32[]{:S(2)}) collective-permute-start(f32[370,128]{1,0:T(8,128)S(1)} %get-tuple-element.16), channel_id=1, source_target_pairs={{1,0},{2,1},{3,2},{5,4},{6,5},{7,6},{9,8},{10,9},{11,10},{13,12},{... | collective-permute-start | bytes 568328 | tf_op jit(solution)/shard_map/ppermute | solution.py:994
  18.8 3.3 %collective-permute-done.low_ref = f32[370,128]{1,0:T(8,128)S(1)} collective-permute-done((f32[370,128]{1,0:T(8,128)S(1)}, f32[370,128]{1,0:T(8,128)S(1)}, u32[]{:S(2)}, u32[]{:S(2)}) %collective-permute-start) | collective-permute-done | bytes 189472 | tf_op jit(solution)/shard_map/ppermute | solution.py:993
  22.0 4.1 %collective-permute-done.1.high_ref = f32[370,128]{1,0:T(8,128)S(1)} collective-permute-done((f32[370,128]{1,0:T(8,128)S(1)}, f32[370,128]{1,0:T(8,128)S(1)}, u32[]{:S(2)}, u32[]{:S(2)}) %collective-permute-start.1) | collective-permute-done | bytes 189472 | tf_op jit(solution)/shard_map/ppermute | solution.py:994
  26.2 3.4 %shard_map.29 = (f32[216,128]{1,0:T(8,128)S(1)}, f32[184,128]{1,0:T(8,128)S(1)}, f32[120,128]{1,0:T(8,128)S(1)}, f32[12,16,128]{2,1,0:T(8,128)S(1)}) custom-call(f32[12,32,128]{2,1,0:T(8,128)S(1)} %get-tuple-element.13.c1_ref, f32[17,26,128]{2,1,0:T(8,128)S(1)} %get-tuple-element.14.win_ref, f32[3,12,16,128]{3,2,1,0:T(8,128)S(1)} %copy-done, ...), custom_call_target="tpu_custom_call" | custom-call | flops 16777216 | bytes 1048576 | tf_op jit(solution)/shard_map/pallas_call | solution.py:496
  29.6 0.1 collective-permute-start.2
  29.6 1.2 %collective-permute-start.3 = (f32[184,128]{1,0:T(8,128)S(1)}, f32[184,128]{1,0:T(8,128)S(1)}, u32[]{:S(2)}, u32[]{:S(2)}) collective-permute-start(f32[184,128]{1,0:T(8,128)S(1)} %get-tuple-element.18), channel_id=1, source_target_pairs={{0,16},{4,20},{8,24},{12,28},{16,0},{20,4},{24,8},{28,12},{1,17},{... | collective-permute-start | bytes 282632 | tf_op jit(solution)/shard_map/ppermute | solution.py:1000
  30.9 1.7 %collective-permute-start.4 = (f32[120,128]{1,0:T(8,128)S(1)}, f32[120,128]{1,0:T(8,128)S(1)}, u32[]{:S(2)}, u32[]{:S(2)}) collective-permute-start(f32[120,128]{1,0:T(8,128)S(1)} %get-tuple-element.19), channel_id=1, source_target_pairs={{0,28},{4,24},{8,20},{12,16},{16,12},{20,8},{24,4},{28,0},{1,29},{... | collective-permute-start | bytes 184328 | tf_op jit(solution)/shard_map/ppermute | solution.py:1000
  32.6 3.3 %collective-permute-done.4.got7_ref = f32[120,128]{1,0:T(8,128)S(1)} collective-permute-done((f32[120,128]{1,0:T(8,128)S(1)}, f32[120,128]{1,0:T(8,128)S(1)}, u32[]{:S(2)}, u32[]{:S(2)}) %collective-permute-start.4) | collective-permute-done | bytes 61472 | tf_op jit(solution)/shard_map/ppermute | solution.py:1000
  35.9 0.0 collective-permute-done.3.got4_ref
  35.9 0.0 collective-permute-done.2.got3_ref
  35.9 0.6 %collective-permute-start.5 = (f32[528,128]{1,0:T(8,128)S(1)}, f32[528,128]{1,0:T(8,128)S(1)}, u32[]{:S(2)}, u32[]{:S(2)}) collective-permute-start(f32[528,128]{1,0:T(8,128)S(1)} %shard_map.30.mine_ref), channel_id=1, source_target_pairs={{0,4},{4,0},{8,12},{12,8},{16,20},{20,16},{24,28},{28,24},{1,5},{5... | collective-permute-start | bytes 811016 | tf_op jit(solution)/shard_map/ppermute | solution.py:1000
  36.5 1.2 %collective-permute-done.5.got_ref = f32[528,128]{1,0:T(8,128)S(1)} collective-permute-done((f32[528,128]{1,0:T(8,128)S(1)}, f32[528,128]{1,0:T(8,128)S(1)}, u32[]{:S(2)}, u32[]{:S(2)}) %collective-permute-start.5) | collective-permute-done | bytes 270368 | tf_op jit(solution)/shard_map/ppermute | solution.py:1000
  37.7 2.4 %shard_map.31 = f32[12,16,128]{2,1,0:T(8,128)} custom-call(f32[528,128]{1,0:T(8,128)S(1)} %shard_map.30.mine_ref, f32[528,128]{1,0:T(8,128)S(1)} %collective-permute-done.5.got_ref, f32[216,128]{1,0:T(8,128)S(1)} %collective-permute-done.2.got3_ref, f32[184,128]{1,0:T(8,128)S(1)} %collective-permute-done.3.got4_ref, ...), custom_call_target="tpu_custom_call" | custom-call | flops 8388608 | bytes 1048576 | tf_op jit(solution)/shard_map/pallas_call | solution.py:496
  (1 shorter events, 0.0 us)
Async XLA Ops:
  0.0 12.4 %copy-start = (f32[3,12,16,128]{3,2,1,0:T(8,128)S(1)}, f32[3,12,16,128]{3,2,1,0:T(8,128)}, u32[]{:S(2)}) copy-start(f32[3,12,16,128]{3,2,1,0:T(8,128)} %w_ref.3) | copy-start | bytes 884740
  14.0 8.1 %collective-permute-start = (f32[370,128]{1,0:T(8,128)S(1)}, f32[370,128]{1,0:T(8,128)S(1)}, u32[]{:S(2)}, u32[]{:S(2)}) collective-permute-start(f32[370,128]{1,0:T(8,128)S(1)} %get-tuple-element.15), channel_id=1, source_target_pairs={{0,1},{1,2},{2,3},{4,5},{5,6},{6,7},{8,9},{9,10},{10,11},{12,13},{... | collective-permute-start | bytes 568328 | tf_op jit(solution)/shard_map/ppermute | solution.py:993
  17.5 8.7 %collective-permute-start.1 = (f32[370,128]{1,0:T(8,128)S(1)}, f32[370,128]{1,0:T(8,128)S(1)}, u32[]{:S(2)}, u32[]{:S(2)}) collective-permute-start(f32[370,128]{1,0:T(8,128)S(1)} %get-tuple-element.16), channel_id=1, source_target_pairs={{1,0},{2,1},{3,2},{5,4},{6,5},{7,6},{9,8},{10,9},{11,10},{13,12},{... | collective-permute-start | bytes 568328 | tf_op jit(solution)/shard_map/ppermute | solution.py:994
  29.6 6.3 %collective-permute-start.2 = (f32[216,128]{1,0:T(8,128)S(1)}, f32[216,128]{1,0:T(8,128)S(1)}, u32[]{:S(2)}, u32[]{:S(2)}) collective-permute-start(f32[216,128]{1,0:T(8,128)S(1)} %get-tuple-element.17.own_ref), channel_id=1, source_target_pairs={{0,12},{4,8},{8,4},{12,0},{16,28},{20,24},{24,20},{28,16},{1,13},{... | collective-permute-start | bytes 331784 | tf_op jit(solution)/shard_map/ppermute | solution.py:1000
  29.6 6.2 %collective-permute-start.3 = (f32[184,128]{1,0:T(8,128)S(1)}, f32[184,128]{1,0:T(8,128)S(1)}, u32[]{:S(2)}, u32[]{:S(2)}) collective-permute-start(f32[184,128]{1,0:T(8,128)S(1)} %get-tuple-element.18), channel_id=1, source_target_pairs={{0,16},{4,20},{8,24},{12,28},{16,0},{20,4},{24,8},{28,12},{1,17},{... | collective-permute-start | bytes 282632 | tf_op jit(solution)/shard_map/ppermute | solution.py:1000
  30.9 5.0 %collective-permute-start.4 = (f32[120,128]{1,0:T(8,128)S(1)}, f32[120,128]{1,0:T(8,128)S(1)}, u32[]{:S(2)}, u32[]{:S(2)}) collective-permute-start(f32[120,128]{1,0:T(8,128)S(1)} %get-tuple-element.19), channel_id=1, source_target_pairs={{0,28},{4,24},{8,20},{12,16},{16,12},{20,8},{24,4},{28,0},{1,29},{... | collective-permute-start | bytes 184328 | tf_op jit(solution)/shard_map/ppermute | solution.py:1000
  35.9 1.8 %collective-permute-start.5 = (f32[528,128]{1,0:T(8,128)S(1)}, f32[528,128]{1,0:T(8,128)S(1)}, u32[]{:S(2)}, u32[]{:S(2)}) collective-permute-start(f32[528,128]{1,0:T(8,128)S(1)} %shard_map.30.mine_ref), channel_id=1, source_target_pairs={{0,4},{4,0},{8,12},{12,8},{16,20},{20,16},{24,28},{28,24},{1,5},{5... | collective-permute-start | bytes 811016 | tf_op jit(solution)/shard_map/ppermute | solution.py:1000

commit v6 on v5

--- a/solution.py
+++ b/solution.py
@@ -739,7 +739,7 @@
     return lane_roll(ref[at:at + rows, :], to - k.part * (i % 4))
 
 
-def plane_kernel(k, g_ref, w_ref, c1_ref, win_ref, right_ref, left_ref, p, m, q, half_ref):
+def plane_kernel(k, g_ref, w_ref, c1_ref, win_ref, first_ref, second_ref, p, m, q, half_ref):
     ix, iy, iz = place()
     bx, by, bz, nx, ny, part = k.bx, k.by, k.bz, k.nx, k.ny, k.part
     p[0] = jnp.zeros(p.shape[1:], jnp.float32)
@@ -784,27 +784,35 @@
         s = half_ref[j, pl.ds(0, half_rows, stride=2), :] + half_ref[j, pl.ds(1, half_rows, stride=2), :]
         c1_ref[j] = exact_dot(s, own) + exact_dot(W * t, rim)
 
-    def pack(ref, base, rows, n, load, from_lane):
+    even = lax.rem(iz, 2) == 0
+
+    def pack(base, rows, n, load, right_lane, left_lane):
         lane = iota((rows, bz), 1)
         for group in range(-(-n // 4)):
-            total = jnp.zeros((rows, bz), jnp.float32)
+            right, left = jnp.zeros((rows, bz), jnp.float32), jnp.zeros((rows, bz), jnp.float32)
             for r in range(min(4, n - 4 * group)):
-                moved = lane_roll(load(4 * group + r), part * r - from_lane)
-                total = jnp.where((lane >= part * r) & (lane < part * (r + 1)), moved, total)
-            ref[base + group * rows:base + (group + 1) * rows, :] = total
+                here = (lane >= part * r) & (lane < part * (r + 1))
+                c = load(4 * group + r)
+                right = jnp.where(here, lane_roll(c, part * r - right_lane), right)
+                left = jnp.where(here, lane_roll(c, part * r - left_lane), left)
+            at = slice(base + group * rows, base + (group + 1) * rows)
+            first_ref[at, :] = jnp.where(even, right, left)
+            second_ref[at, :] = jnp.where(even, left, right)
 
     for i in range(k.fine_n):
         win_ref[i] = p[i + 1, pl.ds(pl.multiple_of(iy * by, 8), k.rows), :]
-    for ref, lane1, lane0 in ((right_ref, part + 1, 3 * part), (left_ref, bz - 1, 0)):
-        pack(ref, 0, k.ny1, k.nx1, lambda i: c1_ref[i], lane1)
-        pack(ref, k.at_fine, k.rows, k.fine_n, lambda i: win_ref[i], lane0)
-        pack(ref, k.at_wind, by, 3 * bx, lambda i: w_ref[i // bx, from_end(ix, i % bx, bx)], lane0)
-
-
-def solve_kernel(k, c1_ref, win_ref, w_ref, low_ref, high_ref, to3_ref, to4_ref, to7_ref, own_ref,
-                 b1, m1, e1, half1, b2, u2, v2, b, m, v, vel, flux, half_ref):
+    pack(0, k.ny1, k.nx1, lambda i: c1_ref[i], part + 1, bz - 1)
+    pack(k.at_fine, k.rows, k.fine_n, lambda i: win_ref[i], 3 * part, 0)
+    pack(k.at_wind, by, 3 * bx, lambda i: w_ref[i // bx, from_end(ix, i % bx, bx)], 3 * part, 0)
+
+
+def solve_kernel(k, c1_ref, win_ref, w_ref, first_ref, second_ref, to3_ref, to4_ref, to7_ref, own_ref,
+                 low_ref, high_ref, b1, m1, e1, half1, b2, u2, v2, b, m, v, vel, flux, half_ref):
     ix, iy, iz = place()
     bx, by, bz, part, n = k.bx, k.by, k.bz, k.part, k.core
+    even = lax.rem(iz, 2) == 0
+    low_ref[...] = jnp.where(even, second_ref[...], first_ref[...])
+    high_ref[...] = jnp.where(even, first_ref[...], second_ref[...])
     lane = iota((k.ny1, bz), 1)
     for s in (b1,):
         for i in (0, k.nx1 + 1):
@@ -985,18 +993,17 @@
     level1 = [(n1 + 2, k.rows1, bz)] * 3
     level2 = [(n2, k.ny1, bz), (n2, k.ny1 // 2, bz)] + [(n2 + 2, k.ny1 // 2 + 2, bz)] * 2
     gathered = lax.all_gather(pressure, PLANE)
-    c1, window, right, left = call(
+    c1, window, first, second = call(
         functools.partial(plane_kernel, k),
         [(n1, k.ny1, bz), (k.fine_n, k.rows, bz), (k.slab_rows, bz), (k.slab_rows, bz)],
         [(k.nx + 2, -(-(k.ny + 2 * FR) // 8) * 8, bz), (k.nx + 2, k.ny + 2, bz), (k.nx, k.ny, bz), (n1, k.ny, bz)],
         (gathered, wind), 1 << 22)
-    low = lax.ppermute(right, "gz", chain(k.gz, 1))
-    high = lax.ppermute(left, "gz", chain(k.gz, -1))
+    first, second = (lax.ppermute(v, "gz", p) for v, p in zip((first, second), pairs(k.gz)))
     to3, to4, to7, own = call(
         functools.partial(solve_kernel, k),
         [(k.to3, bz), (k.to4, bz), (k.to7, bz), (bx, by, bz)],
-        level1 + level2 + [fine(bx + 5)] * 3 + [(3, bx + 3, 2, k.core, bz), (3,) + fine(bx + 1), (2, k.c2_n, 16, bz)],
-        (c1, window, wind, low, high), 1 << 24)
+        [(k.slab_rows, bz)] * 2 + level1 + level2 + [fine(bx + 5)] * 3 + [(3, bx + 3, 2, k.core, bz), (3,) + fine(bx + 1), (2, k.c2_n, 16, bz)],
+        (c1, window, wind, first, second), 1 << 24)
     crossed = lambda v, d: lax.ppermute(v, PLANE, [(i, i ^ d) for i in range(k.gx * k.gy)])
     got3, got4, got7 = crossed(to3, 3), crossed(to4, 4), crossed(to7, 7)
     (mine,) = call(functools.partial(share_kernel, k), [(k.to1, bz)], [], (to3, got3, got4, got7), 1 << 12)

time: 40.3 us -> 37.7 us (0.935)
  the two profiles are of different devices: /device:TPU:0 before, /device:TPU:9 now
where the time goes in v6:
time: 37.7 us; the launch traced here: 37.6 us
  blocking collectives  11.4 us (30%)
  waiting for transfers between devices  10.3 us (27%)
  starting transfers between devices  8.37 us (22%)
  Pallas kernels  7.42 us (20%)
    all_gather x1, blocking collectives, mirrored(): gathered = lax.all_gather(pressure, PLANE)  11.4 us
    pallas_call x4, Pallas kernels, call(): pl.pallas_call(kernel, out_shape=[f32(s) for s in outs], scratch_shapes=[...  7.42 us
    ppermute x4, waiting for transfers between devices, mirrored(): lax.ppermute(v, PLANE, [(i, i ^ d) for i in range(k.gx * k.gy)])  5.6 us
    ppermute x2, waiting for transfers between devices, mirrored(): lax.ppermute(v, 'gz', p)  4.74 us
    ppermute x2, starting transfers between devices, mirrored(): lax.ppermute(v, 'gz', p)  4.55 us
    ppermute x4, starting transfers between devices, mirrored(): lax.ppermute(v, PLANE, [(i, i ^ d) for i in range(k.gx * k.gy)])  3.82 us
  transfers between devices with their start and end apart: 6, of which 5 were waited for; matrix products, arithmetic and copies ran while one was open for 0% of the time, Pallas kernels for 0%

profile of v6, /device:TPU:9, one launch (start us, length us, event | category | flops | bytes accessed | tf_op | source)
XLA Modules:
  0.0 37.6 jit_solution(1867942738502219416)
XLA Ops:
  0.0 0.0 copy-start
  0.0 11.4 %all-gather = f32[96,16,128]{2,1,0:T(8,128)S(1)} all-gather(f32[12,16,128]{2,1,0:T(8,128)} %param.2), channel_id=2, replica_groups=mesh['gx'=2,'gy'=4,'gz'=4] {'gx','gy'}, dimensions={0}, use_global_device_ids=true | all-gather | bytes 884736 | tf_op jit(solution)/shard_map/all_gather | solution.py:995
  11.4 0.0 copy-done
  11.4 1.6 %shard_map.28 = (f32[12,32,128]{2,1,0:T(8,128)S(1)}, f32[17,26,128]{2,1,0:T(8,128)S(1)}, f32[370,128]{1,0:T(8,128)S(1)}, f32[370,128]{1,0:T(8,128)S(1)}) custom-call(f32[8,12,16,128]{3,2,1,0:T(8,128)S(1)} %bitcast.1, f32[3,12,16,128]{3,2,1,0:T(8,128)S(1)} %copy-done), custom_call_target="tpu_custom_call" | custom-call | flops 4194304 | bytes 1048576 | tf_op jit(solution)/shard_map/pallas_call | solution.py:496
  13.0 0.2 collective-permute-start
  13.2 4.3 %collective-permute-start.1 = (f32[370,128]{1,0:T(8,128)S(1)}, f32[370,128]{1,0:T(8,128)S(1)}, u32[]{:S(2)}, u32[]{:S(2)}) collective-permute-start(f32[370,128]{1,0:T(8,128)S(1)} %get-tuple-element.16), channel_id=1, source_target_pairs={{1,2},{2,1},{5,6},{6,5},{9,10},{10,9},{13,14},{14,13},{17,18},{18,... | collective-permute-start | bytes 568328 | tf_op jit(solution)/shard_map/ppermute | solution.py:1001
  17.5 1.7 %collective-permute-done.first_ref = f32[370,128]{1,0:T(8,128)S(1)} collective-permute-done((f32[370,128]{1,0:T(8,128)S(1)}, f32[370,128]{1,0:T(8,128)S(1)}, u32[]{:S(2)}, u32[]{:S(2)}) %collective-permute-start) | collective-permute-done | bytes 189472 | tf_op jit(solution)/shard_map/ppermute | solution.py:1001
  19.3 3.0 %collective-permute-done.1.second_ref = f32[370,128]{1,0:T(8,128)S(1)} collective-permute-done((f32[370,128]{1,0:T(8,128)S(1)}, f32[370,128]{1,0:T(8,128)S(1)}, u32[]{:S(2)}, u32[]{:S(2)}) %collective-permute-start.1) | collective-permute-done | bytes 189472 | tf_op jit(solution)/shard_map/ppermute | solution.py:1001
  22.3 3.5 %shard_map.29 = (f32[216,128]{1,0:T(8,128)S(1)}, f32[184,128]{1,0:T(8,128)S(1)}, f32[120,128]{1,0:T(8,128)S(1)}, f32[12,16,128]{2,1,0:T(8,128)S(1)}) custom-call(f32[12,32,128]{2,1,0:T(8,128)S(1)} %get-tuple-element.13.c1_ref, f32[17,26,128]{2,1,0:T(8,128)S(1)} %get-tuple-element.14.win_ref, f32[3,12,16,128]{3,2,1,0:T(8,128)S(1)} %copy-done, ...), custom_call_target="tpu_custom_call" | custom-call | flops 16777216 | bytes 1048576 | tf_op jit(solution)/shard_map/pallas_call | solution.py:496
  25.8 1.8 %collective-permute-start.2 = (f32[216,128]{1,0:T(8,128)S(1)}, f32[216,128]{1,0:T(8,128)S(1)}, u32[]{:S(2)}, u32[]{:S(2)}) collective-permute-start(f32[216,128]{1,0:T(8,128)S(1)} %get-tuple-element.17.own_ref), channel_id=1, source_target_pairs={{0,12},{4,8},{8,4},{12,0},{16,28},{20,24},{24,20},{28,16},{1,13},{... | collective-permute-start | bytes 331784 | tf_op jit(solution)/shard_map/ppermute | solution.py:1007
  27.6 0.6 %collective-permute-start.3 = (f32[184,128]{1,0:T(8,128)S(1)}, f32[184,128]{1,0:T(8,128)S(1)}, u32[]{:S(2)}, u32[]{:S(2)}) collective-permute-start(f32[184,128]{1,0:T(8,128)S(1)} %get-tuple-element.18), channel_id=1, source_target_pairs={{0,16},{4,20},{8,24},{12,28},{16,0},{20,4},{24,8},{28,12},{1,17},{... | collective-permute-start | bytes 282632 | tf_op jit(solution)/shard_map/ppermute | solution.py:1007
  28.2 0.9 %collective-permute-start.4 = (f32[120,128]{1,0:T(8,128)S(1)}, f32[120,128]{1,0:T(8,128)S(1)}, u32[]{:S(2)}, u32[]{:S(2)}) collective-permute-start(f32[120,128]{1,0:T(8,128)S(1)} %get-tuple-element.19), channel_id=1, source_target_pairs={{0,28},{4,24},{8,20},{12,16},{16,12},{20,8},{24,4},{28,0},{1,29},{... | collective-permute-start | bytes 184328 | tf_op jit(solution)/shard_map/ppermute | solution.py:1007
  29.1 4.1 %collective-permute-done.4.got7_ref = f32[120,128]{1,0:T(8,128)S(1)} collective-permute-done((f32[120,128]{1,0:T(8,128)S(1)}, f32[120,128]{1,0:T(8,128)S(1)}, u32[]{:S(2)}, u32[]{:S(2)}) %collective-permute-start.4) | collective-permute-done | bytes 61472 | tf_op jit(solution)/shard_map/ppermute | solution.py:1007
  33.2 0.4 collective-permute-done.3.got4_ref
  33.5 0.0 collective-permute-done.2.got3_ref
  33.6 0.5 %collective-permute-start.5 = (f32[528,128]{1,0:T(8,128)S(1)}, f32[528,128]{1,0:T(8,128)S(1)}, u32[]{:S(2)}, u32[]{:S(2)}) collective-permute-start(f32[528,128]{1,0:T(8,128)S(1)} %shard_map.30.mine_ref), channel_id=1, source_target_pairs={{0,4},{4,0},{8,12},{12,8},{16,20},{20,16},{24,28},{28,24},{1,5},{5... | collective-permute-start | bytes 811016 | tf_op jit(solution)/shard_map/ppermute | solution.py:1007
  34.0 1.2 %collective-permute-done.5.got_ref = f32[528,128]{1,0:T(8,128)S(1)} collective-permute-done((f32[528,128]{1,0:T(8,128)S(1)}, f32[528,128]{1,0:T(8,128)S(1)}, u32[]{:S(2)}, u32[]{:S(2)}) %collective-permute-start.5) | collective-permute-done | bytes 270368 | tf_op jit(solution)/shard_map/ppermute | solution.py:1007
  35.2 2.4 %shard_map.31 = f32[12,16,128]{2,1,0:T(8,128)} custom-call(f32[528,128]{1,0:T(8,128)S(1)} %shard_map.30.mine_ref, f32[528,128]{1,0:T(8,128)S(1)} %collective-permute-done.5.got_ref, f32[216,128]{1,0:T(8,128)S(1)} %collective-permute-done.2.got3_ref, f32[184,128]{1,0:T(8,128)S(1)} %collective-permute-done.3.got4_ref, ...), custom_call_target="tpu_custom_call" | custom-call | flops 8388608 | bytes 1048576 | tf_op jit(solution)/shard_map/pallas_call | solution.py:496
  (1 shorter events, 0.0 us)
Async XLA Ops:
  0.0 11.4 %copy-start = (f32[3,12,16,128]{3,2,1,0:T(8,128)S(1)}, f32[3,12,16,128]{3,2,1,0:T(8,128)}, u32[]{:S(2)}) copy-start(f32[3,12,16,128]{3,2,1,0:T(8,128)} %w_ref.3) | copy-start | bytes 884740
  13.0 6.3 %collective-permute-start = (f32[370,128]{1,0:T(8,128)S(1)}, f32[370,128]{1,0:T(8,128)S(1)}, u32[]{:S(2)}, u32[]{:S(2)}) collective-permute-start(f32[370,128]{1,0:T(8,128)S(1)} %get-tuple-element.15), channel_id=1, source_target_pairs={{0,1},{1,0},{2,3},{3,2},{4,5},{5,4},{6,7},{7,6},{8,9},{9,8},{10,11... | collective-permute-start | bytes 568328 | tf_op jit(solution)/shard_map/ppermute | solution.py:1001
  13.2 9.1 %collective-permute-start.1 = (f32[370,128]{1,0:T(8,128)S(1)}, f32[370,128]{1,0:T(8,128)S(1)}, u32[]{:S(2)}, u32[]{:S(2)}) collective-permute-start(f32[370,128]{1,0:T(8,128)S(1)} %get-tuple-element.16), channel_id=1, source_target_pairs={{1,2},{2,1},{5,6},{6,5},{9,10},{10,9},{13,14},{14,13},{17,18},{18,... | collective-permute-start | bytes 568328 | tf_op jit(solution)/shard_map/ppermute | solution.py:1001
  25.8 7.8 %collective-permute-start.2 = (f32[216,128]{1,0:T(8,128)S(1)}, f32[216,128]{1,0:T(8,128)S(1)}, u32[]{:S(2)}, u32[]{:S(2)}) collective-permute-start(f32[216,128]{1,0:T(8,128)S(1)} %get-tuple-element.17.own_ref), channel_id=1, source_target_pairs={{0,12},{4,8},{8,4},{12,0},{16,28},{20,24},{24,20},{28,16},{1,13},{... | collective-permute-start | bytes 331784 | tf_op jit(solution)/shard_map/ppermute | solution.py:1007
  27.6 6.0 %collective-permute-start.3 = (f32[184,128]{1,0:T(8,128)S(1)}, f32[184,128]{1,0:T(8,128)S(1)}, u32[]{:S(2)}, u32[]{:S(2)}) collective-permute-start(f32[184,128]{1,0:T(8,128)S(1)} %get-tuple-element.18), channel_id=1, source_target_pairs={{0,16},{4,20},{8,24},{12,28},{16,0},{20,4},{24,8},{28,12},{1,17},{... | collective-permute-start | bytes 282632 | tf_op jit(solution)/shard_map/ppermute | solution.py:1007
  28.2 5.0 %collective-permute-start.4 = (f32[120,128]{1,0:T(8,128)S(1)}, f32[120,128]{1,0:T(8,128)S(1)}, u32[]{:S(2)}, u32[]{:S(2)}) collective-permute-start(f32[120,128]{1,0:T(8,128)S(1)} %get-tuple-element.19), channel_id=1, source_target_pairs={{0,28},{4,24},{8,20},{12,16},{16,12},{20,8},{24,4},{28,0},{1,29},{... | collective-permute-start | bytes 184328 | tf_op jit(solution)/shard_map/ppermute | solution.py:1007
  33.6 1.6 %collective-permute-start.5 = (f32[528,128]{1,0:T(8,128)S(1)}, f32[528,128]{1,0:T(8,128)S(1)}, u32[]{:S(2)}, u32[]{:S(2)}) collective-permute-start(f32[528,128]{1,0:T(8,128)S(1)} %shard_map.30.mine_ref), channel_id=1, source_target_pairs={{0,4},{4,0},{8,12},{12,8},{16,20},{20,16},{24,28},{28,24},{1,5},{5... | collective-permute-start | bytes 811016 | tf_op jit(solution)/shard_map/ppermute | solution.py:1007

commit v7 on v6

--- a/solution.py
+++ b/solution.py
@@ -6,6 +6,7 @@
 from jax.experimental import pallas as pl
 from jax.experimental.pallas import tpu as pltpu
 from jax.sharding import PartitionSpec as P
+
 
 OMEGA = 0.8
 W = OMEGA / 6.0
@@ -283,7 +284,7 @@
 
 def assemble_edges(k, refs, b1, b, pad):
     g_ref, win_ref, got_a, got_b, w_ref, low_ref, high_ref = refs
-    ix, iy, iz = place()
+    ix, iy, _ = place()
     bx, by = k.bx, k.by
     overlap_add(k, g_ref, b1, k.c1_n, k.c1_rows, 2, k.c1_first)
     even = lax.rem(iy, 2) == 0
@@ -576,7 +577,9 @@
         (gathered, own, *got), 1 << 23)
     return result
 
+
 FR = 5
+TOP = 8
 CR = 2
 
 
@@ -592,8 +595,8 @@
         groups = lambda n: -(-n // 4)
         self.fine_n = bx + 5
         self.at_fine = groups(self.nx1) * self.ny1
-        self.at_wind = self.at_fine + groups(self.fine_n) * self.rows
-        self.slab_rows = self.at_wind + groups(3 * bx) * by
+        self.slab_rows = self.at_fine + groups(self.fine_n) * self.rows
+        self.wind_rows = groups(3 * bx) * by
         self.c2_n, self.c2_rows = bx // 2 + 2, by // 2 + 4
         self.c2 = self.c2_n * self.c2_rows
         self.yf_n = bx + 3
@@ -656,7 +659,7 @@
             s[i, h, n - 1:n, :] = jnp.zeros((1, s.shape[3]), jnp.float32)
 
 
-def mix1(k, s, i, n, at):
+def mix1(s, i, n, at):
     c = s[i + 1, at:at + n, :]
     near = (s[i, at:at + n, :] + s[i + 2, at:at + n, :]) + (s[i + 1, at + 1:at + n + 1, :] + s[i + 1, at - 1:at + n - 1, :])
     return (1.0 - OMEGA) * c + W * (near + (up(c, 1) + down(c, 1)))
@@ -683,13 +686,13 @@
     for i in range(n1):
         b1[i + 1, CR:CR + ny, :] = b1[i + 1, CR:CR + ny, :] * mask1
     for i in range(n1):
-        c = mix1(k, b1, i, ny, CR) * mask1
+        c = mix1(b1, i, ny, CR) * mask1
         m1[i + 1, CR:CR + ny, :] = c
         e1[i + 1, CR:CR + ny, :] = C1 * (b1[i + 1, CR:CR + ny, :] + c)
     row, column = iota((l1, l1), 0), iota((l1, l1), 1)
     linear = lambda x: (jnp.where(x < 3 * l1 // 4, x, x - l1) >> 1) + own2
     for j in range(n2):
-        half_ref[j] = mix1(k, m1, 2 * j, ny, CR) + mix1(k, m1, 2 * j + 1, ny, CR)
+        half_ref[j] = mix1(m1, 2 * j, ny, CR) + mix1(m1, 2 * j + 1, ny, CR)
     pairs_sum = [half_ref[j, pl.ds(0, ny2, stride=2), :] + half_ref[j, pl.ds(1, ny2, stride=2), :] for j in range(n2)]
     r2 = exact_dot(jnp.concatenate(pairs_sum, axis=0), matrix(linear(row) == column, 0.125))
     for j in range(n2):
@@ -699,7 +702,7 @@
     src, dst = u2, v2
     for _ in range(3):
         for j in range(n2):
-            dst[j + 1, 1:1 + ny2, :] = (mix1(k, src, j, ny2, 1) + b2[j]) * mask2
+            dst[j + 1, 1:1 + ny2, :] = (mix1(src, j, ny2, 1) + b2[j]) * mask2
         src, dst = dst, src
     stack = jnp.concatenate([src[j + 1, 1:1 + ny2, :] for j in range(n2)], axis=0)
     spread = exact_dot(stack, matrix(row == linear(column), 1.0))
@@ -713,7 +716,7 @@
             e1[2 * j + t + 1, CR:CR + ny, :] = e1[2 * j + t + 1, CR:CR + ny, :] + e
     for src, dst in ((e1, m1), (m1, e1)):
         for i in range(n1):
-            dst[i + 1, CR:CR + ny, :] = (mix1(k, src, i, ny, CR) + C1 * b1[i + 1, CR:CR + ny, :]) * mask1
+            dst[i + 1, CR:CR + ny, :] = (mix1(src, i, ny, CR) + C1 * b1[i + 1, CR:CR + ny, :]) * mask1
 
 
 def from_end(ix, i, count):
@@ -721,7 +724,7 @@
 
 
 def prolong_halves(k, iy, e1, n, v):
-    half, rows = k.bz // 2, k.core // 2
+    rows = k.core // 2
     first = pl.multiple_of(iy * (k.by // 2), 8)
     stack = jnp.concatenate([e1[j + 1, pl.ds(first, 16), :] for j in range(n)], axis=0)
     row, column = iota((k.bz, 2 * k.bz), 0), iota((k.bz, 2 * k.bz), 1)
@@ -739,7 +742,35 @@
     return lane_roll(ref[at:at + rows, :], to - k.part * (i % 4))
 
 
-def plane_kernel(k, g_ref, w_ref, c1_ref, win_ref, first_ref, second_ref, p, m, q, half_ref):
+def pack_slabs(k, iz, first_ref, second_ref, base, rows, n, load, right_lane, left_lane):
+    part, bz = k.part, k.bz
+    even = lax.rem(iz, 2) == 0
+    lane = iota((rows, bz), 1)
+    for group in range(-(-n // 4)):
+        right, left = jnp.zeros((rows, bz), jnp.float32), jnp.zeros((rows, bz), jnp.float32)
+        for r in range(min(4, n - 4 * group)):
+            here = (lane >= part * r) & (lane < part * (r + 1))
+            c = load(4 * group + r)
+            right = jnp.where(here, lane_roll(c, part * r - right_lane), right)
+            left = jnp.where(here, lane_roll(c, part * r - left_lane), left)
+        at = slice(base + group * rows, base + (group + 1) * rows)
+        first_ref[at, :] = jnp.where(even, right, left)
+        second_ref[at, :] = jnp.where(even, left, right)
+
+
+def wind_kernel(k, p_ref, w_ref, own_ref, first_ref, second_ref):
+    ix, _, iz = place()
+    own_ref[...] = p_ref[...]
+    pack_slabs(k, iz, first_ref, second_ref, 0, k.by, 3 * k.bx,
+               lambda i: w_ref[i // k.bx, from_end(ix, i % k.bx, k.bx)], 3 * k.part, 0)
+
+
+def join_kernel(a_ref, b_ref, c_ref, d_ref, out_ref):
+    for i, ref in enumerate((a_ref, b_ref, c_ref, d_ref)):
+        out_ref[i] = ref[...]
+
+
+def plane_kernel(k, mine_ref, theirs_ref, c1_ref, win_ref, first_ref, second_ref, p, m, q, half_ref, wide):
     ix, iy, iz = place()
     bx, by, bz, nx, ny, part = k.bx, k.by, k.bz, k.nx, k.ny, k.part
     p[0] = jnp.zeros(p.shape[1:], jnp.float32)
@@ -747,13 +778,15 @@
     m[0] = jnp.zeros(m.shape[1:], jnp.float32)
     m[nx + 1] = jnp.zeros(m.shape[1:], jnp.float32)
     for x in range(nx):
-        p[x + 1, :FR, :] = jnp.zeros((FR, bz), jnp.float32)
-        p[x + 1, FR + ny:, :] = jnp.zeros((p.shape[1] - FR - ny, bz), jnp.float32)
+        p[x + 1, :TOP, :] = jnp.zeros((TOP, bz), jnp.float32)
+        p[x + 1, TOP + ny:, :] = jnp.zeros((p.shape[1] - TOP - ny, bz), jnp.float32)
         m[x + 1, 0:1, :] = jnp.zeros((1, bz), jnp.float32)
         m[x + 1, ny + 1:, :] = jnp.zeros((m.shape[1] - ny - 1, bz), jnp.float32)
-        who = ix if x < bx else 1 - ix
-        for j in range(k.gy):
-            p[x + 1, FR + j * by:FR + (j + 1) * by, :] = g_ref[who * k.gy + j, from_end(ix, x % bx, bx)]
+    for side in range(2):
+        for other, ref, block in ((0, mine_ref, 0), (3, mine_ref, 1), (1, theirs_ref, 0), (2, theirs_ref, 1)):
+            at = pl.multiple_of(TOP + by * (iy ^ other), 8)
+            for x in range(bx):
+                p[side * bx + x + 1, pl.ds(at, by), :] = ref[2 * side + block, from_end(ix, x, bx)]
     lane = iota((ny, bz), 1)
     first, last = lane == 0, lane == bz - 1
     ends = jnp.where(first, flag(iz > 0), jnp.where(last, flag(iz < k.gz - 1), 0.0)) * (W * W)
@@ -765,7 +798,7 @@
         return c, four, (1.0 - OMEGA) * c + W * (four + along)
 
     for x in range(nx):
-        c, four, mixed = parts(p, x, FR)
+        c, four, mixed = parts(p, x, TOP)
         m[x + 1, 1:1 + ny, :] = mixed
         q[x] = (1.0 - OMEGA + W) * c + (mixed + W * four)
     row, column = iota((bz, bz), 0), iota((bz, bz), 1)
@@ -776,7 +809,7 @@
     for j in range(k.nx1):
         s = None
         for x in (2 * j, 2 * j + 1):
-            r = parts(m, x, 1)[2] + ends * p[x + 1, FR:FR + ny, :]
+            r = parts(m, x, 1)[2] + ends * p[x + 1, TOP:TOP + ny, :]
             s = r if s is None else s + r
         half_ref[j] = s
         t = (q[2 * j, pl.ds(0, half_rows, stride=2), :] + q[2 * j, pl.ds(1, half_rows, stride=2), :]
@@ -784,35 +817,23 @@
         s = half_ref[j, pl.ds(0, half_rows, stride=2), :] + half_ref[j, pl.ds(1, half_rows, stride=2), :]
         c1_ref[j] = exact_dot(s, own) + exact_dot(W * t, rim)
 
-    even = lax.rem(iz, 2) == 0
-
-    def pack(base, rows, n, load, right_lane, left_lane):
-        lane = iota((rows, bz), 1)
-        for group in range(-(-n // 4)):
-            right, left = jnp.zeros((rows, bz), jnp.float32), jnp.zeros((rows, bz), jnp.float32)
-            for r in range(min(4, n - 4 * group)):
-                here = (lane >= part * r) & (lane < part * (r + 1))
-                c = load(4 * group + r)
-                right = jnp.where(here, lane_roll(c, part * r - right_lane), right)
-                left = jnp.where(here, lane_roll(c, part * r - left_lane), left)
-            at = slice(base + group * rows, base + (group + 1) * rows)
-            first_ref[at, :] = jnp.where(even, right, left)
-            second_ref[at, :] = jnp.where(even, left, right)
-
     for i in range(k.fine_n):
-        win_ref[i] = p[i + 1, pl.ds(pl.multiple_of(iy * by, 8), k.rows), :]
+        wide[i] = p[i + 1, pl.ds(pl.multiple_of(iy * by, 8), by + 16), :]
+    for i in range(k.fine_n):
+        win_ref[i] = wide[i, TOP - FR:TOP + by + FR, :]
+    pack = functools.partial(pack_slabs, k, iz, first_ref, second_ref)
     pack(0, k.ny1, k.nx1, lambda i: c1_ref[i], part + 1, bz - 1)
     pack(k.at_fine, k.rows, k.fine_n, lambda i: win_ref[i], 3 * part, 0)
-    pack(k.at_wind, by, 3 * bx, lambda i: w_ref[i // bx, from_end(ix, i % bx, bx)], 3 * part, 0)
-
-
-def solve_kernel(k, c1_ref, win_ref, w_ref, first_ref, second_ref, to3_ref, to4_ref, to7_ref, own_ref,
-                 low_ref, high_ref, b1, m1, e1, half1, b2, u2, v2, b, m, v, vel, flux, half_ref):
+
+
+def solve_kernel(k, c1_ref, win_ref, w_ref, first_ref, second_ref, wind1_ref, wind2_ref, to3_ref, to4_ref, to7_ref, own_ref,
+                 low_ref, high_ref, low_wind, high_wind, b1, m1, e1, half1, b2, u2, v2, b, m, v, vel, flux, half_ref):
     ix, iy, iz = place()
     bx, by, bz, part, n = k.bx, k.by, k.bz, k.part, k.core
     even = lax.rem(iz, 2) == 0
-    low_ref[...] = jnp.where(even, second_ref[...], first_ref[...])
-    high_ref[...] = jnp.where(even, first_ref[...], second_ref[...])
+    for low, high, first, second in ((low_ref, high_ref, first_ref, second_ref), (low_wind, high_wind, wind1_ref, wind2_ref)):
+        low[...] = jnp.where(even, second[...], first[...])
+        high[...] = jnp.where(even, first[...], second[...])
     lane = iota((k.ny1, bz), 1)
     for s in (b1,):
         for i in (0, k.nx1 + 1):
@@ -862,8 +883,8 @@
     for x in range(bx):
         winds = []
         for d in range(3):
-            low = take_slab(k, low_ref, k.at_wind, by, d * bx + x, 3 * part)
-            high = take_slab(k, high_ref, k.at_wind, by, d * bx + x, 0)
+            low = take_slab(k, low_wind, 0, by, d * bx + x, 3 * part)
+            high = take_slab(k, high_wind, 0, by, d * bx + x, 0)
             scale = sign if d == 0 else 0.5
             winds.append((scale * w_ref[d, from_end(ix, x, bx)], scale * outer(low, high, lane)))
         for d in range(3):
@@ -937,7 +958,7 @@
 def close_kernel(k, mine_ref, got_ref, got3_ref, got4_ref, got7_ref, own_ref, out_ref,
                  parts, b1, m1, e1, half1, b2, u2, v2, v, m):
     ix, iy, iz = place()
-    bx, by, bz, n, c2 = k.bx, k.by, k.bz, k.core, k.c2
+    bx, by, n, c2 = k.bx, k.by, k.core, k.c2
     for slot, near, far in ((0, mine_ref, 0), (3, mine_ref, 1), (1, got_ref, 0), (2, got_ref, 1)):
         parts[slot] = near[far * c2:(far + 1) * c2, :]
         parts[4 + slot] = near[(2 + far) * c2:(3 + far) * c2, :]
@@ -992,19 +1013,24 @@
     fine = lambda n: (n + 2, 2, k.rows, bz)
     level1 = [(n1 + 2, k.rows1, bz)] * 3
     level2 = [(n2, k.ny1, bz), (n2, k.ny1 // 2, bz)] + [(n2 + 2, k.ny1 // 2 + 2, bz)] * 2
-    gathered = lax.all_gather(pressure, PLANE)
+    crossed = lambda v, d: lax.ppermute(v, PLANE, [(i, i ^ d) for i in range(k.gx * k.gy)])
+    swapped = lambda pair: [lax.ppermute(v, "gz", p) for v, p in zip(pair, pairs(k.gz))]
+    got = [crossed(pressure, d) for d in (3, 4, 7)]
+    mine, *wind_slabs = call(
+        functools.partial(wind_kernel, k), [(bx, by, bz)] + [(k.wind_rows, bz)] * 2, [], (pressure, wind), 1 << 18)
+    wind_slabs = swapped(wind_slabs)
+    (mine,) = call(join_kernel, [(4, bx, by, bz)], [], (mine, *got), 1 << 12)
     c1, window, first, second = call(
         functools.partial(plane_kernel, k),
         [(n1, k.ny1, bz), (k.fine_n, k.rows, bz), (k.slab_rows, bz), (k.slab_rows, bz)],
-        [(k.nx + 2, -(-(k.ny + 2 * FR) // 8) * 8, bz), (k.nx + 2, k.ny + 2, bz), (k.nx, k.ny, bz), (n1, k.ny, bz)],
-        (gathered, wind), 1 << 22)
-    first, second = (lax.ppermute(v, "gz", p) for v, p in zip((first, second), pairs(k.gz)))
+        [(k.nx + 2, k.ny + 2 * TOP, bz), (k.nx + 2, k.ny + 2, bz), (k.nx, k.ny, bz), (n1, k.ny, bz), (k.fine_n, by + 16, bz)],
+        (mine, crossed(mine, 1)), 1 << 22)
+    first, second = swapped((first, second))
     to3, to4, to7, own = call(
         functools.partial(solve_kernel, k),
         [(k.to3, bz), (k.to4, bz), (k.to7, bz), (bx, by, bz)],
-        [(k.slab_rows, bz)] * 2 + level1 + level2 + [fine(bx + 5)] * 3 + [(3, bx + 3, 2, k.core, bz), (3,) + fine(bx + 1), (2, k.c2_n, 16, bz)],
-        (c1, window, wind, first, second), 1 << 24)
-    crossed = lambda v, d: lax.ppermute(v, PLANE, [(i, i ^ d) for i in range(k.gx * k.gy)])
+        [(k.slab_rows, bz)] * 2 + [(k.wind_rows, bz)] * 2 + level1 + level2 + [fine(bx + 5)] * 3 + [(3, bx + 3, 2, k.core, bz), (3,) + fine(bx + 1), (2, k.c2_n, 16, bz)],
+        (c1, window, wind, first, second, *wind_slabs), 1 << 24)
     got3, got4, got7 = crossed(to3, 3), crossed(to4, 4), crossed(to7, 7)
     (mine,) = call(functools.partial(share_kernel, k), [(k.to1, bz)], [], (to3, got3, got4, got7), 1 << 12)
     (result,) = call(
@@ -1016,9 +1042,10 @@
 
 def solution(mesh):
     gx, gy, gz = (mesh.shape[a] for a in ("gx", "gy", "gz"))
+    mirror = (gx, gy) == (2, 4)
 
     def run(pressure, wind):
-        form, sizes = (mirrored, Mirror) if (gx, gy) == (2, 4) else (general, Sizes)
+        form, sizes = (mirrored, Mirror) if mirror else (general, Sizes)
         return form(sizes(gx, gy, gz, *pressure.shape), pressure, wind)
 
     in_specs = (P("gx", "gy", "gz"), P(None, "gx", "gy", "gz"))

time: 37.7 us -> 39 us (1.034)
  blocking collectives: 11.4 us -> 0 us
  starting transfers between devices: 8.37 us -> 15.8 us
  waiting for transfers between devices: 10.3 us -> 13.5 us
  local copies, waits for them, and re-layouts: 0.01 us -> 1.86 us
    all_gather x1 -> x0, blocking collectives: 11.4 us -> none  [mirrored(): gathered = lax.all_gather(pressure, PLANE)]
    ppermute x4 -> x8, starting transfers between devices: 3.82 us -> 9.29 us  [mirrored(): lax.ppermute(v, PLANE, [(i, i ^ d) for i in range(k.gx * k.gy)])]
    ppermute x4 -> x8, waiting for transfers between devices: 5.6 us -> 10.4 us  [mirrored(): lax.ppermute(v, PLANE, [(i, i ^ d) for i in range(k.gx * k.gy)])]
    ppermute x2 -> x4, starting transfers between devices: 4.55 us -> 6.55 us  [mirrored(): lax.ppermute(v, 'gz', p)]
    unnamed x2 -> x6, local copies, waits for them, and re-layouts: 0.01 us -> 1.86 us
    ppermute x2 -> x4, waiting for transfers between devices: 4.74 us -> 3.17 us  [mirrored(): lax.ppermute(v, 'gz', p)]
    pallas_call x4 -> x6, Pallas kernels: 7.42 us -> 7.47 us  [call(): pl.pallas_call(kernel, out_shape=[f32(s) for s in outs], scratch_shapes=[...]
  transfers between devices with their start and end apart: 6 -> 12, of which waited for: 5 -> 9; matrix products, arithmetic and copies ran while one was open for 0% -> 0% of each run, Pallas kernels for 0% -> 0%
where the time goes in v7:
time: 39 us; the launch traced here: 38.8 us
  starting transfers between devices  15.8 us (41%)
  waiting for transfers between devices  13.5 us (35%)
  Pallas kernels  7.47 us (19%)
  local copies, waits for them, and re-layouts  1.86 us (5%)
    ppermute x8, waiting for transfers between devices, mirrored(): lax.ppermute(v, PLANE, [(i, i ^ d) for i in range(k.gx * k.gy)])  10.4 us
    ppermute x8, starting transfers between devices, mirrored(): lax.ppermute(v, PLANE, [(i, i ^ d) for i in range(k.gx * k.gy)])  9.29 us
    pallas_call x6, Pallas kernels, call(): pl.pallas_call(kernel, out_shape=[f32(s) for s in outs], scratch_shapes=[...  7.47 us
    ppermute x4, starting transfers between devices, mirrored(): lax.ppermute(v, 'gz', p)  6.55 us
    ppermute x4, waiting for transfers between devices, mirrored(): lax.ppermute(v, 'gz', p)  3.17 us
    unnamed x6, local copies, waits for them, and re-layouts  1.86 us
  transfers between devices with their start and end apart: 12, of which 9 were waited for; matrix products, arithmetic and copies ran while one was open for 0% of the time, Pallas kernels for 0%

profile of v7, /device:TPU:9, one launch (start us, length us, event | category | flops | bytes accessed | tf_op | source)
XLA Modules:
  0.0 38.8 jit_solution(13598983682298314225)
XLA Ops:
  0.0 1.8 %collective-permute-start = (f32[12,16,128]{2,1,0:T(8,128)}, f32[12,16,128]{2,1,0:T(8,128)S(1)}, u32[]{:S(2)}, u32[]{:S(2)}) collective-permute-start(f32[12,16,128]{2,1,0:T(8,128)} %p_ref.1), channel_id=1, source_target_pairs={{0,12},{4,8},{8,4},{12,0},{16,28},{20,24},{24,20},{28,16},{1,13},{... | collective-permute-start | bytes 294920 | tf_op jit(solution)/shard_map/ppermute | solution.py:1016
  1.8 1.0 %collective-permute-start.2 = (f32[12,16,128]{2,1,0:T(8,128)}, f32[12,16,128]{2,1,0:T(8,128)S(1)}, u32[]{:S(2)}, u32[]{:S(2)}) collective-permute-start(f32[12,16,128]{2,1,0:T(8,128)} %p_ref.1), channel_id=1, source_target_pairs={{0,28},{4,24},{8,20},{12,16},{16,12},{20,8},{24,4},{28,0},{1,29},{... | collective-permute-start | bytes 294920 | tf_op jit(solution)/shard_map/ppermute | solution.py:1016
  2.7 0.3 collective-permute-start.1
  3.0 0.0 copy-start
  3.0 1.0 %copy-done = f32[3,12,16,128]{3,2,1,0:T(8,128)S(1)} copy-done((f32[3,12,16,128]{3,2,1,0:T(8,128)S(1)}, f32[3,12,16,128]{3,2,1,0:T(8,128)}, u32[]{:S(2)}) %copy-start) | copy-done | bytes 294936
  4.0 0.0 copy-start.2
  4.0 0.9 %copy-done.2 = f32[12,16,128]{2,1,0:T(8,128)S(1)} copy-done((f32[12,16,128]{2,1,0:T(8,128)S(1)}, f32[12,16,128]{2,1,0:T(8,128)}, u32[]{:S(2)}) %copy-start.2) | copy-done | bytes 98328
  4.9 0.2 shard_map.28
  5.1 0.5 %collective-permute-done.b_ref = f32[12,16,128]{2,1,0:T(8,128)S(1)} collective-permute-done((f32[12,16,128]{2,1,0:T(8,128)}, f32[12,16,128]{2,1,0:T(8,128)S(1)}, u32[]{:S(2)}, u32[]{:S(2)}) %collective-permute-start) | collective-permute-done | bytes 98336 | tf_op jit(solution)/shard_map/ppermute | solution.py:1016
  5.5 3.1 %collective-permute-done.2.d_ref = f32[12,16,128]{2,1,0:T(8,128)S(1)} collective-permute-done((f32[12,16,128]{2,1,0:T(8,128)}, f32[12,16,128]{2,1,0:T(8,128)S(1)}, u32[]{:S(2)}, u32[]{:S(2)}) %collective-permute-start.2) | collective-permute-done | bytes 98336 | tf_op jit(solution)/shard_map/ppermute | solution.py:1016
  8.7 0.2 collective-permute-done.1.c_ref
  8.9 0.0 copy-start.1
  8.9 1.5 %collective-permute-start.3 = (f32[4,12,16,128]{3,2,1,0:T(8,128)S(1)}, f32[4,12,16,128]{3,2,1,0:T(8,128)S(1)}, u32[]{:S(2)}, u32[]{:S(2)}) collective-permute-start(f32[4,12,16,128]{3,2,1,0:T(8,128)S(1)} %shard_map.29.mine_ref), channel_id=1, source_target_pairs={{0,4},{4,0},{8,12},{12,8},{16,20},{20,16},{24,28},{28,24},{1,5},{5... | collective-permute-start | bytes 1179656 | tf_op jit(solution)/shard_map/ppermute | solution.py:1016
  10.4 1.3 %collective-permute-done.3.theirs_ref = f32[4,12,16,128]{3,2,1,0:T(8,128)S(1)} collective-permute-done((f32[4,12,16,128]{3,2,1,0:T(8,128)S(1)}, f32[4,12,16,128]{3,2,1,0:T(8,128)S(1)}, u32[]{:S(2)}, u32[]{:S(2)}) %collective-permute-start.3) | collective-permute-done | bytes 393248 | tf_op jit(solution)/shard_map/ppermute | solution.py:1016
  11.7 1.4 %shard_map.30 = (f32[12,32,128]{2,1,0:T(8,128)S(1)}, f32[17,26,128]{2,1,0:T(8,128)S(1)}, f32[226,128]{1,0:T(8,128)S(1)}, f32[226,128]{1,0:T(8,128)S(1)}) custom-call(f32[4,12,16,128]{3,2,1,0:T(8,128)S(1)} %shard_map.29.mine_ref, f32[4,12,16,128]{3,2,1,0:T(8,128)S(1)} %collective-permute-done.3.theirs_ref), custom_call_target="tpu_custom_call" | custom-call | flops 4194304 | bytes 1048576 | tf_op jit(solution)/shard_map/pallas_call | solution.py:497
  13.1 0.2 collective-permute-start.4
  13.4 4.3 %collective-permute-start.5 = (f32[226,128]{1,0:T(8,128)S(1)}, f32[226,128]{1,0:T(8,128)S(1)}, u32[]{:S(2)}, u32[]{:S(2)}) collective-permute-start(f32[226,128]{1,0:T(8,128)S(1)} %get-tuple-element.20), channel_id=1, source_target_pairs={{1,2},{2,1},{5,6},{6,5},{9,10},{10,9},{13,14},{14,13},{17,18},{18,... | collective-permute-start | bytes 347144 | tf_op jit(solution)/shard_map/ppermute | solution.py:1017
  17.7 0.1 collective-permute-start.6
  17.8 1.9 %collective-permute-start.7 = (f32[144,128]{1,0:T(8,128)S(1)}, f32[144,128]{1,0:T(8,128)S(1)}, u32[]{:S(2)}, u32[]{:S(2)}) collective-permute-start(f32[144,128]{1,0:T(8,128)S(1)} %get-tuple-element.22), channel_id=1, source_target_pairs={{1,2},{2,1},{5,6},{6,5},{9,10},{10,9},{13,14},{14,13},{17,18},{18,... | collective-permute-start | bytes 221192 | tf_op jit(solution)/shard_map/ppermute | solution.py:1017
  19.7 1.6 %collective-permute-done.6.wind1_ref = f32[144,128]{1,0:T(8,128)S(1)} collective-permute-done((f32[144,128]{1,0:T(8,128)S(1)}, f32[144,128]{1,0:T(8,128)S(1)}, u32[]{:S(2)}, u32[]{:S(2)}) %collective-permute-start.6) | collective-permute-done | bytes 73760 | tf_op jit(solution)/shard_map/ppermute | solution.py:1017
  21.3 1.6 %collective-permute-done.7.wind2_ref = f32[144,128]{1,0:T(8,128)S(1)} collective-permute-done((f32[144,128]{1,0:T(8,128)S(1)}, f32[144,128]{1,0:T(8,128)S(1)}, u32[]{:S(2)}, u32[]{:S(2)}) %collective-permute-start.7) | collective-permute-done | bytes 73760 | tf_op jit(solution)/shard_map/ppermute | solution.py:1017
  22.9 0.0 collective-permute-done.4.first_ref
  22.9 0.0 collective-permute-done.5.second_ref
  22.9 0.0 copy-done.1
  22.9 3.5 %shard_map.31 = (f32[216,128]{1,0:T(8,128)S(1)}, f32[184,128]{1,0:T(8,128)S(1)}, f32[120,128]{1,0:T(8,128)S(1)}, f32[12,16,128]{2,1,0:T(8,128)S(1)}) custom-call(f32[12,32,128]{2,1,0:T(8,128)S(1)} %get-tuple-element.17.c1_ref, f32[17,26,128]{2,1,0:T(8,128)S(1)} %get-tuple-element.18.win_ref, f32[3,12,16,128]{3,2,1,0:T(8,128)S(1)} %copy-done.1, ...), custom_call_target="tpu_custom_call" | custom-call | flops 16777216 | bytes 1048576 | tf_op jit(solution)/shard_map/pallas_call | solution.py:497
  26.4 3.2 %collective-permute-start.8 = (f32[216,128]{1,0:T(8,128)S(1)}, f32[216,128]{1,0:T(8,128)S(1)}, u32[]{:S(2)}, u32[]{:S(2)}) collective-permute-start(f32[216,128]{1,0:T(8,128)S(1)} %get-tuple-element.23.own_ref), channel_id=1, source_target_pairs={{0,12},{4,8},{8,4},{12,0},{16,28},{20,24},{24,20},{28,16},{1,13},{... | collective-permute-start | bytes 331784 | tf_op jit(solution)/shard_map/ppermute | solution.py:1016
  29.6 0.2 collective-permute-start.9
  29.8 1.3 %collective-permute-start.10 = (f32[120,128]{1,0:T(8,128)S(1)}, f32[120,128]{1,0:T(8,128)S(1)}, u32[]{:S(2)}, u32[]{:S(2)}) collective-permute-start(f32[120,128]{1,0:T(8,128)S(1)} %get-tuple-element.25), channel_id=1, source_target_pairs={{0,28},{4,24},{8,20},{12,16},{16,12},{20,8},{24,4},{28,0},{1,29},{... | collective-permute-start | bytes 184328 | tf_op jit(solution)/shard_map/ppermute | solution.py:1016
  31.1 3.4 %collective-permute-done.10.got7_ref = f32[120,128]{1,0:T(8,128)S(1)} collective-permute-done((f32[120,128]{1,0:T(8,128)S(1)}, f32[120,128]{1,0:T(8,128)S(1)}, u32[]{:S(2)}, u32[]{:S(2)}) %collective-permute-start.10) | collective-permute-done | bytes 61472 | tf_op jit(solution)/shard_map/ppermute | solution.py:1016
  34.6 0.2 collective-permute-done.9.got4_ref
  34.8 0.0 collective-permute-done.8.got3_ref
  34.8 0.1 collective-permute-start.11
  34.9 1.5 %collective-permute-done.11.got_ref = f32[528,128]{1,0:T(8,128)S(1)} collective-permute-done((f32[528,128]{1,0:T(8,128)S(1)}, f32[528,128]{1,0:T(8,128)S(1)}, u32[]{:S(2)}, u32[]{:S(2)}) %collective-permute-start.11) | collective-permute-done | bytes 270368 | tf_op jit(solution)/shard_map/ppermute | solution.py:1016
  36.4 2.4 %shard_map.33 = f32[12,16,128]{2,1,0:T(8,128)} custom-call(f32[528,128]{1,0:T(8,128)S(1)} %shard_map.32.mine_ref, f32[528,128]{1,0:T(8,128)S(1)} %collective-permute-done.11.got_ref, f32[216,128]{1,0:T(8,128)S(1)} %collective-permute-done.8.got3_ref, f32[184,128]{1,0:T(8,128)S(1)} %collective-permute-done.9.got4_ref, ...), custom_call_target="tpu_custom_call" | custom-call | flops 8388608 | bytes 1048576 | tf_op jit(solution)/shard_map/pallas_call | solution.py:497
  (2 shorter events, 0.0 us)
Async XLA Ops:
  0.0 5.5 %collective-permute-start = (f32[12,16,128]{2,1,0:T(8,128)}, f32[12,16,128]{2,1,0:T(8,128)S(1)}, u32[]{:S(2)}, u32[]{:S(2)}) collective-permute-start(f32[12,16,128]{2,1,0:T(8,128)} %p_ref.1), channel_id=1, source_target_pairs={{0,12},{4,8},{8,4},{12,0},{16,28},{20,24},{24,20},{28,16},{1,13},{... | collective-permute-start | bytes 294920 | tf_op jit(solution)/shard_map/ppermute | solution.py:1016
  1.8 6.9 %collective-permute-start.2 = (f32[12,16,128]{2,1,0:T(8,128)}, f32[12,16,128]{2,1,0:T(8,128)S(1)}, u32[]{:S(2)}, u32[]{:S(2)}) collective-permute-start(f32[12,16,128]{2,1,0:T(8,128)} %p_ref.1), channel_id=1, source_target_pairs={{0,28},{4,24},{8,20},{12,16},{16,12},{20,8},{24,4},{28,0},{1,29},{... | collective-permute-start | bytes 294920 | tf_op jit(solution)/shard_map/ppermute | solution.py:1016
  2.7 6.1 %collective-permute-start.1 = (f32[12,16,128]{2,1,0:T(8,128)}, f32[12,16,128]{2,1,0:T(8,128)S(1)}, u32[]{:S(2)}, u32[]{:S(2)}) collective-permute-start(f32[12,16,128]{2,1,0:T(8,128)} %p_ref.1), channel_id=1, source_target_pairs={{0,16},{4,20},{8,24},{12,28},{16,0},{20,4},{24,8},{28,12},{1,17},{... | collective-permute-start | bytes 294920 | tf_op jit(solution)/shard_map/ppermute | solution.py:1016
  3.0 1.0 %copy-start = (f32[3,12,16,128]{3,2,1,0:T(8,128)S(1)}, f32[3,12,16,128]{3,2,1,0:T(8,128)}, u32[]{:S(2)}) copy-start(f32[3,12,16,128]{3,2,1,0:T(8,128)} %w_ref.3) | copy-start | bytes 884740
  4.0 0.9 %copy-start.2 = (f32[12,16,128]{2,1,0:T(8,128)S(1)}, f32[12,16,128]{2,1,0:T(8,128)}, u32[]{:S(2)}) copy-start(f32[12,16,128]{2,1,0:T(8,128)} %p_ref.1) | copy-start | bytes 294916
  8.9 14.0 %copy-start.1 = (f32[3,12,16,128]{3,2,1,0:T(8,128)S(1)}, f32[3,12,16,128]{3,2,1,0:T(8,128)}, u32[]{:S(2)}) copy-start(f32[3,12,16,128]{3,2,1,0:T(8,128)} %w_ref.3) | copy-start | bytes 884740
  8.9 2.8 %collective-permute-start.3 = (f32[4,12,16,128]{3,2,1,0:T(8,128)S(1)}, f32[4,12,16,128]{3,2,1,0:T(8,128)S(1)}, u32[]{:S(2)}, u32[]{:S(2)}) collective-permute-start(f32[4,12,16,128]{3,2,1,0:T(8,128)S(1)} %shard_map.29.mine_ref), channel_id=1, source_target_pairs={{0,4},{4,0},{8,12},{12,8},{16,20},{20,16},{24,28},{28,24},{1,5},{5... | collective-permute-start | bytes 1179656 | tf_op jit(solution)/shard_map/ppermute | solution.py:1016
  13.1 9.7 %collective-permute-start.4 = (f32[226,128]{1,0:T(8,128)S(1)}, f32[226,128]{1,0:T(8,128)S(1)}, u32[]{:S(2)}, u32[]{:S(2)}) collective-permute-start(f32[226,128]{1,0:T(8,128)S(1)} %get-tuple-element.19), channel_id=1, source_target_pairs={{0,1},{1,0},{2,3},{3,2},{4,5},{5,4},{6,7},{7,6},{8,9},{9,8},{10,11... | collective-permute-start | bytes 347144 | tf_op jit(solution)/shard_map/ppermute | solution.py:1017
  13.4 9.5 %collective-permute-start.5 = (f32[226,128]{1,0:T(8,128)S(1)}, f32[226,128]{1,0:T(8,128)S(1)}, u32[]{:S(2)}, u32[]{:S(2)}) collective-permute-start(f32[226,128]{1,0:T(8,128)S(1)} %get-tuple-element.20), channel_id=1, source_target_pairs={{1,2},{2,1},{5,6},{6,5},{9,10},{10,9},{13,14},{14,13},{17,18},{18,... | collective-permute-start | bytes 347144 | tf_op jit(solution)/shard_map/ppermute | solution.py:1017
  17.7 3.6 %collective-permute-start.6 = (f32[144,128]{1,0:T(8,128)S(1)}, f32[144,128]{1,0:T(8,128)S(1)}, u32[]{:S(2)}, u32[]{:S(2)}) collective-permute-start(f32[144,128]{1,0:T(8,128)S(1)} %get-tuple-element.21), channel_id=1, source_target_pairs={{0,1},{1,0},{2,3},{3,2},{4,5},{5,4},{6,7},{7,6},{8,9},{9,8},{10,11... | collective-permute-start | bytes 221192 | tf_op jit(solution)/shard_map/ppermute | solution.py:1017
  17.8 5.1 %collective-permute-start.7 = (f32[144,128]{1,0:T(8,128)S(1)}, f32[144,128]{1,0:T(8,128)S(1)}, u32[]{:S(2)}, u32[]{:S(2)}) collective-permute-start(f32[144,128]{1,0:T(8,128)S(1)} %get-tuple-element.22), channel_id=1, source_target_pairs={{1,2},{2,1},{5,6},{6,5},{9,10},{10,9},{13,14},{14,13},{17,18},{18,... | collective-permute-start | bytes 221192 | tf_op jit(solution)/shard_map/ppermute | solution.py:1017
  26.4 8.4 %collective-permute-start.8 = (f32[216,128]{1,0:T(8,128)S(1)}, f32[216,128]{1,0:T(8,128)S(1)}, u32[]{:S(2)}, u32[]{:S(2)}) collective-permute-start(f32[216,128]{1,0:T(8,128)S(1)} %get-tuple-element.23.own_ref), channel_id=1, source_target_pairs={{0,12},{4,8},{8,4},{12,0},{16,28},{20,24},{24,20},{28,16},{1,13},{... | collective-permute-start | bytes 331784 | tf_op jit(solution)/shard_map/ppermute | solution.py:1016
  29.6 5.2 %collective-permute-start.9 = (f32[184,128]{1,0:T(8,128)S(1)}, f32[184,128]{1,0:T(8,128)S(1)}, u32[]{:S(2)}, u32[]{:S(2)}) collective-permute-start(f32[184,128]{1,0:T(8,128)S(1)} %get-tuple-element.24), channel_id=1, source_target_pairs={{0,16},{4,20},{8,24},{12,28},{16,0},{20,4},{24,8},{28,12},{1,17},{... | collective-permute-start | bytes 282632 | tf_op jit(solution)/shard_map/ppermute | solution.py:1016
  29.8 4.8 %collective-permute-start.10 = (f32[120,128]{1,0:T(8,128)S(1)}, f32[120,128]{1,0:T(8,128)S(1)}, u32[]{:S(2)}, u32[]{:S(2)}) collective-permute-start(f32[120,128]{1,0:T(8,128)S(1)} %get-tuple-element.25), channel_id=1, source_target_pairs={{0,28},{4,24},{8,20},{12,16},{16,12},{20,8},{24,4},{28,0},{1,29},{... | collective-permute-start | bytes 184328 | tf_op jit(solution)/shard_map/ppermute | solution.py:1016
  34.8 1.6 %collective-permute-start.11 = (f32[528,128]{1,0:T(8,128)S(1)}, f32[528,128]{1,0:T(8,128)S(1)}, u32[]{:S(2)}, u32[]{:S(2)}) collective-permute-start(f32[528,128]{1,0:T(8,128)S(1)} %shard_map.32.mine_ref), channel_id=1, source_target_pairs={{0,4},{4,0},{8,12},{12,8},{16,20},{20,16},{24,28},{28,24},{1,5},{5... | collective-permute-start | bytes 811016 | tf_op jit(solution)/shard_map/ppermute | solution.py:1016
